TPU v7x, 128 devices: a whole 4x4x4 slice. The times are simulated.
128 devices in a mesh: wide: 32 (over x, z, core), narrow: 4 (over y).
Axes of the slice: x: 4, y: 4, z: 4, core: 2. Of those that a mesh axis runs over, the one named last changes fastest.
Arguments:
- cost: float32 [4096, 16384], P('wide', 'narrow'), may hold values from 0 to 2
- plan: float32 [4096, 16384], P('wide', 'narrow'), may hold values from 0 to 2
- row_mass: float32 [4096], P('wide'), may hold values from 4096 to 28672
- col_mass: float32 [16384], P('narrow'), may hold values from 1024 to 7168
- row_dual: float32 [4096], P('wide'), may hold values from -3 to 3
- col_dual: float32 [16384], P('narrow'), may hold values from -3 to 3
Outputs:
- plan_out: float32 [4096, 16384], P('wide', 'narrow')
- row_out: float32 [4096], P('wide')
- col_out: float32 [16384], P('narrow')
All inputs are finite; a program needn't handle non-finite values.
Results may differ from a plain program's by a relative error of at most 0.0001.
Values sent between devices are 32-bit elements; how exact they have to be, the bound alone decides.
No kernel may reach another device: no remote copies, remote signals or barrier semaphores. Data moves between devices by JAX's collectives and lax.ppermute only.
A program may use at most 64 MiB of HBM per device.

v0:
```python
import math

import jax
import jax.numpy as jnp
from jax import lax
from jax.sharding import Mesh
from jax.sharding import PartitionSpec as P

ITERS = 4
WIDE = ("wide_0", "wide_1", "wide_2")
WIDE_NARROW = ("wide_0", "wide_1", "wide_2", "narrow")


def over_pieces(array, axis):
    parts = lax.all_gather(array, axis)
    return parts.sum(axis=0)


def copy_for_each(array, axis):
    copies = jnp.broadcast_to(array, (lax.axis_size(axis), *array.shape))
    return lax.all_to_all(copies, axis, split_axis=0, concat_axis=0, tiled=True)


def of_everyone(array, axis):
    everything = copy_for_each(array, axis)
    return jnp.sum(everything, axis=0)


def one_axis_at_a_time(array, axes):
    for axis in axes:
        array = lax.psum(array, axis)
    return array


def shards(cost, plan, row_mass, col_mass, row_dual, col_dual):
    wide_count = lax.axis_size(WIDE)
    narrow_count = lax.axis_size("narrow")
    total_rows = plan.shape[0] * wide_count
    total_cols = plan.shape[1] * narrow_count
    step_base = 0.9 / math.sqrt(total_rows + total_cols)
    weight = jnp.float32(step_base)
    for step in range(ITERS):
        primal_step = step_base / weight
        dual_step = step_base * weight
        fresh = jnp.maximum(
            plan - primal_step * (cost - row_dual[:, None] - col_dual[None, :]), 0.0
        )
        change = fresh - plan
        extrap = fresh + change
        moved = jnp.sum(change * change)
        row_total = over_pieces(jnp.sum(extrap, axis=1), "narrow")
        new_row = row_dual + dual_step * (row_mass - row_total)
        row_square = jnp.sum((new_row - row_dual) ** 2)
        col_local = jnp.sum(extrap, axis=0)
        col_total = of_everyone(col_local, WIDE)
        new_col = col_dual + dual_step * (col_mass - col_total)
        col_share = jnp.sum((new_col - col_dual) ** 2) / wide_count
        dual_share = row_square / narrow_count + col_share
        moved_all, dual_moved = (
            one_axis_at_a_time(moved, WIDE_NARROW),
            one_axis_at_a_time(dual_share, WIDE_NARROW),
        )
        weight = jnp.sqrt(weight * jnp.sqrt((dual_moved + 1.0) / (moved_all + 1.0)))
        plan, row_dual, col_dual = (fresh, new_row, new_col)
    return (plan, row_dual, col_dual)


def solution(mesh):
    split = Mesh(
        mesh.devices.reshape(4, 4, 2, mesh.shape["narrow"]),
        ("wide_0", "wide_1", "wide_2", "narrow"),
    )
    placed = (P(WIDE, "narrow"), P(WIDE, "narrow"), P(WIDE), P("narrow"), P(WIDE), P("narrow"))
    return jax.shard_map(
        shards,
        mesh=split,
        in_specs=placed,
        out_specs=(P(WIDE, "narrow"), P(WIDE), P("narrow")),
        check_vma=False,
    )
```

profile of v0, /device:TPU:1, one launch (start us, length us, event | category | flops | bytes accessed | tf_op | source)
XLA Modules:
  0.0 199.3 jit_solution(1360637981968702370)
XLA Ops:
  0.6 0.0 copy-start.3
  0.6 0.0 copy-start.4
  0.7 4.0 %multiply_reduce_fusion.2 = (f32[]{:T(128)}, f32[4096]{0:T(1024)S(1)}, f32[128]{0:T(128)S(1)}) fusion(f32[128,4096]{1,0:T(8,128)} %param.7, f32[4096]{0:T(1024)} %param.11, f32[128,4096]{1,0:T(8,128)} %param.6, f32[128]{0:T(128)} %param.10), kind=kLoop, calls=%fused_computation.6 | loop fusion | flops 5238655 | bytes 4228100 | tf_op jit(solution)/shard_map/reduce_sum | solution.py:50
  4.7 1.3 broadcast_in_dim.8
  5.9 9.4 %all-to-all-start = ((f32[32,1,4096]{2,1,0:T(1,128)}), f32[32,1,4096]{2,1,0:T(1,128)S(1)}, u32[]{:S(2)}, u32[]{:S(2)}) async-start(f32[32,1,4096]{2,1,0:T(1,128)} %broadcast_in_dim.8), calls=%async_computation | async-start | bytes 1048576 | tf_op jit(solution)/shard_map/all_to_all | solution.py:21
  15.4 8.5 %all-gather.4 = f32[4,1,128]{2,1,0:T(1,128)S(1)} all-gather(f32[1,1,128]{2,1,0:T(1,128)S(1)} %bitcast.7), channel_id=2, replica_groups=mesh['wide_0'=4,'wide_1'=4,'wide_2'=2,'narrow'=4] {'narrow'}, dimensions={0}, use_global_device_ids=true | all-gather | bytes 2560 | tf_op jit(solution)/shard_map/all_gather | solution.py:15
  23.9 0.0 copy-done.3
  23.9 0.0 copy-done.4
  23.9 0.6 multiply_reduce_fusion.8
  25.2 1.8 all-to-all-done
  27.0 0.4 reduce_sum.229
  27.3 0.6 multiply_reduce_fusion.5
  28.6 7.5 %all-reduce.8 = (f32[]{:T(128)}, f32[]{:T(128)}) all-reduce(f32[]{:T(128)S(6)} %add.114, f32[]{:T(128)} %get-tuple-element.11), channel_id=1, replica_groups=mesh['wide_0'=4,'wide_1'=4,'wide_2'=2,'narrow'=4] {'wide_0'}, use_global_device_ids=true, to_apply=%region_6.0 | all-reduce | flops 2 | bytes 16 | tf_op jit(solution)/shard_map/psum | solution.py:31
  36.1 8.7 %all-reduce.5 = (f32[]{:T(128)}, f32[]{:T(128)}) all-reduce(f32[]{:T(128)} %get-tuple-element.30, f32[]{:T(128)} %get-tuple-element.31), channel_id=1, replica_groups=mesh['wide_0'=4,'wide_1'=4,'wide_2'=2,'narrow'=4] {'wide_1'}, use_global_device_ids=true, to_apply=%region_7.0 | all-reduce | flops 2 | bytes 16 | tf_op jit(solution)/shard_map/psum | solution.py:31
  44.9 8.9 %all-reduce.11 = (f32[]{:T(128)}, f32[]{:T(128)}) all-reduce(f32[]{:T(128)} %get-tuple-element.24, f32[]{:T(128)} %get-tuple-element.25), channel_id=1, replica_groups=mesh['wide_0'=4,'wide_1'=4,'wide_2'=2,'narrow'=4] {'wide_2'}, use_global_device_ids=true, to_apply=%region_8.0 | all-reduce | flops 2 | bytes 16 | tf_op jit(solution)/shard_map/psum | solution.py:31
  53.8 6.7 %all-reduce.2 = (f32[]{:T(128)}, f32[]{:T(128)}) all-reduce(f32[]{:T(128)} %get-tuple-element.36, f32[]{:T(128)} %get-tuple-element.37), channel_id=1, replica_groups=mesh['wide_0'=4,'wide_1'=4,'wide_2'=2,'narrow'=4] {'narrow'}, use_global_device_ids=true, to_apply=%region_9.0 | all-reduce | flops 2 | bytes 16 | tf_op jit(solution)/shard_map/psum | solution.py:31
  61.9 3.7 %multiply_reduce_fusion.1 = (f32[]{:T(128)}, f32[128]{0:T(128)S(1)}, f32[4096]{0:T(1024)S(1)}) fusion(f32[4096]{0:T(1024)S(1)} %get-tuple-element.48, f32[128,4096]{1,0:T(8,128)} %param.6, f32[128]{0:T(128)S(1)} %get-tuple-element.50, f32[]{:T(128)S(6)} %div.39, f32[128,4096]{1,0:T(8,128)S(1)} %copy-done, f32[4096]{0:T(1024)S(1)} %copy-done.1, ...), kind=kLoop, calls=%fused_computation.4 | loop fusion | flops 7860095 | bytes 4245000 | tf_op jit(solution)/shard_map/reduce_sum | solution.py:50
  65.6 1.3 broadcast_in_dim.9
  66.9 5.5 %all-to-all-start.1 = ((f32[32,1,4096]{2,1,0:T(1,128)}), f32[32,1,4096]{2,1,0:T(1,128)S(1)}, u32[]{:S(2)}, u32[]{:S(2)}) async-start(f32[32,1,4096]{2,1,0:T(1,128)} %broadcast_in_dim.9), calls=%async_computation.1 | async-start | bytes 1048576 | tf_op jit(solution)/shard_map/all_to_all | solution.py:21
  72.5 7.5 %all-gather.5 = f32[4,1,128]{2,1,0:T(1,128)S(1)} all-gather(f32[1,1,128]{2,1,0:T(1,128)S(1)} %bitcast.5), channel_id=3, replica_groups=mesh['wide_0'=4,'wide_1'=4,'wide_2'=2,'narrow'=4] {'narrow'}, dimensions={0}, use_global_device_ids=true | all-gather | bytes 2560 | tf_op jit(solution)/shard_map/all_gather | solution.py:15
  80.0 0.6 multiply_reduce_fusion.7
  81.3 2.9 %all-to-all-done.1 = f32[32,1,4096]{2,1,0:T(1,128)S(1)} async-done(((f32[32,1,4096]{2,1,0:T(1,128)}), f32[32,1,4096]{2,1,0:T(1,128)S(1)}, u32[]{:S(2)}, u32[]{:S(2)}) %all-to-all-start.1) | async-done | bytes 524320 | tf_op jit(solution)/shard_map/all_to_all | solution.py:21
  84.2 0.4 reduce_sum.236
  84.5 0.6 multiply_reduce_fusion.4
  85.8 7.3 %all-reduce.7 = (f32[]{:T(128)}, f32[]{:T(128)}) all-reduce(f32[]{:T(128)S(6)} %add.120, f32[]{:T(128)} %get-tuple-element.8), channel_id=1, replica_groups=mesh['wide_0'=4,'wide_1'=4,'wide_2'=2,'narrow'=4] {'wide_0'}, use_global_device_ids=true, to_apply=%region_21.0 | all-reduce | flops 2 | bytes 16 | tf_op jit(solution)/shard_map/psum | solution.py:31
  93.1 8.2 %all-reduce.4 = (f32[]{:T(128)}, f32[]{:T(128)}) all-reduce(f32[]{:T(128)} %get-tuple-element.28, f32[]{:T(128)} %get-tuple-element.29), channel_id=1, replica_groups=mesh['wide_0'=4,'wide_1'=4,'wide_2'=2,'narrow'=4] {'wide_1'}, use_global_device_ids=true, to_apply=%region_22.0 | all-reduce | flops 2 | bytes 16 | tf_op jit(solution)/shard_map/psum | solution.py:31
  101.3 8.6 %all-reduce.10 = (f32[]{:T(128)}, f32[]{:T(128)}) all-reduce(f32[]{:T(128)} %get-tuple-element.22, f32[]{:T(128)} %get-tuple-element.23), channel_id=1, replica_groups=mesh['wide_0'=4,'wide_1'=4,'wide_2'=2,'narrow'=4] {'wide_2'}, use_global_device_ids=true, to_apply=%region_23.0 | all-reduce | flops 2 | bytes 16 | tf_op jit(solution)/shard_map/psum | solution.py:31
  109.9 6.7 %all-reduce.1 = (f32[]{:T(128)}, f32[]{:T(128)}) all-reduce(f32[]{:T(128)} %get-tuple-element.34, f32[]{:T(128)} %get-tuple-element.35), channel_id=1, replica_groups=mesh['wide_0'=4,'wide_1'=4,'wide_2'=2,'narrow'=4] {'narrow'}, use_global_device_ids=true, to_apply=%region_24.0 | all-reduce | flops 2 | bytes 16 | tf_op jit(solution)/shard_map/psum | solution.py:31
  118.1 4.2 %multiply_reduce_fusion = (f32[]{:T(128)}, f32[128]{0:T(128)S(1)}, f32[4096]{0:T(1024)S(1)}) fusion(f32[4096]{0:T(1024)S(1)} %get-tuple-element.44, f32[128,4096]{1,0:T(8,128)} %param.6, f32[128]{0:T(128)S(1)} %get-tuple-element.46, f32[]{:T(128)S(6)} %div.43, f32[4096]{0:T(1024)S(1)} %get-tuple-element.48, f32[128]{0:T(128)S(1)} %get-tuple-element.50, ...), kind=kLoop, calls=%fused_computation.2 | loop fusion | flops 10481535 | bytes 4261900 | tf_op jit(solution)/shard_map/reduce_sum | solution.py:50
  122.3 1.3 broadcast_in_dim.10
  123.5 5.5 %all-to-all-start.2 = ((f32[32,1,4096]{2,1,0:T(1,128)}), f32[32,1,4096]{2,1,0:T(1,128)S(1)}, u32[]{:S(2)}, u32[]{:S(2)}) async-start(f32[32,1,4096]{2,1,0:T(1,128)} %broadcast_in_dim.10), calls=%async_computation.2 | async-start | bytes 1048576 | tf_op jit(solution)/shard_map/all_to_all | solution.py:21
  129.1 7.5 %all-gather.6 = f32[4,1,128]{2,1,0:T(1,128)S(1)} all-gather(f32[1,1,128]{2,1,0:T(1,128)S(1)} %bitcast.6), channel_id=4, replica_groups=mesh['wide_0'=4,'wide_1'=4,'wide_2'=2,'narrow'=4] {'narrow'}, dimensions={0}, use_global_device_ids=true | all-gather | bytes 2560 | tf_op jit(solution)/shard_map/all_gather | solution.py:15
  136.6 0.6 multiply_reduce_fusion.6
  137.9 2.9 %all-to-all-done.2 = f32[32,1,4096]{2,1,0:T(1,128)S(1)} async-done(((f32[32,1,4096]{2,1,0:T(1,128)}), f32[32,1,4096]{2,1,0:T(1,128)S(1)}, u32[]{:S(2)}, u32[]{:S(2)}) %all-to-all-start.2) | async-done | bytes 524320 | tf_op jit(solution)/shard_map/all_to_all | solution.py:21
  140.8 0.4 reduce_sum.243
  141.1 0.6 multiply_reduce_fusion.3
  142.4 7.3 %all-reduce.6 = (f32[]{:T(128)}, f32[]{:T(128)}) all-reduce(f32[]{:T(128)S(6)} %add.126, f32[]{:T(128)} %get-tuple-element.5), channel_id=1, replica_groups=mesh['wide_0'=4,'wide_1'=4,'wide_2'=2,'narrow'=4] {'wide_0'}, use_global_device_ids=true, to_apply=%region_36.0 | all-reduce | flops 2 | bytes 16 | tf_op jit(solution)/shard_map/psum | solution.py:31
  149.7 8.2 %all-reduce.3 = (f32[]{:T(128)}, f32[]{:T(128)}) all-reduce(f32[]{:T(128)} %get-tuple-element.26, f32[]{:T(128)} %get-tuple-element.27), channel_id=1, replica_groups=mesh['wide_0'=4,'wide_1'=4,'wide_2'=2,'narrow'=4] {'wide_1'}, use_global_device_ids=true, to_apply=%region_37.0 | all-reduce | flops 2 | bytes 16 | tf_op jit(solution)/shard_map/psum | solution.py:31
  157.9 8.6 %all-reduce.9 = (f32[]{:T(128)}, f32[]{:T(128)}) all-reduce(f32[]{:T(128)} %get-tuple-element.20, f32[]{:T(128)} %get-tuple-element.21), channel_id=1, replica_groups=mesh['wide_0'=4,'wide_1'=4,'wide_2'=2,'narrow'=4] {'wide_2'}, use_global_device_ids=true, to_apply=%region_38.0 | all-reduce | flops 2 | bytes 16 | tf_op jit(solution)/shard_map/psum | solution.py:31
  166.5 6.9 %all-reduce = (f32[]{:T(128)}, f32[]{:T(128)}) all-reduce(f32[]{:T(128)} %get-tuple-element.32, f32[]{:T(128)} %get-tuple-element.33), channel_id=1, replica_groups=mesh['wide_0'=4,'wide_1'=4,'wide_2'=2,'narrow'=4] {'narrow'}, use_global_device_ids=true, to_apply=%region_39.0 | all-reduce | flops 2 | bytes 16 | tf_op jit(solution)/shard_map/psum | solution.py:31
  174.9 4.9 %fusion.6 = (f32[4096]{0:T(1024)S(1)}, f32[128]{0:T(128)S(1)}, f32[128,4096]{1,0:T(8,128)}) fusion(f32[4096]{0:T(1024)S(1)} %get-tuple-element.44, f32[128,4096]{1,0:T(8,128)} %param.6, f32[128]{0:T(128)S(1)} %get-tuple-element.46, f32[]{:T(128)S(6)} %div.43, f32[4096]{0:T(1024)S(1)} %get-tuple-element.48, f32[128]{0:T(128)S(1)} %get-tuple-element.50, ...), kind=kLoop, calls=%fused_computation.17 | loop fusion | flops 12054400 | bytes 6375948 | tf_op jit(solution)/shard_map/reduce_sum | solution.py:54
  179.8 1.3 broadcast_in_dim.11
  181.1 5.5 %all-to-all-start.3 = ((f32[32,1,4096]{2,1,0:T(1,128)}), f32[32,1,4096]{2,1,0:T(1,128)S(1)}, u32[]{:S(2)}, u32[]{:S(2)}) async-start(f32[32,1,4096]{2,1,0:T(1,128)} %broadcast_in_dim.11), calls=%async_computation.3 | async-start | bytes 1048576 | tf_op jit(solution)/shard_map/all_to_all | solution.py:21
  186.6 7.5 %all-gather.7 = f32[4,1,128]{2,1,0:T(1,128)S(1)} all-gather(f32[1,1,128]{2,1,0:T(1,128)S(1)} %bitcast.4), channel_id=5, replica_groups=mesh['wide_0'=4,'wide_1'=4,'wide_2'=2,'narrow'=4] {'narrow'}, dimensions={0}, use_global_device_ids=true | all-gather | bytes 2560 | tf_op jit(solution)/shard_map/all_gather | solution.py:15
  194.2 0.5 multiply_add_fusion.4
  194.7 3.6 %all-to-all-done.3 = f32[32,1,4096]{2,1,0:T(1,128)S(1)} async-done(((f32[32,1,4096]{2,1,0:T(1,128)}), f32[32,1,4096]{2,1,0:T(1,128)S(1)}, u32[]{:S(2)}, u32[]{:S(2)}) %all-to-all-start.3) | async-done | bytes 524320 | tf_op jit(solution)/shard_map/all_to_all | solution.py:21
  198.3 0.4 reduce_sum.249
  198.7 0.6 multiply_add_fusion
  (10 shorter events, 0.1 us)
Async XLA Ops:
  0.6 23.3 %copy-start.3 = (f32[128]{0:T(128)S(1)}, f32[128]{0:T(128)}, u32[]{:S(2)}) copy-start(f32[128]{0:T(128)} %param.10) | copy-start | bytes 1540
  0.6 23.3 %copy-start.4 = (f32[128]{0:T(128)S(1)}, f32[128]{0:T(128)}, u32[]{:S(2)}) copy-start(f32[128]{0:T(128)} %param.8) | copy-start | bytes 1540
  4.7 22.7 %copy-start.1 = (f32[4096]{0:T(1024)S(1)}, f32[4096]{0:T(1024)}, u32[]{:S(2)}) copy-start(f32[4096]{0:T(1024)} %param.11) | copy-start | bytes 49156
  4.7 22.7 %copy-start.2 = (f32[4096]{0:T(1024)S(1)}, f32[4096]{0:T(1024)}, u32[]{:S(2)}) copy-start(f32[4096]{0:T(1024)} %param.9) | copy-start | bytes 49156
  4.7 57.2 %copy-start = (f32[128,4096]{1,0:T(8,128)S(1)}, f32[128,4096]{1,0:T(8,128)}, u32[]{:S(2)}) copy-start(f32[128,4096]{1,0:T(8,128)} %param.7) | copy-start | bytes 6291460
  5.9 21.0 %all-to-all-start = ((f32[32,1,4096]{2,1,0:T(1,128)}), f32[32,1,4096]{2,1,0:T(1,128)S(1)}, u32[]{:S(2)}, u32[]{:S(2)}) async-start(f32[32,1,4096]{2,1,0:T(1,128)} %broadcast_in_dim.8), calls=%async_computation | async-start | bytes 1048576 | tf_op jit(solution)/shard_map/all_to_all | solution.py:21
  66.9 17.2 %all-to-all-start.1 = ((f32[32,1,4096]{2,1,0:T(1,128)}), f32[32,1,4096]{2,1,0:T(1,128)S(1)}, u32[]{:S(2)}, u32[]{:S(2)}) async-start(f32[32,1,4096]{2,1,0:T(1,128)} %broadcast_in_dim.9), calls=%async_computation.1 | async-start | bytes 1048576 | tf_op jit(solution)/shard_map/all_to_all | solution.py:21
  123.5 17.3 %all-to-all-start.2 = ((f32[32,1,4096]{2,1,0:T(1,128)}), f32[32,1,4096]{2,1,0:T(1,128)S(1)}, u32[]{:S(2)}, u32[]{:S(2)}) async-start(f32[32,1,4096]{2,1,0:T(1,128)} %broadcast_in_dim.10), calls=%async_computation.2 | async-start | bytes 1048576 | tf_op jit(solution)/shard_map/all_to_all | solution.py:21
  181.1 17.3 %all-to-all-start.3 = ((f32[32,1,4096]{2,1,0:T(1,128)}), f32[32,1,4096]{2,1,0:T(1,128)S(1)}, u32[]{:S(2)}, u32[]{:S(2)}) async-start(f32[32,1,4096]{2,1,0:T(1,128)} %broadcast_in_dim.11), calls=%async_computation.3 | async-start | bytes 1048576 | tf_op jit(solution)/shard_map/all_to_all | solution.py:21
where the time goes:
time: 200 us; the launch traced here: 199 us
  blocking collectives  125 us (62%)
  starting transfers between devices  26 us (13%)
  other arithmetic  23.1 us (12%)
  waiting for transfers between devices  11.2 us (6%)
  between operations  9.07 us (5%)
  local copies, waits for them, and re-layouts  5.07 us (3%)
    psum x12, blocking collectives, one_axis_at_a_time(): array = lax.psum(array, axis)  93.7 us
    all_gather x4, blocking collectives, over_pieces(): parts = lax.all_gather(array, axis)  31.1 us
    all_to_all x4, starting transfers between devices, copy_for_each(): return lax.all_to_all(copies, axis, split_axis=0, concat_axis=0, tiled=True)  26 us
    reduce_sum x3, other arithmetic, shards(): moved = jnp.sum(change * change)  11.9 us
    all_to_all x4, waiting for transfers between devices, copy_for_each(): return lax.all_to_all(copies, axis, split_axis=0, concat_axis=0, tiled=True)  11.2 us
    broadcast_in_dim x4, local copies, waits for them, and re-layouts, copy_for_each(): copies = jnp.broadcast_to(array, (lax.axis_size(axis), *array.shape))  5.05 us
    reduce_sum x1, other arithmetic, shards(): col_local = jnp.sum(extrap, axis=0)  4.91 us
  transfers between devices with their start and end apart: 4, of which 4 were waited for; matrix products, arithmetic and copies ran while one was open for 1% of the time, Pallas kernels for 0%

commit v1 on v0

v1 whole, which is shorter than its diff:
```python
import math

import jax
import jax.numpy as jnp
from jax import lax
from jax.sharding import Mesh
from jax.sharding import PartitionSpec as P

ITERS = 4
WIDE = ("wide_0", "wide_1", "wide_2")
CHIP_COLUMN = ("wide_2", "narrow")


def exchange(array, axes):
    return lax.all_to_all(array, axes, split_axis=0, concat_axis=0, tiled=True)


def shards(cost, plan, row_mass, col_mass, row_dual, col_dual):
    rows, cols = plan.shape
    half = cols // 2
    narrow_count = lax.axis_size("narrow")
    wide_count = lax.axis_size(WIDE)
    chips = wide_count // 2
    mine = lax.axis_index(("wide_0", "wide_1"))
    core = lax.axis_index("wide_2")
    column = lax.axis_index("narrow")
    step_base = 0.9 / math.sqrt(rows * wide_count + cols * narrow_count)
    weight = jnp.float32(step_base)
    row_share_mass = row_mass / narrow_count
    col_share_mass = col_mass / wide_count
    for step in range(ITERS):
        primal_step = step_base / weight
        dual_step = step_base * weight
        fresh = jnp.maximum(
            plan - primal_step * (cost - row_dual[:, None] - col_dual[None, :]), 0.0
        )
        change = fresh - plan
        extrap = fresh + change
        row_share = row_share_mass - jnp.sum(extrap, axis=1)
        col_share = col_share_mass - jnp.sum(extrap, axis=0)
        plan = fresh
        if step == ITERS - 1:
            copies = jnp.broadcast_to(col_share, (wide_count, 1, cols))
            col_left = jnp.sum(exchange(copies, WIDE), axis=(0, 1))
            row_left = jnp.sum(lax.all_gather(row_share, "narrow"), axis=0)
            row_dual = row_dual + dual_step * row_left
            col_dual = col_dual + dual_step * col_left
            break
        moved = jnp.broadcast_to(jnp.sum(change * change), (128,))
        tail = jnp.broadcast_to(jnp.concatenate([row_share, moved]), (2, rows + 128))
        sent = jnp.concatenate([col_share.reshape(2, half), tail], axis=1)
        sent = jnp.broadcast_to(sent[None], (chips, 2, half + rows + 128))
        got = exchange(sent.reshape(wide_count, 1, -1), WIDE)[:, 0]
        col_half = jnp.sum(got[:, :half], axis=0)
        row_half = lax.dynamic_index_in_dim(
            got[:, half : half + rows].reshape(chips, 2, rows), core, 1, False
        )
        scalars = jnp.stack([jnp.sum(col_half * col_half), jnp.sum(got[:, -1])])
        scalars = jnp.pad(scalars, (0, 126))
        sent = jnp.concatenate([col_half, row_half.reshape(-1), scalars])
        sent = jnp.broadcast_to(sent, (2 * narrow_count, 1, sent.shape[0]))
        got = exchange(sent, CHIP_COLUMN).reshape(2, narrow_count, -1)
        col_left = lax.dynamic_index_in_dim(got[:, :, :half], column, 1, False)
        row_left = jnp.sum(got[:, :, half : half + chips * rows], axis=1)
        left_square = jnp.sum(got[:, :, -128]) + jnp.sum(row_left * row_left)
        moved_all = 0.5 * jnp.sum(got[:, :, -127])
        own = lax.dynamic_index_in_dim(row_left.reshape(2, chips, rows), core, 0, False)
        row_dual = row_dual + dual_step * lax.dynamic_index_in_dim(own, mine, 0, False)
        col_dual = col_dual + dual_step * col_left.reshape(-1)
        dual_moved = dual_step * dual_step * left_square
        weight = jnp.sqrt(weight * jnp.sqrt((dual_moved + 1.0) / (moved_all + 1.0)))
    return (plan, row_dual, col_dual)


def solution(mesh):
    split = Mesh(
        mesh.devices.reshape(4, 4, 2, mesh.shape["narrow"]),
        ("wide_0", "wide_1", "wide_2", "narrow"),
    )
    placed = (P(WIDE, "narrow"), P(WIDE, "narrow"), P(WIDE), P("narrow"), P(WIDE), P("narrow"))
    return jax.shard_map(
        shards,
        mesh=split,
        in_specs=placed,
        out_specs=(P(WIDE, "narrow"), P(WIDE), P("narrow")),
        check_vma=False,
    )
```

time: 200 us -> 135 us (0.68)
  blocking collectives: 125 us -> 33.2 us
  waiting for transfers between devices: 11.2 us -> 28.8 us
  other arithmetic: 23.1 us -> 33.7 us
    psum x12 -> x0, blocking collectives: 93.7 us -> none  [one_axis_at_a_time(): array = lax.psum(array, axis)]
    all_to_all x0 -> x2, blocking collectives: none -> 25.9 us  [exchange(): return lax.all_to_all(array, axes, split_axis=0, concat_axis=0, tiled=True)]
    all_gather x4 -> x1, blocking collectives: 31.1 us -> 7.23 us  [shards(): row_left = jnp.sum(lax.all_gather(row_share, 'narrow'), axis=0)]
    all_to_all x4 -> x5, waiting for transfers between devices: 11.2 us -> 28.8 us  [exchange(): return lax.all_to_all(array, axes, split_axis=0, concat_axis=0, tiled=True)]
    another operation x0 -> x3, other arithmetic: none -> 4.1 us  [shards(): scalars = jnp.stack([jnp.sum(col_half * col_half), jnp.sum(got[:, -1])])]
    reduce_sum x18 -> x24, other arithmetic: 22 us -> 25.1 us  [the longest x3 11.9 us: shards(): moved = jnp.broadcast_to(jnp.sum(change * change), (128,))]
    reshape x0 -> x9, local copies, waits for them, and re-layouts: none -> 2.2 us  [the longest x3 2.03 us: shards(): got = exchange(sent.reshape(wide_count, 1, -1), WIDE)[:, 0]]
    concatenate x0 -> x9, other arithmetic: none -> 2.16 us  [the longest x6 2.14 us: shards(): sent = jnp.concatenate([col_share.reshape(2, half), tail], axis=1)]
  transfers between devices with their start and end apart: 4 -> 5, of which waited for: 4 -> 5; matrix products, arithmetic and copies ran while one was open for 1% -> 0% of each run, Pallas kernels for 0% -> 0%
where the time goes in v1:
time: 135 us; the launch traced here: 134 us
  other arithmetic  33.7 us (25%)
  blocking collectives  33.2 us (25%)
  waiting for transfers between devices  28.8 us (21%)
  starting transfers between devices  24.9 us (18%)
  between operations  7.41 us (5%)
  local copies, waits for them, and re-layouts  6.01 us (4%)
    all_to_all x5, waiting for transfers between devices, exchange(): return lax.all_to_all(array, axes, split_axis=0, concat_axis=0, tiled=True)  28.8 us
    all_to_all x2, blocking collectives, exchange(): return lax.all_to_all(array, axes, split_axis=0, concat_axis=0, tiled=True)  25.9 us
    all_to_all x5, starting transfers between devices, exchange(): return lax.all_to_all(array, axes, split_axis=0, concat_axis=0, tiled=True)  24.9 us
    reduce_sum x3, other arithmetic, shards(): moved = jnp.broadcast_to(jnp.sum(change * change), (128,))  11.9 us
    all_gather x1, blocking collectives, shards(): row_left = jnp.sum(lax.all_gather(row_share, 'narrow'), axis=0)  7.23 us
    reduce_sum x1, other arithmetic, shards(): col_share = col_share_mass - jnp.sum(extrap, axis=0)  4.91 us
    another operation x3, other arithmetic, shards(): scalars = jnp.stack([jnp.sum(col_half * col_half), jnp.sum(got[:, -1])])  4.1 us
    reduce_sum x6, other arithmetic, shards(): scalars = jnp.stack([jnp.sum(col_half * col_half), jnp.sum(got[:, -1])])  3.82 us
  transfers between devices with their start and end apart: 5, of which 5 were waited for; matrix products, arithmetic and copies ran while one was open for 0% of the time, Pallas kernels for 0%

profile of v1, /device:TPU:1, one launch (start us, length us, event | category | flops | bytes accessed | tf_op | source)
XLA Modules:
  0.0 134.0 jit_solution(9512962981400979611)
XLA Ops:
  0.7 4.0 %multiply_reduce_fusion.2 = (f32[]{:T(128)}, f32[128]{0:T(128)S(1)}, f32[4096]{0:T(1024)S(1)}) fusion(f32[128,4096]{1,0:T(8,128)} %param.7, f32[4096]{0:T(1024)} %param.11, f32[128,4096]{1,0:T(8,128)} %param.6, f32[128]{0:T(128)} %param.10), kind=kLoop, calls=%fused_computation.6 | loop fusion | flops 5238655 | bytes 4228100 | tf_op jit(solution)/shard_map/reduce_sum | solution.py:49
  4.7 0.8 fusion.8
  5.7 1.2 reshape.99
  6.8 9.4 %all-to-all-start = ((f32[32,1,2304]{2,1,0:T(1,128)}), f32[32,1,2304]{2,1,0:T(1,128)S(1)}, u32[]{:S(2)}, u32[]{:S(2)}) async-start(f32[32,1,2304]{2,1,0:T(1,128)} %reshape.99), calls=%async_computation | async-start | bytes 589824 | tf_op jit(solution)/shard_map/all_to_all | solution.py:15
  16.2 9.3 %all-to-all-done = f32[32,1,2304]{2,1,0:T(1,128)S(1)} async-done(((f32[32,1,2304]{2,1,0:T(1,128)}), f32[32,1,2304]{2,1,0:T(1,128)S(1)}, u32[]{:S(2)}, u32[]{:S(2)}) %all-to-all-start) | async-done | bytes 294944 | tf_op jit(solution)/shard_map/all_to_all | solution.py:15
  25.5 0.7 slice_reduce_fusion.8
  26.3 0.6 multiply_reduce_fusion.8
  26.9 1.4 %select_maximum_fusion.2 = f32[128]{0:T(128)S(1)} fusion(f32[1]{0:T(128)} %bitcast.3, f32[1]{0:T(128)} %bitcast.2), kind=kLoop, calls=%fused_computation.81 | loop fusion | flops 512 | bytes 520 | tf_op jit(solution)/shard_map/stack | solution.py:58
  28.3 0.7 broadcast_in_dim.22
  29.0 4.6 %all-to-all-start.1 = ((f32[8,1,4224]{2,1,0:T(1,128)}), f32[8,1,4224]{2,1,0:T(1,128)S(1)}, u32[]{:S(2)}, u32[]{:S(2)}) async-start(f32[8,1,4224]{2,1,0:T(1,128)} %broadcast_in_dim.22), calls=%async_computation.1 | async-start | bytes 270336 | tf_op jit(solution)/shard_map/all_to_all | solution.py:15
  33.6 5.2 %all-to-all-done.1 = f32[8,1,4224]{2,1,0:T(1,128)S(1)} async-done(((f32[8,1,4224]{2,1,0:T(1,128)}), f32[8,1,4224]{2,1,0:T(1,128)S(1)}, u32[]{:S(2)}, u32[]{:S(2)}) %all-to-all-start.1) | async-done | bytes 135200 | tf_op jit(solution)/shard_map/all_to_all | solution.py:15
  38.8 0.3 reduce.10
  39.2 0.7 slice_reduce_fusion.13
  39.9 0.6 multiply_reduce_fusion.5
  42.8 3.7 %multiply_reduce_fusion.1 = (f32[]{:T(128)}, f32[4096]{0:T(1024)S(1)}, f32[128]{0:T(128)S(1)}) fusion(f32[4096]{0:T(1024)S(1)} %add.118, f32[128,4096]{1,0:T(8,128)} %param.6, f32[128]{0:T(128)S(1)} %fusion.11, f32[]{:T(128)S(6)} %div.35, f32[128,4096]{1,0:T(8,128)S(1)} %copy-done, f32[4096]{0:T(1024)S(1)} %copy-done.1, f32[128]{0:T(128)S(1)} %copy-done.3), kind=kLoop, calls=%fused_computation.4 | loop fusion | flops 7860095 | bytes 4245000 | tf_op jit(solution)/shard_map/reduce_sum | solution.py:49
  46.5 0.7 pad_select_fusion.1
  47.3 0.4 reshape.105
  47.7 13.0 %all_to_all.35 = f32[32,1,2304]{2,1,0:T(1,128)S(1)} all-to-all(f32[32,1,2304]{2,1,0:T(1,128)S(1)} %reshape.105), channel_id=1, replica_groups=mesh['wide_0'=4,'wide_1'=4,'wide_2'=2,'narrow'=4] {'wide_0','wide_1','wi..., dimensions={0} | all-to-all | bytes 589824 | tf_op jit(solution)/shard_map/all_to_all | solution.py:15
  60.7 0.7 slice_reduce_fusion.7
  61.4 0.6 multiply_reduce_fusion.7
  62.0 1.4 %select_maximum_fusion.1 = f32[128]{0:T(128)S(1)} fusion(f32[1]{0:T(128)} %bitcast.9, f32[1]{0:T(128)} %bitcast.8), kind=kLoop, calls=%fused_computation.80 | loop fusion | flops 512 | bytes 520 | tf_op jit(solution)/shard_map/stack | solution.py:58
  63.4 0.7 broadcast_in_dim.25
  64.2 3.5 %all-to-all-start.3 = ((f32[8,1,4224]{2,1,0:T(1,128)}), f32[8,1,4224]{2,1,0:T(1,128)S(1)}, u32[]{:S(2)}, u32[]{:S(2)}) async-start(f32[8,1,4224]{2,1,0:T(1,128)} %broadcast_in_dim.25), calls=%async_computation.3 | async-start | bytes 270336 | tf_op jit(solution)/shard_map/all_to_all | solution.py:15
  67.6 5.2 %all-to-all-done.3 = f32[8,1,4224]{2,1,0:T(1,128)S(1)} async-done(((f32[8,1,4224]{2,1,0:T(1,128)}), f32[8,1,4224]{2,1,0:T(1,128)S(1)}, u32[]{:S(2)}, u32[]{:S(2)}) %all-to-all-start.3) | async-done | bytes 135200 | tf_op jit(solution)/shard_map/all_to_all | solution.py:15
  72.8 0.3 reduce.11
  73.2 0.7 slice_reduce_fusion.11
  74.6 0.6 multiply_reduce_fusion.4
  76.8 4.2 %multiply_reduce_fusion = (f32[]{:T(128)}, f32[4096]{0:T(1024)S(1)}, f32[128]{0:T(128)S(1)}) fusion(f32[4096]{0:T(1024)S(1)} %add.124, f32[128,4096]{1,0:T(8,128)} %param.6, f32[128]{0:T(128)S(1)} %fusion.14, f32[]{:T(128)S(6)} %div.37, f32[4096]{0:T(1024)S(1)} %add.118, f32[128]{0:T(128)S(1)} %fusion.11, f32[]{:T(128)S(6)} %div.35, ...), kind=kLoop, calls=%fused_computation.2 | loop fusion | flops 10481535 | bytes 4261900 | tf_op jit(solution)/shard_map/reduce_sum | solution.py:49
  81.0 0.7 pad_select_fusion
  81.7 0.4 reshape.111
  82.2 13.0 %all_to_all.36 = f32[32,1,2304]{2,1,0:T(1,128)S(1)} all-to-all(f32[32,1,2304]{2,1,0:T(1,128)S(1)} %reshape.111), channel_id=1, replica_groups=mesh['wide_0'=4,'wide_1'=4,'wide_2'=2,'narrow'=4] {'wide_0','wide_1','wi..., dimensions={0} | all-to-all | bytes 589824 | tf_op jit(solution)/shard_map/all_to_all | solution.py:15
  95.2 0.7 slice_reduce_fusion.6
  95.9 0.6 multiply_reduce_fusion.6
  96.5 1.4 %select_maximum_fusion = f32[128]{0:T(128)S(1)} fusion(f32[1]{0:T(128)} %bitcast.15, f32[1]{0:T(128)} %bitcast.14), kind=kLoop, calls=%fused_computation.79 | loop fusion | flops 512 | bytes 520 | tf_op jit(solution)/shard_map/stack | solution.py:58
  97.9 0.7 broadcast_in_dim.28
  98.6 3.5 %all-to-all-start.5 = ((f32[8,1,4224]{2,1,0:T(1,128)}), f32[8,1,4224]{2,1,0:T(1,128)S(1)}, u32[]{:S(2)}, u32[]{:S(2)}) async-start(f32[8,1,4224]{2,1,0:T(1,128)} %broadcast_in_dim.28), calls=%async_computation.5 | async-start | bytes 270336 | tf_op jit(solution)/shard_map/all_to_all | solution.py:15
  102.1 5.2 %all-to-all-done.5 = f32[8,1,4224]{2,1,0:T(1,128)S(1)} async-done(((f32[8,1,4224]{2,1,0:T(1,128)}), f32[8,1,4224]{2,1,0:T(1,128)S(1)}, u32[]{:S(2)}, u32[]{:S(2)}) %all-to-all-start.5) | async-done | bytes 135200 | tf_op jit(solution)/shard_map/all_to_all | solution.py:15
  107.3 0.3 reduce.12
  107.7 0.7 slice_reduce_fusion.9
  109.1 0.6 multiply_reduce_fusion.3
  111.2 4.9 %fusion.6 = (f32[4096]{0:T(1024)S(1)}, f32[128]{0:T(128)S(1)}, f32[128,4096]{1,0:T(8,128)}) fusion(f32[4096]{0:T(1024)S(1)} %add.124, f32[128,4096]{1,0:T(8,128)} %param.6, f32[128]{0:T(128)S(1)} %fusion.14, f32[]{:T(128)S(6)} %div.37, f32[4096]{0:T(1024)S(1)} %add.118, f32[128]{0:T(128)S(1)} %fusion.11, f32[]{:T(128)S(6)} %div.35, ...), kind=kLoop, calls=%fused_computation.17 | loop fusion | flops 12054400 | bytes 6375948 | tf_op jit(solution)/shard_map/reduce_sum | solution.py:40
  116.1 1.3 broadcast_in_dim.29
  117.4 3.9 %all-to-all-start.6 = ((f32[32,1,4096]{2,1,0:T(1,128)}), f32[32,1,4096]{2,1,0:T(1,128)S(1)}, u32[]{:S(2)}, u32[]{:S(2)}) async-start(f32[32,1,4096]{2,1,0:T(1,128)} %broadcast_in_dim.29), calls=%async_computation.6 | async-start | bytes 1048576 | tf_op jit(solution)/shard_map/all_to_all | solution.py:15
  121.4 7.2 %all-gather.1 = f32[4,1,128]{2,1,0:T(1,128)S(1)} all-gather(f32[1,1,128]{2,1,0:T(1,128)S(1)} %subtract_bitcast_fusion), channel_id=2, replica_groups=mesh['wide_0'=4,'wide_1'=4,'wide_2'=2,'narrow'=4] {'narrow'}, dimensions={0}, use_global_device_ids=true | all-gather | bytes 2560 | tf_op jit(solution)/shard_map/all_gather | solution.py:45
  128.6 0.5 multiply_add_fusion.1
  129.1 3.9 %all-to-all-done.6 = f32[32,1,4096]{2,1,0:T(1,128)S(1)} async-done(((f32[32,1,4096]{2,1,0:T(1,128)}), f32[32,1,4096]{2,1,0:T(1,128)S(1)}, u32[]{:S(2)}, u32[]{:S(2)}) %all-to-all-start.6) | async-done | bytes 524320 | tf_op jit(solution)/shard_map/all_to_all | solution.py:15
  133.1 0.4 reduce_sum.339
  133.4 0.6 multiply_add_fusion
  (61 shorter events, 1.0 us)
Async XLA Ops:
  0.6 4.1 %copy-start.2 = (f32[4096]{0:T(1024)S(1)}, f32[4096]{0:T(1024)}, u32[]{:S(2)}) copy-start(f32[4096]{0:T(1024)} %param.9) | copy-start | bytes 49156
  0.6 4.1 %copy-start.4 = (f32[128]{0:T(128)S(1)}, f32[128]{0:T(128)}, u32[]{:S(2)}) copy-start(f32[128]{0:T(128)} %param.8) | copy-start | bytes 1540
  4.7 38.0 %copy-start.1 = (f32[4096]{0:T(1024)S(1)}, f32[4096]{0:T(1024)}, u32[]{:S(2)}) copy-start(f32[4096]{0:T(1024)} %param.11) | copy-start | bytes 49156
  4.7 38.0 %copy-start.3 = (f32[128]{0:T(128)S(1)}, f32[128]{0:T(128)}, u32[]{:S(2)}) copy-start(f32[128]{0:T(128)} %param.10) | copy-start | bytes 1540
  4.7 38.1 %copy-start = (f32[128,4096]{1,0:T(8,128)S(1)}, f32[128,4096]{1,0:T(8,128)}, u32[]{:S(2)}) copy-start(f32[128,4096]{1,0:T(8,128)} %param.7) | copy-start | bytes 6291460
  6.8 18.7 %all-to-all-start = ((f32[32,1,2304]{2,1,0:T(1,128)}), f32[32,1,2304]{2,1,0:T(1,128)S(1)}, u32[]{:S(2)}, u32[]{:S(2)}) async-start(f32[32,1,2304]{2,1,0:T(1,128)} %reshape.99), calls=%async_computation | async-start | bytes 589824 | tf_op jit(solution)/shard_map/all_to_all | solution.py:15
  29.0 9.8 %all-to-all-start.1 = ((f32[8,1,4224]{2,1,0:T(1,128)}), f32[8,1,4224]{2,1,0:T(1,128)S(1)}, u32[]{:S(2)}, u32[]{:S(2)}) async-start(f32[8,1,4224]{2,1,0:T(1,128)} %broadcast_in_dim.22), calls=%async_computation.1 | async-start | bytes 270336 | tf_op jit(solution)/shard_map/all_to_all | solution.py:15
  64.2 8.7 %all-to-all-start.3 = ((f32[8,1,4224]{2,1,0:T(1,128)}), f32[8,1,4224]{2,1,0:T(1,128)S(1)}, u32[]{:S(2)}, u32[]{:S(2)}) async-start(f32[8,1,4224]{2,1,0:T(1,128)} %broadcast_in_dim.25), calls=%async_computation.3 | async-start | bytes 270336 | tf_op jit(solution)/shard_map/all_to_all | solution.py:15
  98.6 8.7 %all-to-all-start.5 = ((f32[8,1,4224]{2,1,0:T(1,128)}), f32[8,1,4224]{2,1,0:T(1,128)S(1)}, u32[]{:S(2)}, u32[]{:S(2)}) async-start(f32[8,1,4224]{2,1,0:T(1,128)} %broadcast_in_dim.28), calls=%async_computation.5 | async-start | bytes 270336 | tf_op jit(solution)/shard_map/all_to_all | solution.py:15
  117.4 15.7 %all-to-all-start.6 = ((f32[32,1,4096]{2,1,0:T(1,128)}), f32[32,1,4096]{2,1,0:T(1,128)S(1)}, u32[]{:S(2)}, u32[]{:S(2)}) async-start(f32[32,1,4096]{2,1,0:T(1,128)} %broadcast_in_dim.29), calls=%async_computation.6 | async-start | bytes 1048576 | tf_op jit(solution)/shard_map/all_to_all | solution.py:15

commit v2 on v0

v2 whole, which is shorter than its diff:
```python
import functools
import math

import jax
import jax.numpy as jnp
from jax import lax
from jax.experimental import pallas as pl
from jax.experimental.pallas import tpu as pltpu
from jax.sharding import Mesh
from jax.sharding import PartitionSpec as P

ITERS = 4
LANES = 128
GROUP = 8
CHUNKS = 4
WIDE = ("wide_0", "wide_1", "wide_2")
CHIP_COLUMN = ("wide_2", "narrow")


def exchange(array, axes):
    return lax.all_to_all(array, axes, split_axis=0, concat_axis=0, tiled=True)


def total(block):
    return jnp.sum(jnp.sum(block, axis=0, keepdims=True), axis=1, keepdims=True)


def down(block):
    return jnp.sum(block, axis=0, keepdims=True)


def dual_update(got, weight, row_dual, col_dual, new_row, new_col, left_rows, sizes):
    narrow, base, half = sizes
    core, column = lax.axis_index("wide_2"), lax.axis_index("narrow")
    mine = lax.axis_index("wide_0") * lax.axis_size("wide_1") + lax.axis_index("wide_1")
    squares = jnp.zeros((GROUP, LANES), jnp.float32)
    for c in range(2):
        for r in range(0, half, GROUP):
            rows = got[c * narrow, half + r : half + r + GROUP, :]
            for n in range(1, narrow):
                rows = rows + got[c * narrow + n, half + r : half + r + GROUP, :]
            squares = squares + rows * rows
            left_rows[c * half + r : c * half + r + GROUP, :] = rows
    tails = got[0, 2 * half : 2 * half + GROUP, :]
    for n in range(1, 2 * narrow):
        tails = tails + got[n, 2 * half : 2 * half + GROUP, :]
    left_square = total(squares) + total(tails[0:1, :])
    moved = 0.5 * total(tails[1:2, :])
    old = weight[...]
    dual_step = base * old
    dual_moved = dual_step * dual_step * left_square
    fresh_weight = jnp.sqrt(old * jnp.sqrt((dual_moved + 1.0) / (moved + 1.0)))
    step = dual_step[0:1, :]
    new_row[...] = row_dual[...] + step * left_rows[pl.ds(core * half + mine, 1), :]
    for c in range(2):
        span = slice(c * half, (c + 1) * half)
        new_col[span, :] = col_dual[span, :] + step * got[c * narrow + column, 0:half, :]
    return base / fresh_weight, fresh_weight


def sweep(step, cost, plan, fresh_plan, row_all, col_dual, first, last, rows_so_far, moved, done):
    groups = len(rows_so_far)

    def tile(j, state):
        rows, moved = list(state[0]), state[1]
        lanes = pl.ds(pl.multiple_of(j * LANES, LANES), LANES)
        col = jnp.broadcast_to(col_dual[pl.ds(j, 1), :], (GROUP, LANES))
        cols = None
        for g in range(groups):
            span = slice(g * GROUP, (g + 1) * GROUP)
            old = plan[span, lanes]
            gap = cost[span, lanes] - row_all[span, :] - col
            fresh = jnp.maximum(old - step * gap, 0.0)
            change = fresh - old
            extrap = fresh + change
            fresh_plan[span, lanes] = fresh
            rows[g] = rows[g] + extrap
            cols = extrap if cols is None else cols + extrap
            moved = moved + change * change
        done(j, down(cols))
        return tuple(rows), moved

    return lax.fori_loop(first, last, tile, (tuple(rows_so_far), moved), unroll=2)


def spread_rows(row_dual, row_all):
    row_all[...] = jnp.transpose(jnp.broadcast_to(row_dual, (LANES, LANES)))


def gather_rows(rows):
    return down(jnp.transpose(jnp.concatenate(rows, axis=0)))


def zeros(groups):
    zero = jnp.zeros((GROUP, LANES), jnp.float32)
    return tuple(zero for _ in range(groups)), zero


def send_first(sent, col_mass, chips, half):
    def done(j, cols):
        upper = j // half
        lanes = pl.ds(pl.multiple_of((j - upper * half) * LANES, LANES), LANES)
        share = col_mass[pl.ds(j, 1), :] * (1.0 / (2 * chips)) - cols
        for p in range(chips):
            sent[2 * p + upper, :, lanes] = share

    return done


def send_tail(sent, chips, half, row_share, moved):
    for p in range(2 * chips):
        sent[p, :, half * LANES : (half + 1) * LANES] = row_share
        sent[p, :, (half + 1) * LANES : (half + 2) * LANES] = moved


def open_kernel(sizes, *refs):
    narrow, base, half, chips = sizes
    sources, targets, (sent, weight, row_all, sems) = refs[:6], refs[6:12], refs[12:]
    cost, plan, row_mass, col_mass, row_dual, col_dual = targets
    tiles = 2 * half // CHUNKS
    weight[...] = jnp.full((GROUP, LANES), base, jnp.float32)
    small = [pltpu.make_async_copy(sources[n], targets[n], sems.at[n, 0]) for n in range(2, 6)]
    for copy in small:
        copy.start()
    copies = []
    for k in range(CHUNKS):
        lanes = slice(k * tiles * LANES, (k + 1) * tiles * LANES)
        for n in range(2):
            copy = pltpu.make_async_copy(
                sources[n].at[:, lanes], targets[n].at[:, lanes], sems.at[n, k]
            )
            copy.start()
            copies.append(copy)
    for copy in small:
        copy.wait()
    spread_rows(row_dual[...], row_all)
    rows, moved = zeros(row_all.shape[0] // GROUP)
    done = send_first(sent, col_mass, chips, half)
    for k in range(CHUNKS):
        copies[2 * k].wait()
        copies[2 * k + 1].wait()
        rows, moved = sweep(
            jnp.float32(1.0), cost, plan, plan, row_all, col_dual,
            k * tiles, (k + 1) * tiles, rows, moved, done,
        )
    row_share = row_mass[...] * (1.0 / narrow) - gather_rows(rows)
    send_tail(sent, chips, half, row_share, down(moved))


def middle_kernel(
    sizes, got, weight, cost, plan, row_mass, col_mass, row_dual, col_dual,
    fresh_plan, sent, new_weight, new_row, new_col, row_all, left_rows,
):
    narrow, base, half, chips = sizes
    step, fresh_weight = dual_update(
        got, weight, row_dual, col_dual, new_row, new_col, left_rows, sizes[:3]
    )
    new_weight[...] = fresh_weight
    spread_rows(new_row[...], row_all)
    rows, moved = zeros(row_all.shape[0] // GROUP)
    done = send_first(sent, col_mass, chips, half)
    rows, moved = sweep(
        step, cost, plan, fresh_plan, row_all, new_col, 0, 2 * half, rows, moved, done
    )
    row_share = row_mass[...] * (1.0 / narrow) - gather_rows(rows)
    send_tail(sent, chips, half, row_share, down(moved))


def close_kernel(
    sizes, got, weight, cost, plan, row_mass, col_mass, row_dual, col_dual,
    plan_out, sent, row_sent, new_weight, new_row, new_col, row_all, left_rows, fresh_plan, sems,
):
    narrow, base, half, chips = sizes
    step, fresh_weight = dual_update(
        got, weight, row_dual, col_dual, new_row, new_col, left_rows, sizes[:3]
    )
    new_weight[...] = fresh_weight
    spread_rows(new_row[...], row_all)
    rows, moved = zeros(row_all.shape[0] // GROUP)

    def done(j, cols):
        share = col_mass[pl.ds(j, 1), :] * (1.0 / (2 * chips)) - cols
        for p in range(2 * chips):
            sent[p, pl.ds(j, 1), :] = share

    tiles = 2 * half // CHUNKS
    copies = []
    for k in range(CHUNKS):
        rows, moved = sweep(
            step, cost, plan, fresh_plan, row_all, new_col,
            k * tiles, (k + 1) * tiles, rows, moved, done,
        )
        lanes = slice(k * tiles * LANES, (k + 1) * tiles * LANES)
        copy = pltpu.make_async_copy(fresh_plan.at[:, lanes], plan_out.at[:, lanes], sems.at[k])
        copy.start()
        copies.append(copy)
    row_sent[...] = row_mass[...] * (1.0 / narrow) - gather_rows(rows)
    for copy in copies:
        copy.wait()


def reduce_kernel(sizes, got, sent, held):
    narrow, base, half, chips = sizes
    core = lax.axis_index("wide_2")
    cols = got[0]
    for p in range(1, 2 * chips):
        cols = cols + got[p]
    squares = jnp.zeros((1, LANES), jnp.float32)
    for r in range(half):
        col = cols[:, r * LANES : (r + 1) * LANES]
        squares = squares + col * col
        held[r : r + 1, :] = col
        held[half + r : half + r + 1, :] = got[2 * r + core, :, half * LANES : (half + 1) * LANES]
    moved = cols[:, (half + 1) * LANES : (half + 2) * LANES]
    place_of = lax.broadcasted_iota(jnp.int32, (GROUP, LANES), 0)
    held[2 * half : 2 * half + GROUP, :] = jnp.where(
        place_of == 0, squares, jnp.where(place_of == 1, moved, 0.0)
    )
    everything = held[...]
    for q in range(2 * narrow):
        sent[q] = everything


def finish_kernel(sizes, got, row_got, weight, row_dual, col_dual, row_out, col_out):
    narrow, base, half, chips = sizes
    cols = got[0]
    for p in range(1, 2 * chips):
        cols = cols + got[p]
    rows = row_got[0]
    for n in range(1, narrow):
        rows = rows + row_got[n]
    step = base * weight[0:1, :]
    col_out[...] = col_dual[...] + step * cols
    row_out[...] = row_dual[...] + step * rows


VM = pl.BlockSpec(memory_space=pltpu.VMEM)
HB = pl.BlockSpec(memory_space=pltpu.HBM)
ROOM = pltpu.CompilerParams(vmem_limit_bytes=16 << 20)


def shards(cost, plan, row_mass, col_mass, row_dual, col_dual):
    rows, cols = plan.shape
    tiles = cols // LANES
    half = tiles // 2
    narrow = lax.axis_size("narrow")
    wide = lax.axis_size(WIDE)
    chips = wide // 2
    base = 0.9 / math.sqrt(rows * wide + cols * narrow)
    sizes = (narrow, base, half, chips)
    row_mass, row_dual = row_mass.reshape(1, rows), row_dual.reshape(1, rows)
    col_mass, col_dual = col_mass.reshape(tiles, LANES), col_dual.reshape(tiles, LANES)

    def vm(*shape):
        return pltpu.VMEM(shape, jnp.float32)

    def near(array):
        return pltpu.with_memory_space_constraint(array, pltpu.VMEM)

    f32 = vm

    first = f32(wide, 1, (half + 2) * LANES)
    second = f32(2 * narrow, 2 * half + GROUP, LANES)
    big, state, one, many = (rows, cols), f32(GROUP, LANES), f32(1, rows), f32(tiles, LANES)
    scratch = [vm(rows, LANES), vm(2 * half, LANES)]

    inputs = (cost, plan, row_mass, col_mass, row_dual, col_dual)
    *held, sent, weight = pl.pallas_call(
        functools.partial(open_kernel, sizes),
        out_shape=(vm(*big), vm(*big), one, many, one, many, first, state),
        in_specs=[HB] * 6,
        out_specs=(VM,) * 8,
        scratch_shapes=[scratch[0], pltpu.SemaphoreType.DMA((6, CHUNKS))],
        compiler_params=ROOM,
        name="open_step",
    )(*(pltpu.with_memory_space_constraint(array, pltpu.HBM) for array in inputs))
    cost, plan, row_mass, col_mass, row_dual, col_dual = held
    for step in range(1, ITERS):
        got = exchange(sent, WIDE)
        sent = pl.pallas_call(
            functools.partial(reduce_kernel, sizes),
            out_shape=second,
            compiler_params=ROOM,
            in_specs=[VM],
            out_specs=VM,
            scratch_shapes=[vm(2 * half + GROUP, LANES)],
            name="reduce_step",
        )(near(got))
        got = exchange(sent, CHIP_COLUMN)
        operands = tuple(map(near, (got, weight, cost, plan, row_mass, col_mass, row_dual, col_dual)))
        if step < ITERS - 1:
            plan, sent, weight, row_dual, col_dual = pl.pallas_call(
                functools.partial(middle_kernel, sizes),
                out_shape=(f32(*big), first, state, one, many),
                in_specs=[VM] * 8,
                out_specs=(VM,) * 5,
                scratch_shapes=scratch,
                name="middle_step",
                compiler_params=ROOM,
            )(*operands)
        else:
            plan, sent, row_sent, weight, row_dual, col_dual = pl.pallas_call(
                functools.partial(close_kernel, sizes),
                out_shape=(jax.ShapeDtypeStruct(big, jnp.float32), vm(wide, tiles, LANES), one, state, one, many),
                in_specs=[VM] * 8,
                out_specs=(HB,) + (VM,) * 5,
                scratch_shapes=scratch + [vm(*big), pltpu.SemaphoreType.DMA((CHUNKS,))],
                name="close_step",
                compiler_params=ROOM,
            )(*operands)
    got = exchange(sent, WIDE)
    row_got = lax.all_gather(row_sent, "narrow")
    row_dual, col_dual = pl.pallas_call(
        functools.partial(finish_kernel, sizes),
        out_shape=tuple(jax.ShapeDtypeStruct(s.shape, s.dtype) for s in (one, many)),
        in_specs=[VM] * 5,
        out_specs=(VM, VM),
        name="finish_step",
        compiler_params=ROOM,
    )(near(got), row_got, weight, row_dual, col_dual)
    return (plan, row_dual.reshape(rows), col_dual.reshape(cols))


def solution(mesh):
    split = Mesh(
        mesh.devices.reshape(4, 4, 2, mesh.shape["narrow"]),
        ("wide_0", "wide_1", "wide_2", "narrow"),
    )
    placed = (P(WIDE, "narrow"), P(WIDE, "narrow"), P(WIDE), P("narrow"), P(WIDE), P("narrow"))
    return jax.shard_map(
        shards,
        mesh=split,
        in_specs=placed,
        out_specs=(P(WIDE, "narrow"), P(WIDE), P("narrow")),
        check_vma=False,
    )
```

time: 200 us -> 97.3 us (0.49)
  blocking collectives: 125 us -> 78.7 us
  other arithmetic: 23.1 us -> 0 us
  starting transfers between devices: 26 us -> 3.81 us
  Pallas kernels: 0 us -> 9.46 us
  between operations: 9.07 us -> 0.68 us
  waiting for transfers between devices: 11.2 us -> 4.28 us
  local copies, waits for them, and re-layouts: 5.07 us -> 0 us
    psum x12 -> x0, blocking collectives: 93.7 us -> none  [one_axis_at_a_time(): array = lax.psum(array, axis)]
    all_to_all x0 -> x6, blocking collectives: none -> 71.3 us  [exchange(): return lax.all_to_all(array, axes, split_axis=0, concat_axis=0, tiled=True)]
    all_gather x4 -> x1, blocking collectives: 31.1 us -> 7.43 us  [shards(): row_got = lax.all_gather(row_sent, 'narrow')]
    all_to_all x4 -> x1, starting transfers between devices: 26 us -> 3.81 us  [exchange(): return lax.all_to_all(array, axes, split_axis=0, concat_axis=0, tiled=True)]
    reduce_sum x18 -> x0, other arithmetic: 22 us -> none  [the longest x3 11.9 us: shards(): moved = jnp.sum(change * change)]
    pallas_call x0 -> x8, Pallas kernels: none -> 9.46 us  [the longest x1 3.08 us: shards(): pl.pallas_call(functools.partial(close_kernel, sizes), out_shape=(jax.Sha...]
    all_to_all x4 -> x1, waiting for transfers between devices: 11.2 us -> 4.28 us  [exchange(): return lax.all_to_all(array, axes, split_axis=0, concat_axis=0, tiled=True)]
    broadcast_in_dim x4 -> x0, local copies, waits for them, and re-layouts: 5.05 us -> none  [copy_for_each(): copies = jnp.broadcast_to(array, (lax.axis_size(axis), *array.shape))]
  transfers between devices with their start and end apart: 4 -> 1, of which waited for: 4 -> 1; matrix products, arithmetic and copies ran while one was open for 1% -> 0% of each run, Pallas kernels for 0% -> 0%
where the time goes in v2:
time: 97.3 us; the launch traced here: 96.9 us
  blocking collectives  78.7 us (81%)
  Pallas kernels  9.46 us (10%)
  waiting for transfers between devices  4.28 us (4%)
  starting transfers between devices  3.81 us (4%)
    all_to_all x6, blocking collectives, exchange(): return lax.all_to_all(array, axes, split_axis=0, concat_axis=0, tiled=True)  71.3 us
    all_gather x1, blocking collectives, shards(): row_got = lax.all_gather(row_sent, 'narrow')  7.43 us
    all_to_all x1, waiting for transfers between devices, exchange(): return lax.all_to_all(array, axes, split_axis=0, concat_axis=0, tiled=True)  4.28 us
    all_to_all x1, starting transfers between devices, exchange(): return lax.all_to_all(array, axes, split_axis=0, concat_axis=0, tiled=True)  3.81 us
    pallas_call x1, Pallas kernels, shards(): pl.pallas_call(functools.partial(close_kernel, sizes), out_shape=(jax.Sha...  3.08 us
    pallas_call x1, Pallas kernels, shards(): pl.pallas_call(functools.partial(open_kernel, sizes), out_shape=(vm(*big)...  2.78 us
    pallas_call x2, Pallas kernels, shards(): pl.pallas_call(functools.partial(middle_kernel, sizes), out_shape=(f32(*b...  2.76 us
  transfers between devices with their start and end apart: 1, of which 1 were waited for; matrix products, arithmetic and copies ran while one was open for 0% of the time, Pallas kernels for 0%

profile of v2, /device:TPU:1, one launch (start us, length us, event | category | flops | bytes accessed | tf_op | source)
XLA Modules:
  0.0 96.9 jit_solution(209531106482303856)
XLA Ops:
  0.6 2.8 %open_step.1 = (f32[128,4096]{1,0:T(8,128)S(1)}, f32[128,4096]{1,0:T(8,128)S(1)}, f32[1,128]{1,0:T(1,128)S(1)}, f32[32,128]{1,0:T(8,128)S(1)}, f32[1,128]{1,0:T(...) custom-call(f32[128,4096]{1,0:T(8,128)} %refs_0_.1, f32[128,4096]{1,0:T(8,128)} %refs_1_.1, ...), custom_call_target="tpu_custom_call" | custom-call | tf_op jit(solution)/shard_map/open_step/pallas_call | solution.py:268
  3.4 18.5 %all_to_all.35.got = f32[32,1,2304]{2,1,0:T(1,128)S(1)} all-to-all(f32[32,1,2304]{2,1,0:T(1,128)S(1)} %get-tuple-element.29), channel_id=1, replica_groups=mesh['wide_0'=4,'wide_1'=4,'wide_2'=2,'narrow'=4] {'wide_0','wide_1','wi..., dimensions={0} | all-to-all | bytes 589824 | tf_op jit(solution)/shard_map/all_to_all | solution.py:21
  21.9 0.1 reduce_step.3
  22.0 9.9 %all_to_all.36.got = f32[8,40,128]{2,1,0:T(8,128)S(1)} all-to-all(f32[8,40,128]{2,1,0:T(8,128)S(1)} %reduce_step.3), channel_id=1, replica_groups=mesh['wide_0'=4,'wide_1'=4,'wide_2'=2,'narrow'=4] {'wide_2','narrow'}, dimensions={0} | all-to-all | bytes 327680 | tf_op jit(solution)/shard_map/all_to_all | solution.py:21
  31.9 1.4 %middle_step.2 = (f32[128,4096]{1,0:T(8,128)S(1)}, f32[32,1,2304]{2,1,0:T(1,128)S(1)}, f32[8,128]{1,0:T(8,128)S(1)}, f32[1,128]{1,0:T(1,128)S(1)}, f32[32,128]{1,0:T(8,128)S(1)}) custom-call(f32[8,40,128]{2,1,0:T(8,128)S(1)} %all_to_all.36.got, f32[8,128]{1,0:T(8,128)S(1)} %get-tuple-element.30.weight, f32[128,4096]{1,0:T(8,128)S(1)} %get-tuple-element.31.cost, ...), custom_call_target="tpu_custom_call" | custom-call | tf_op jit(solution)/shard_map/middle_step/pallas_call | solution.py:292
  33.3 12.8 %all_to_all.37.got = f32[32,1,2304]{2,1,0:T(1,128)S(1)} all-to-all(f32[32,1,2304]{2,1,0:T(1,128)S(1)} %get-tuple-element.37), channel_id=1, replica_groups=mesh['wide_0'=4,'wide_1'=4,'wide_2'=2,'narrow'=4] {'wide_0','wide_1','wi..., dimensions={0} | all-to-all | bytes 589824 | tf_op jit(solution)/shard_map/all_to_all | solution.py:21
  46.1 0.1 reduce_step.4
  46.2 8.6 %all_to_all.38.got = f32[8,40,128]{2,1,0:T(8,128)S(1)} all-to-all(f32[8,40,128]{2,1,0:T(8,128)S(1)} %reduce_step.4), channel_id=1, replica_groups=mesh['wide_0'=4,'wide_1'=4,'wide_2'=2,'narrow'=4] {'wide_2','narrow'}, dimensions={0} | all-to-all | bytes 327680 | tf_op jit(solution)/shard_map/all_to_all | solution.py:21
  54.8 1.4 %middle_step.3 = (f32[128,4096]{1,0:T(8,128)S(1)}, f32[32,1,2304]{2,1,0:T(1,128)S(1)}, f32[8,128]{1,0:T(8,128)S(1)}, f32[1,128]{1,0:T(1,128)S(1)}, f32[32,128]{1,0:T(8,128)S(1)}) custom-call(f32[8,40,128]{2,1,0:T(8,128)S(1)} %all_to_all.38.got, f32[8,128]{1,0:T(8,128)S(1)} %get-tuple-element.38.weight, f32[128,4096]{1,0:T(8,128)S(1)} %get-tuple-element.31.cost, ...), custom_call_target="tpu_custom_call" | custom-call | tf_op jit(solution)/shard_map/middle_step/pallas_call | solution.py:292
  56.1 12.8 %all_to_all.39.got = f32[32,1,2304]{2,1,0:T(1,128)S(1)} all-to-all(f32[32,1,2304]{2,1,0:T(1,128)S(1)} %get-tuple-element.42), channel_id=1, replica_groups=mesh['wide_0'=4,'wide_1'=4,'wide_2'=2,'narrow'=4] {'wide_0','wide_1','wi..., dimensions={0} | all-to-all | bytes 589824 | tf_op jit(solution)/shard_map/all_to_all | solution.py:21
  69.0 0.1 reduce_step.5
  69.0 8.6 %all_to_all.40.got = f32[8,40,128]{2,1,0:T(8,128)S(1)} all-to-all(f32[8,40,128]{2,1,0:T(8,128)S(1)} %reduce_step.5), channel_id=1, replica_groups=mesh['wide_0'=4,'wide_1'=4,'wide_2'=2,'narrow'=4] {'wide_2','narrow'}, dimensions={0} | all-to-all | bytes 327680 | tf_op jit(solution)/shard_map/all_to_all | solution.py:21
  77.6 3.1 %close_step.1 = (f32[128,4096]{1,0:T(8,128)}, f32[32,32,128]{2,1,0:T(8,128)}, f32[1,128]{1,0:T(1,128)S(1)}, f32[8,128]{1,0:T(8,128)S(1)}, f32[1,128]{1,0:T(1,128)S(1)}, /*index=5*/f32[32,128]{1,0:T(8,128)S(1)}) custom-call(f32[8,40,128]{2,1,0:T(8,128)S(1)} %all_to_all.40.got, f32[8,128]{1,0:T(8,128)S(1)} %get-tuple-element.43.weight, ...), custom_call_target="tpu_custom_call" | custom-call | tf_op jit(solution)/shard_map/close_step/pallas_call | solution.py:302
  80.7 3.8 %all-to-all-start.6 = ((f32[32,32,128]{2,1,0:T(8,128)}), f32[32,32,128]{2,1,0:T(8,128)S(1)}, u32[]{:S(2)}, u32[]{:S(2)}) async-start(f32[32,32,128]{2,1,0:T(8,128)} %get-tuple-element.48), calls=%async_computation.6 | async-start | bytes 1048576 | tf_op jit(solution)/shard_map/all_to_all | solution.py:21
  84.5 7.4 %all-gather.1.row_got = f32[4,1,128]{2,1,0:T(1,128)S(1)} all-gather(f32[1,1,128]{2,1,0:T(1,128)S(1)} %bitcast.7), channel_id=2, replica_groups=mesh['wide_0'=4,'wide_1'=4,'wide_2'=2,'narrow'=4] {'narrow'}, dimensions={0}, use_global_device_ids=true | all-gather | bytes 2560 | tf_op jit(solution)/shard_map/all_gather | solution.py:312
  92.0 4.3 %all-to-all-done.6.got = f32[32,32,128]{2,1,0:T(8,128)S(1)} async-done(((f32[32,32,128]{2,1,0:T(8,128)}), f32[32,32,128]{2,1,0:T(8,128)S(1)}, u32[]{:S(2)}, u32[]{:S(2)}) %all-to-all-start.6) | async-done | bytes 524320 | tf_op jit(solution)/shard_map/all_to_all | solution.py:21
  96.2 0.7 finish_step.1
Async XLA Ops:
  80.7 15.5 %all-to-all-start.6 = ((f32[32,32,128]{2,1,0:T(8,128)}), f32[32,32,128]{2,1,0:T(8,128)S(1)}, u32[]{:S(2)}, u32[]{:S(2)}) async-start(f32[32,32,128]{2,1,0:T(8,128)} %get-tuple-element.48), calls=%async_computation.6 | async-start | bytes 1048576 | tf_op jit(solution)/shard_map/all_to_all | solution.py:21

commit v3 on v2

v3 whole, which is shorter than its diff:
```python
import functools
import math

import jax
import jax.numpy as jnp
from jax import lax
from jax.experimental import pallas as pl
from jax.experimental.pallas import tpu as pltpu
from jax.sharding import Mesh
from jax.sharding import PartitionSpec as P

ITERS = 4
LANES = 128
GROUP = 8
CHUNKS = 4
CORE = "wide_2"
WIDE = ("wide_0", "wide_1", "wide_2")
CHIPS = ("wide_0", "wide_1", "narrow")


def exchange(array, axes):
    return lax.all_to_all(array, axes, split_axis=0, concat_axis=0, tiled=True)


def swap(array):
    return lax.ppermute(array, CORE, [(0, 1), (1, 0)])


def total(block):
    return jnp.sum(jnp.sum(block, axis=0, keepdims=True), axis=1, keepdims=True)


def down(block):
    return jnp.sum(block, axis=0, keepdims=True)


def span(start, size):
    return pl.ds(pl.multiple_of(start * LANES, LANES), size * LANES)


def tile_of(n, size=1):
    return slice(n * LANES, (n + size) * LANES)


def dual_update(mine, theirs, own_row, weight, row_dual, col_dual, new_weight, new_row, new_col, sizes):
    base, half = sizes[1], sizes[2]
    core = lax.axis_index(CORE)
    left_square = total(mine[:, tile_of(half)]) + total(theirs[:, tile_of(half)])
    moved = total(mine[:, tile_of(half + 1)]) + total(theirs[:, tile_of(half + 1)])
    old = weight[...]
    dual_step = base * old
    dual_moved = dual_step * dual_step * left_square
    fresh_weight = jnp.sqrt(old * jnp.sqrt((dual_moved + 1.0) / (moved + 1.0)))
    new_weight[...] = fresh_weight
    new_row[...] = row_dual[...] + dual_step[0:1, :] * own_row[...]
    scale = jnp.broadcast_to(dual_step[0:1, 0:1], (1, half * LANES))
    for side, part in ((core, mine), (1 - core, theirs)):
        lanes = span(side * half, half)
        new_col[:, lanes] = col_dual[:, lanes] + scale * part[:, tile_of(0, half)]
    return base / fresh_weight


def sweep(step, cost, plan, fresh_plan, row_all, col_dual, tiles, state, done):
    first, count = tiles
    groups = len(state[0])

    def tile(n, state):
        rows, moved = list(state[0]), state[1]
        j = first + n
        lanes = span(j, 1)
        col = jnp.broadcast_to(col_dual[:, lanes], (GROUP, LANES))
        cols = None
        for g in range(groups):
            part = slice(g * GROUP, (g + 1) * GROUP)
            old = plan[part, lanes]
            gap = cost[part, lanes] - row_all[part, :] - col
            fresh = jnp.maximum(old - step * gap, 0.0)
            change = fresh - old
            extrap = fresh + change
            fresh_plan[part, lanes] = fresh
            rows[g] = rows[g] + extrap
            cols = extrap if cols is None else cols + extrap
            moved = moved + change * change
        done(n, j, down(cols))
        return tuple(rows), moved

    return lax.fori_loop(0, count, tile, state, unroll=2)


def spread_rows(row_dual, row_all):
    row_all[...] = jnp.transpose(jnp.broadcast_to(row_dual, (LANES, LANES)))


def gather_rows(rows):
    return down(jnp.transpose(jnp.concatenate(rows, axis=0)))


def zeros(row_all):
    zero = jnp.zeros((GROUP, LANES), jnp.float32)
    return tuple(zero for _ in range(row_all.shape[0] // GROUP)), zero


def into(target, col_mass, wide):
    def done(n, j, cols):
        target[:, span(n, 1)] = col_mass[:, span(j, 1)] * (1.0 / wide) - cols

    return done


def tail(keep, row_mass, state, sizes):
    narrow, _, half, _ = sizes
    keep[:, tile_of(half)] = row_mass[...] * (1.0 / narrow) - gather_rows(state[0])
    keep[:, tile_of(half + 1)] = down(state[1])


def open_kernel(sizes, *refs):
    narrow, base, half, chips = sizes
    sources, targets, (give, keep, weight, row_all, sems) = refs[:6], refs[6:12], refs[12:]
    cost, plan, row_mass, col_mass, row_dual, col_dual = targets
    core = lax.axis_index(CORE)
    tiles = 2 * half // CHUNKS
    weight[...] = jnp.full((GROUP, LANES), base, jnp.float32)
    small = [pltpu.make_async_copy(sources[n], targets[n], sems.at[n, 0]) for n in range(2, 6)]
    for copy in small:
        copy.start()
    firsts, copies = [], []
    for k in range(CHUNKS):
        side = 1 - core if k < CHUNKS // 2 else core
        firsts.append(side * half + (k % (CHUNKS // 2)) * tiles)
        lanes = span(firsts[k], tiles)
        for n in range(2):
            copy = pltpu.make_async_copy(
                sources[n].at[:, lanes], targets[n].at[:, lanes], sems.at[n, k]
            )
            copy.start()
            copies.append(copy)
    for copy in small:
        copy.wait()
    spread_rows(row_dual[...], row_all)
    state = zeros(row_all)
    for k in range(CHUNKS):
        copies[2 * k].wait()
        copies[2 * k + 1].wait()
        target = give if k < CHUNKS // 2 else keep
        shift = (k % (CHUNKS // 2)) * tiles
        put = into(target, col_mass, 2 * chips)
        state = sweep(
            jnp.float32(1.0), cost, plan, plan, row_all, col_dual, (firsts[k], tiles), state,
            lambda n, j, cols, put=put, shift=shift: put(n + shift, j, cols),
        )
    tail(keep, row_mass, state, sizes)


def middle_kernel(
    sizes, mine, theirs, own_row, weight, cost, plan, row_mass, col_mass, row_dual, col_dual,
    fresh_plan, give, keep, new_weight, new_row, new_col, row_all,
):
    narrow, base, half, chips = sizes
    core = lax.axis_index(CORE)
    step = dual_update(
        mine, theirs, own_row, weight, row_dual, col_dual, new_weight, new_row, new_col, sizes
    )
    spread_rows(new_row[...], row_all)
    state = zeros(row_all)
    for side, target in ((1 - core, give), (core, keep)):
        state = sweep(
            step, cost, plan, fresh_plan, row_all, new_col, (side * half, half), state,
            into(target, col_mass, 2 * chips),
        )
    tail(keep, row_mass, state, sizes)


def close_kernel(
    sizes, mine, theirs, own_row, weight, cost, plan, row_mass, col_mass, row_dual, col_dual,
    plan_out, sent, row_sent, new_weight, new_row, new_col, row_all, fresh_plan, sems,
):
    narrow, base, half, chips = sizes
    step = dual_update(
        mine, theirs, own_row, weight, row_dual, col_dual, new_weight, new_row, new_col, sizes
    )
    spread_rows(new_row[...], row_all)
    state = zeros(row_all)

    def done(n, j, cols):
        share = col_mass[:, span(j, 1)] * (1.0 / (2 * chips)) - cols
        for p in range(2 * chips):
            sent[p, pl.ds(j, 1), :] = share

    tiles = 2 * half // CHUNKS
    copies = []
    for k in range(CHUNKS):
        state = sweep(
            step, cost, plan, fresh_plan, row_all, new_col, (k * tiles, tiles), state, done
        )
        lanes = tile_of(k * tiles, tiles)
        copy = pltpu.make_async_copy(fresh_plan.at[:, lanes], plan_out.at[:, lanes], sems.at[k])
        copy.start()
        copies.append(copy)
    row_sent[...] = row_mass[...] * (1.0 / narrow) - gather_rows(state[0])
    for copy in copies:
        copy.wait()


def build_kernel(sizes, keep, came, sent):
    half = sizes[2]
    cols = keep[:, tile_of(0, half)] + came[...]
    rest = keep[:, tile_of(half, 2)]
    for p in range(sent.shape[0]):
        sent[p, :, tile_of(0, half)] = cols
        sent[p, :, tile_of(half, 2)] = rest


def reduce_kernel(sizes, got, mine, own_row, held, rows_held):
    narrow, base, half, chips = sizes
    column = lax.axis_index("narrow")
    place = lax.axis_index("wide_0") * lax.axis_size("wide_1") + lax.axis_index("wide_1")
    col_squares = jnp.zeros((1, half * LANES), jnp.float32)
    moved = jnp.zeros((1, LANES), jnp.float32)
    for n in range(narrow):
        cols = got[n]
        for p in range(1, chips):
            cols = cols + got[p * narrow + n]
        moved = moved + cols[:, tile_of(half + 1)]
        cols = cols[:, tile_of(0, half)]
        held[n] = cols
        col_squares = col_squares + cols * cols
    squares = jnp.zeros((1, LANES), jnp.float32)
    for r in range(half):
        squares = squares + col_squares[:, tile_of(r)]
    for p in range(chips):
        row = got[p * narrow, :, tile_of(half)]
        for n in range(1, narrow):
            row = row + got[p * narrow + n, :, tile_of(half)]
        rows_held[p] = row
        squares = squares + row * row
    mine[:, tile_of(0, half)] = held[column]
    mine[:, tile_of(half)] = squares
    mine[:, tile_of(half + 1)] = moved
    own_row[...] = rows_held[place]


def finish_kernel(sizes, got, row_got, weight, row_dual, col_dual, row_out, col_out):
    narrow, base, half, chips = sizes
    step = base * weight[0:1, :]
    rows = row_got[0]
    for n in range(1, narrow):
        rows = rows + row_got[n]
    row_out[...] = row_dual[...] + step * rows
    cols = got[0]
    for p in range(1, 2 * chips):
        cols = cols + got[p]
    for j in range(2 * half):
        col_out[:, tile_of(j)] = col_dual[:, tile_of(j)] + step * cols[j : j + 1, :]


VM = pl.BlockSpec(memory_space=pltpu.VMEM)
HB = pl.BlockSpec(memory_space=pltpu.HBM)
ROOM = pltpu.CompilerParams(vmem_limit_bytes=16 << 20)


def shards(cost, plan, row_mass, col_mass, row_dual, col_dual):
    rows, cols = plan.shape
    tiles = cols // LANES
    half = tiles // 2
    narrow = lax.axis_size("narrow")
    wide = lax.axis_size(WIDE)
    chips = wide // 2
    base = 0.9 / math.sqrt(rows * wide + cols * narrow)
    sizes = (narrow, base, half, chips)
    row_mass, row_dual = row_mass.reshape(1, rows), row_dual.reshape(1, rows)
    col_mass, col_dual = col_mass.reshape(1, cols), col_dual.reshape(1, cols)

    def vm(*shape):
        return pltpu.VMEM(shape, jnp.float32)

    def near(*arrays):
        return [pltpu.with_memory_space_constraint(array, pltpu.VMEM) for array in arrays]

    big, state, one, many = vm(rows, cols), vm(GROUP, LANES), vm(1, rows), vm(1, cols)
    give, keep = vm(1, half * LANES), vm(1, (half + 2) * LANES)
    spread = vm(rows, LANES)

    inputs = (cost, plan, row_mass, col_mass, row_dual, col_dual)
    *held, given, kept, weight = pl.pallas_call(
        functools.partial(open_kernel, sizes),
        out_shape=(big, big, one, many, one, many, give, keep, state),
        in_specs=[HB] * 6,
        out_specs=(VM,) * 9,
        scratch_shapes=[spread, pltpu.SemaphoreType.DMA((6, CHUNKS))],
        compiler_params=ROOM,
        name="open_step",
    )(*(pltpu.with_memory_space_constraint(array, pltpu.HBM) for array in inputs))
    cost, plan, row_mass, col_mass, row_dual, col_dual = held
    for step in range(1, ITERS):
        came = swap(given)
        sent = pl.pallas_call(
            functools.partial(build_kernel, sizes),
            out_shape=vm(chips * narrow, 1, (half + 2) * LANES),
            in_specs=[VM] * 2,
            out_specs=VM,
            compiler_params=ROOM,
            name="build_step",
        )(*near(kept, came))
        got = exchange(sent, CHIPS)
        mine, own_row = pl.pallas_call(
            functools.partial(reduce_kernel, sizes),
            out_shape=(keep, one),
            in_specs=[VM],
            out_specs=(VM, VM),
            scratch_shapes=[vm(narrow, 1, half * LANES), vm(chips, 1, rows)],
            compiler_params=ROOM,
            name="reduce_step",
        )(*near(got))
        theirs = swap(mine)
        operands = near(
            mine, theirs, own_row, weight, cost, plan, row_mass, col_mass, row_dual, col_dual
        )
        if step < ITERS - 1:
            plan, given, kept, weight, row_dual, col_dual = pl.pallas_call(
                functools.partial(middle_kernel, sizes),
                out_shape=(big, give, keep, state, one, many),
                in_specs=[VM] * 10,
                out_specs=(VM,) * 6,
                scratch_shapes=[spread],
                compiler_params=ROOM,
                name="middle_step",
            )(*operands)
        else:
            plan, sent, row_sent, weight, row_dual, col_dual = pl.pallas_call(
                functools.partial(close_kernel, sizes),
                out_shape=(
                    jax.ShapeDtypeStruct((rows, cols), jnp.float32),
                    vm(wide, tiles, LANES), one, state, one, many,
                ),
                in_specs=[VM] * 10,
                out_specs=(HB,) + (VM,) * 5,
                scratch_shapes=[spread, big, pltpu.SemaphoreType.DMA((CHUNKS,))],
                compiler_params=ROOM,
                name="close_step",
            )(*operands)
    got = exchange(sent, WIDE)
    row_got = lax.all_gather(row_sent, "narrow")
    row_dual, col_dual = pl.pallas_call(
        functools.partial(finish_kernel, sizes),
        out_shape=tuple(jax.ShapeDtypeStruct(s.shape, s.dtype) for s in (one, many)),
        in_specs=[VM] * 5,
        out_specs=(VM, VM),
        compiler_params=ROOM,
        name="finish_step",
    )(*near(got), row_got, weight, row_dual, col_dual)
    return (plan, row_dual.reshape(rows), col_dual.reshape(cols))


def solution(mesh):
    split = Mesh(
        mesh.devices.reshape(4, 4, 2, mesh.shape["narrow"]),
        ("wide_0", "wide_1", "wide_2", "narrow"),
    )
    placed = (P(WIDE, "narrow"), P(WIDE, "narrow"), P(WIDE), P("narrow"), P(WIDE), P("narrow"))
    return jax.shard_map(
        shards,
        mesh=split,
        in_specs=placed,
        out_specs=(P(WIDE, "narrow"), P(WIDE), P("narrow")),
        check_vma=False,
    )
```

time: 97.3 us -> 97.9 us (level)
  blocking collectives: 78.7 us -> 64.2 us
  starting transfers between devices: 3.81 us -> 12.8 us
  waiting for transfers between devices: 4.28 us -> 10.2 us
    all_to_all x6 -> x3, blocking collectives: 71.3 us -> 57.7 us  [exchange(): return lax.all_to_all(array, axes, split_axis=0, concat_axis=0, tiled=True)]
    ppermute x0 -> x6, starting transfers between devices: none -> 8.91 us  [swap(): return lax.ppermute(array, CORE, [(0, 1), (1, 0)])]
    ppermute x0 -> x6, waiting for transfers between devices: none -> 4.98 us  [swap(): return lax.ppermute(array, CORE, [(0, 1), (1, 0)])]
    all_gather x1, blocking collectives: 7.43 us -> 6.43 us  [shards(): row_got = lax.all_gather(row_sent, 'narrow')]
    all_to_all x1, waiting for transfers between devices: 4.28 us -> 5.27 us  [exchange(): return lax.all_to_all(array, axes, split_axis=0, concat_axis=0, tiled=True)]
    pallas_call x6 -> x9, Pallas kernels: 5.72 us -> 5.92 us  [the longest x2 2.77 us: shards(): pl.pallas_call(functools.partial(middle_kernel, sizes), out_shape=(big, g...]
  transfers between devices with their start and end apart: 1 -> 7, of which waited for: 1 -> 7; matrix products, arithmetic and copies ran while one was open for 0% -> 0% of each run, Pallas kernels for 0% -> 0%
where the time goes in v3:
time: 97.9 us; the launch traced here: 97.6 us
  blocking collectives  64.2 us (66%)
  starting transfers between devices  12.8 us (13%)
  waiting for transfers between devices  10.2 us (10%)
  Pallas kernels  9.69 us (10%)
    all_to_all x3, blocking collectives, exchange(): return lax.all_to_all(array, axes, split_axis=0, concat_axis=0, tiled=True)  57.7 us
    ppermute x6, starting transfers between devices, swap(): return lax.ppermute(array, CORE, [(0, 1), (1, 0)])  8.91 us
    all_gather x1, blocking collectives, shards(): row_got = lax.all_gather(row_sent, 'narrow')  6.43 us
    all_to_all x1, waiting for transfers between devices, exchange(): return lax.all_to_all(array, axes, split_axis=0, concat_axis=0, tiled=True)  5.27 us
    ppermute x6, waiting for transfers between devices, swap(): return lax.ppermute(array, CORE, [(0, 1), (1, 0)])  4.98 us
    all_to_all x1, starting transfers between devices, exchange(): return lax.all_to_all(array, axes, split_axis=0, concat_axis=0, tiled=True)  3.9 us
    pallas_call x1, Pallas kernels, shards(): pl.pallas_call(functools.partial(close_kernel, sizes), out_shape=(jax.Sha...  3.09 us
    pallas_call x2, Pallas kernels, shards(): pl.pallas_call(functools.partial(middle_kernel, sizes), out_shape=(big, g...  2.77 us
  transfers between devices with their start and end apart: 7, of which 7 were waited for; matrix products, arithmetic and copies ran while one was open for 0% of the time, Pallas kernels for 0%

profile of v3, /device:TPU:1, one launch (start us, length us, event | category | flops | bytes accessed | tf_op | source)
XLA Modules:
  0.0 97.6 jit_solution(4376600695216169163)
XLA Ops:
  0.6 2.8 %open_step.1 = (f32[128,4096]{1,0:T(8,128)S(1)}, f32[128,4096]{1,0:T(8,128)S(1)}, f32[1,128]{1,0:T(1,128)S(1)}, f32[1,4096]{1,0:T(1,128)S(1)}, f32[1,128]{1,0:T(...) custom-call(f32[128,4096]{1,0:T(8,128)} %refs_0_.1, ...), custom_call_target="tpu_custom_call" | custom-call | tf_op jit(solution)/shard_map/open_step/pallas_call | solution.py:284
  3.4 1.5 %collective-permute-start = (f32[1,2048]{1,0:T(1,128)S(1)}, f32[1,2048]{1,0:T(1,128)S(1)}, u32[]{:S(2)}, u32[]{:S(2)}) collective-permute-start(f32[1,2048]{1,0:T(1,128)S(1)} %get-tuple-element.39), channel_id=1, source_target_pairs={{0,4},{4,0},{1,5},{5,1},{2,6},{6,2},{3,7},{7,3},{8,12},{12,8},{9,1... | collective-permute-start | bytes 24584 | tf_op jit(solution)/shard_map/ppermute | solution.py:26
  4.9 0.8 collective-permute-done.came
  5.7 0.1 build_step.3
  5.8 23.7 %all_to_all.20.got = f32[64,1,2304]{2,1,0:T(1,128)S(1)} all-to-all(f32[64,1,2304]{2,1,0:T(1,128)S(1)} %build_step.3), channel_id=1, replica_groups=mesh['wide_0'=4,'wide_1'=4,'wide_2'=2,'narrow'=4] {'wide_0','wide_1','na..., dimensions={0} | all-to-all | bytes 1179648 | tf_op jit(solution)/shard_map/all_to_all | solution.py:22
  29.5 0.1 reduce_step.3
  29.6 2.2 %collective-permute-start.1 = (f32[1,2304]{1,0:T(1,128)S(1)}, f32[1,2304]{1,0:T(1,128)S(1)}, u32[]{:S(2)}, u32[]{:S(2)}) collective-permute-start(f32[1,2304]{1,0:T(1,128)S(1)} %get-tuple-element.40.mine), channel_id=1, source_target_pairs={{0,4},{4,0},{1,5},{5,1},{2,6},{6,2},{3,7},{7,3},{8,12},{12,8},{9,1... | collective-permute-start | bytes 27656 | tf_op jit(solution)/shard_map/ppermute | solution.py:26
  31.8 0.8 collective-permute-done.1.theirs
  32.6 1.4 %middle_step.2 = (f32[128,4096]{1,0:T(8,128)S(1)}, f32[1,2048]{1,0:T(1,128)S(1)}, f32[1,2304]{1,0:T(1,128)S(1)}, f32[8,128]{1,0:T(8,128)S(1)}, f32[1,128]{1,0:T(1,128)S(1)}, /*index=5*/f32[1,4096]{1,0:T(1,128)S(1)}) custom-call(f32[1,2304]{1,0:T(1,128)S(1)} %get-tuple-element.40.mine, f32[1,2304]{1,0:T(1,128)S(1)} %collective-permute-done.1.theirs, ...), custom_call_target="tpu_custom_call" | custom-call | tf_op jit(solution)/shard_map/middle_step/pallas_call | solution.py:319
  34.0 0.4 collective-permute-start.2
  34.4 0.8 collective-permute-done.2.came
  35.2 0.1 build_step.4
  35.3 17.0 %all_to_all.21.got = f32[64,1,2304]{2,1,0:T(1,128)S(1)} all-to-all(f32[64,1,2304]{2,1,0:T(1,128)S(1)} %build_step.4), channel_id=1, replica_groups=mesh['wide_0'=4,'wide_1'=4,'wide_2'=2,'narrow'=4] {'wide_0','wide_1','na..., dimensions={0} | all-to-all | bytes 1179648 | tf_op jit(solution)/shard_map/all_to_all | solution.py:22
  52.3 0.1 reduce_step.4
  52.4 2.2 %collective-permute-start.3 = (f32[1,2304]{1,0:T(1,128)S(1)}, f32[1,2304]{1,0:T(1,128)S(1)}, u32[]{:S(2)}, u32[]{:S(2)}) collective-permute-start(f32[1,2304]{1,0:T(1,128)S(1)} %get-tuple-element.51.mine), channel_id=1, source_target_pairs={{0,4},{4,0},{1,5},{5,1},{2,6},{6,2},{3,7},{7,3},{8,12},{12,8},{9,1... | collective-permute-start | bytes 27656 | tf_op jit(solution)/shard_map/ppermute | solution.py:26
  54.6 0.8 collective-permute-done.3.theirs
  55.4 1.4 %middle_step.3 = (f32[128,4096]{1,0:T(8,128)S(1)}, f32[1,2048]{1,0:T(1,128)S(1)}, f32[1,2304]{1,0:T(1,128)S(1)}, f32[8,128]{1,0:T(8,128)S(1)}, f32[1,128]{1,0:T(1,128)S(1)}, /*index=5*/f32[1,4096]{1,0:T(1,128)S(1)}) custom-call(f32[1,2304]{1,0:T(1,128)S(1)} %get-tuple-element.51.mine, f32[1,2304]{1,0:T(1,128)S(1)} %collective-permute-done.3.theirs, ...), custom_call_target="tpu_custom_call" | custom-call | tf_op jit(solution)/shard_map/middle_step/pallas_call | solution.py:319
  56.8 0.4 collective-permute-start.4
  57.2 0.8 collective-permute-done.4.came
  58.0 0.1 build_step.5
  58.1 17.0 %all_to_all.22.got = f32[64,1,2304]{2,1,0:T(1,128)S(1)} all-to-all(f32[64,1,2304]{2,1,0:T(1,128)S(1)} %build_step.5), channel_id=1, replica_groups=mesh['wide_0'=4,'wide_1'=4,'wide_2'=2,'narrow'=4] {'wide_0','wide_1','na..., dimensions={0} | all-to-all | bytes 1179648 | tf_op jit(solution)/shard_map/all_to_all | solution.py:22
  75.1 0.1 reduce_step.5
  75.2 2.2 %collective-permute-start.5 = (f32[1,2304]{1,0:T(1,128)S(1)}, f32[1,2304]{1,0:T(1,128)S(1)}, u32[]{:S(2)}, u32[]{:S(2)}) collective-permute-start(f32[1,2304]{1,0:T(1,128)S(1)} %get-tuple-element.59.mine), channel_id=1, source_target_pairs={{0,4},{4,0},{1,5},{5,1},{2,6},{6,2},{3,7},{7,3},{8,12},{12,8},{9,1... | collective-permute-start | bytes 27656 | tf_op jit(solution)/shard_map/ppermute | solution.py:26
  77.4 0.8 collective-permute-done.5.theirs
  78.2 3.1 %close_step.1 = (f32[128,4096]{1,0:T(8,128)}, f32[32,32,128]{2,1,0:T(8,128)}, f32[1,128]{1,0:T(1,128)S(1)}, f32[8,128]{1,0:T(8,128)S(1)}, f32[1,128]{1,0:T(1,128)S(1)}, /*index=5*/f32[1,4096]{1,0:T(1,128)S(1)}) custom-call(f32[1,2304]{1,0:T(1,128)S(1)} %get-tuple-element.59.mine, f32[1,2304]{1,0:T(1,128)S(1)} %collective-permute-done.5.theirs, ...), custom_call_target="tpu_custom_call" | custom-call | tf_op jit(solution)/shard_map/close_step/pallas_call | solution.py:329
  81.3 3.9 %all-to-all-start.3 = ((f32[32,32,128]{2,1,0:T(8,128)}), f32[32,32,128]{2,1,0:T(8,128)S(1)}, u32[]{:S(2)}, u32[]{:S(2)}) async-start(f32[32,32,128]{2,1,0:T(8,128)} %get-tuple-element.66), calls=%async_computation.3 | async-start | bytes 1048576 | tf_op jit(solution)/shard_map/all_to_all | solution.py:22
  85.2 6.4 %all-gather.1.row_got = f32[4,1,128]{2,1,0:T(1,128)S(1)} all-gather(f32[1,1,128]{2,1,0:T(1,128)S(1)} %bitcast.7), channel_id=2, replica_groups=mesh['wide_0'=4,'wide_1'=4,'wide_2'=2,'narrow'=4] {'narrow'}, dimensions={0}, use_global_device_ids=true | all-gather | bytes 2560 | tf_op jit(solution)/shard_map/all_gather | solution.py:342
  91.6 5.3 %all-to-all-done.3.got = f32[32,32,128]{2,1,0:T(8,128)S(1)} async-done(((f32[32,32,128]{2,1,0:T(8,128)}), f32[32,32,128]{2,1,0:T(8,128)S(1)}, u32[]{:S(2)}, u32[]{:S(2)}) %all-to-all-start.3) | async-done | bytes 524320 | tf_op jit(solution)/shard_map/all_to_all | solution.py:22
  96.9 0.7 finish_step.1
Async XLA Ops:
  3.4 2.3 %collective-permute-start = (f32[1,2048]{1,0:T(1,128)S(1)}, f32[1,2048]{1,0:T(1,128)S(1)}, u32[]{:S(2)}, u32[]{:S(2)}) collective-permute-start(f32[1,2048]{1,0:T(1,128)S(1)} %get-tuple-element.39), channel_id=1, source_target_pairs={{0,4},{4,0},{1,5},{5,1},{2,6},{6,2},{3,7},{7,3},{8,12},{12,8},{9,1... | collective-permute-start | bytes 24584 | tf_op jit(solution)/shard_map/ppermute | solution.py:26
  29.6 3.0 %collective-permute-start.1 = (f32[1,2304]{1,0:T(1,128)S(1)}, f32[1,2304]{1,0:T(1,128)S(1)}, u32[]{:S(2)}, u32[]{:S(2)}) collective-permute-start(f32[1,2304]{1,0:T(1,128)S(1)} %get-tuple-element.40.mine), channel_id=1, source_target_pairs={{0,4},{4,0},{1,5},{5,1},{2,6},{6,2},{3,7},{7,3},{8,12},{12,8},{9,1... | collective-permute-start | bytes 27656 | tf_op jit(solution)/shard_map/ppermute | solution.py:26
  34.0 1.3 %collective-permute-start.2 = (f32[1,2048]{1,0:T(1,128)S(1)}, f32[1,2048]{1,0:T(1,128)S(1)}, u32[]{:S(2)}, u32[]{:S(2)}) collective-permute-start(f32[1,2048]{1,0:T(1,128)S(1)} %get-tuple-element.50), channel_id=1, source_target_pairs={{0,4},{4,0},{1,5},{5,1},{2,6},{6,2},{3,7},{7,3},{8,12},{12,8},{9,1... | collective-permute-start | bytes 24584 | tf_op jit(solution)/shard_map/ppermute | solution.py:26
  52.4 3.0 %collective-permute-start.3 = (f32[1,2304]{1,0:T(1,128)S(1)}, f32[1,2304]{1,0:T(1,128)S(1)}, u32[]{:S(2)}, u32[]{:S(2)}) collective-permute-start(f32[1,2304]{1,0:T(1,128)S(1)} %get-tuple-element.51.mine), channel_id=1, source_target_pairs={{0,4},{4,0},{1,5},{5,1},{2,6},{6,2},{3,7},{7,3},{8,12},{12,8},{9,1... | collective-permute-start | bytes 27656 | tf_op jit(solution)/shard_map/ppermute | solution.py:26
  56.8 1.3 %collective-permute-start.4 = (f32[1,2048]{1,0:T(1,128)S(1)}, f32[1,2048]{1,0:T(1,128)S(1)}, u32[]{:S(2)}, u32[]{:S(2)}) collective-permute-start(f32[1,2048]{1,0:T(1,128)S(1)} %get-tuple-element.58), channel_id=1, source_target_pairs={{0,4},{4,0},{1,5},{5,1},{2,6},{6,2},{3,7},{7,3},{8,12},{12,8},{9,1... | collective-permute-start | bytes 24584 | tf_op jit(solution)/shard_map/ppermute | solution.py:26
  75.2 3.0 %collective-permute-start.5 = (f32[1,2304]{1,0:T(1,128)S(1)}, f32[1,2304]{1,0:T(1,128)S(1)}, u32[]{:S(2)}, u32[]{:S(2)}) collective-permute-start(f32[1,2304]{1,0:T(1,128)S(1)} %get-tuple-element.59.mine), channel_id=1, source_target_pairs={{0,4},{4,0},{1,5},{5,1},{2,6},{6,2},{3,7},{7,3},{8,12},{12,8},{9,1... | collective-permute-start | bytes 27656 | tf_op jit(solution)/shard_map/ppermute | solution.py:26
  81.3 15.6 %all-to-all-start.3 = ((f32[32,32,128]{2,1,0:T(8,128)}), f32[32,32,128]{2,1,0:T(8,128)S(1)}, u32[]{:S(2)}, u32[]{:S(2)}) async-start(f32[32,32,128]{2,1,0:T(8,128)} %get-tuple-element.66), calls=%async_computation.3 | async-start | bytes 1048576 | tf_op jit(solution)/shard_map/all_to_all | solution.py:22

commit v4 on v3

--- a/solution.py
+++ b/solution.py
@@ -15,7 +15,8 @@
 CHUNKS = 4
 CORE = "wide_2"
 WIDE = ("wide_0", "wide_1", "wide_2")
-CHIPS = ("wide_0", "wide_1", "narrow")
+CHIPS = ("wide_1", "narrow", "wide_0")
+PLANE = ("wide_1", "wide_0")
 
 
 def exchange(array, axes):
@@ -151,54 +152,39 @@
     tail(keep, row_mass, state, sizes)
 
 
-def middle_kernel(
-    sizes, mine, theirs, own_row, weight, cost, plan, row_mass, col_mass, row_dual, col_dual,
-    fresh_plan, give, keep, new_weight, new_row, new_col, row_all,
+def give_kernel(
+    sizes, mine, theirs, own_row, weight, cost, plan, col_mass, row_dual, col_dual,
+    fresh_plan, give, row_sums, moved_sums, row_all, new_weight, new_row, new_col,
 ):
-    narrow, base, half, chips = sizes
-    core = lax.axis_index(CORE)
+    _, _, half, chips = sizes
     step = dual_update(
         mine, theirs, own_row, weight, row_dual, col_dual, new_weight, new_row, new_col, sizes
     )
     spread_rows(new_row[...], row_all)
-    state = zeros(row_all)
-    for side, target in ((1 - core, give), (core, keep)):
-        state = sweep(
-            step, cost, plan, fresh_plan, row_all, new_col, (side * half, half), state,
-            into(target, col_mass, 2 * chips),
-        )
+    side = 1 - lax.axis_index(CORE)
+    rows, moved = sweep(
+        step, cost, plan, fresh_plan, row_all, new_col, (side * half, half), zeros(row_all),
+        into(give, col_mass, 2 * chips),
+    )
+    row_sums[...] = jnp.concatenate(rows, axis=0)
+    moved_sums[...] = moved
+
+
+def keep_kernel(
+    sizes, weight, cost, plan, row_mass, col_mass, row_all, col_dual, row_sums, moved_sums,
+    fresh_plan, keep, row_share,
+):
+    _, base, half, chips = sizes
+    side = lax.axis_index(CORE)
+    rows = row_sums[...]
+    groups = row_all.shape[0] // GROUP
+    state = tuple(rows[g * GROUP : (g + 1) * GROUP] for g in range(groups)), moved_sums[...]
+    state = sweep(
+        base / weight[...], cost, plan, fresh_plan, row_all, col_dual, (side * half, half), state,
+        into(keep, col_mass, 2 * chips),
+    )
     tail(keep, row_mass, state, sizes)
-
-
-def close_kernel(
-    sizes, mine, theirs, own_row, weight, cost, plan, row_mass, col_mass, row_dual, col_dual,
-    plan_out, sent, row_sent, new_weight, new_row, new_col, row_all, fresh_plan, sems,
-):
-    narrow, base, half, chips = sizes
-    step = dual_update(
-        mine, theirs, own_row, weight, row_dual, col_dual, new_weight, new_row, new_col, sizes
-    )
-    spread_rows(new_row[...], row_all)
-    state = zeros(row_all)
-
-    def done(n, j, cols):
-        share = col_mass[:, span(j, 1)] * (1.0 / (2 * chips)) - cols
-        for p in range(2 * chips):
-            sent[p, pl.ds(j, 1), :] = share
-
-    tiles = 2 * half // CHUNKS
-    copies = []
-    for k in range(CHUNKS):
-        state = sweep(
-            step, cost, plan, fresh_plan, row_all, new_col, (k * tiles, tiles), state, done
-        )
-        lanes = tile_of(k * tiles, tiles)
-        copy = pltpu.make_async_copy(fresh_plan.at[:, lanes], plan_out.at[:, lanes], sems.at[k])
-        copy.start()
-        copies.append(copy)
-    row_sent[...] = row_mass[...] * (1.0 / narrow) - gather_rows(state[0])
-    for copy in copies:
-        copy.wait()
+    row_share[...] = keep[:, tile_of(half)]
 
 
 def build_kernel(sizes, keep, came, sent):
@@ -213,13 +199,18 @@
 def reduce_kernel(sizes, got, mine, own_row, held, rows_held):
     narrow, base, half, chips = sizes
     column = lax.axis_index("narrow")
-    place = lax.axis_index("wide_0") * lax.axis_size("wide_1") + lax.axis_index("wide_1")
+    across, along = lax.axis_index("wide_0"), lax.axis_index("wide_1")
+    wide_0 = lax.axis_size("wide_0")
+    peers = [
+        [(b * narrow + n) * wide_0 + a for b in range(chips // wide_0) for a in range(wide_0)]
+        for n in range(narrow)
+    ]
     col_squares = jnp.zeros((1, half * LANES), jnp.float32)
     moved = jnp.zeros((1, LANES), jnp.float32)
     for n in range(narrow):
-        cols = got[n]
-        for p in range(1, chips):
-            cols = cols + got[p * narrow + n]
+        cols = got[peers[n][0]]
+        for p in peers[n][1:]:
+            cols = cols + got[p]
         moved = moved + cols[:, tile_of(half + 1)]
         cols = cols[:, tile_of(0, half)]
         held[n] = cols
@@ -228,29 +219,50 @@
     for r in range(half):
         squares = squares + col_squares[:, tile_of(r)]
     for p in range(chips):
-        row = got[p * narrow, :, tile_of(half)]
+        row = got[peers[0][p], :, tile_of(half)]
         for n in range(1, narrow):
-            row = row + got[p * narrow + n, :, tile_of(half)]
+            row = row + got[peers[n][p], :, tile_of(half)]
         rows_held[p] = row
         squares = squares + row * row
     mine[:, tile_of(0, half)] = held[column]
     mine[:, tile_of(half)] = squares
     mine[:, tile_of(half + 1)] = moved
-    own_row[...] = rows_held[place]
-
-
-def finish_kernel(sizes, got, row_got, weight, row_dual, col_dual, row_out, col_out):
-    narrow, base, half, chips = sizes
+    own_row[...] = rows_held[along * wide_0 + across]
+
+
+def last_build_kernel(sizes, keep, came, sent):
+    cols = keep[:, tile_of(0, sizes[2])] + came[...]
+    for p in range(sent.shape[0]):
+        sent[p] = cols
+
+
+def store_kernel(plan, plan_out, stored, sem):
+    copy = pltpu.make_async_copy(plan, plan_out, sem)
+    copy.start()
+    stored[...] = jnp.zeros_like(stored)
+    copy.wait()
+
+
+def last_reduce_kernel(sizes, got, row_got, stored, mine, row_left):
+    cols = got[0]
+    for p in range(1, got.shape[0]):
+        cols = cols + got[p]
+    mine[...] = cols
+    rows = row_got[0]
+    for n in range(1, row_got.shape[0]):
+        rows = rows + row_got[n]
+    row_left[...] = rows
+
+
+def finish_kernel(sizes, mine, theirs, row_left, weight, row_dual, col_dual, row_out, col_out):
+    _, base, half, _ = sizes
+    core = lax.axis_index(CORE)
     step = base * weight[0:1, :]
-    rows = row_got[0]
-    for n in range(1, narrow):
-        rows = rows + row_got[n]
-    row_out[...] = row_dual[...] + step * rows
-    cols = got[0]
-    for p in range(1, 2 * chips):
-        cols = cols + got[p]
-    for j in range(2 * half):
-        col_out[:, tile_of(j)] = col_dual[:, tile_of(j)] + step * cols[j : j + 1, :]
+    row_out[...] = row_dual[...] + step * row_left[...]
+    scale = jnp.broadcast_to(step[:, 0:1], (1, half * LANES))
+    for side, part in ((core, mine), (1 - core, theirs)):
+        lanes = span(side * half, half)
+        col_out[:, lanes] = col_dual[:, lanes] + scale * part[...]
 
 
 VM = pl.BlockSpec(memory_space=pltpu.VMEM)
@@ -291,6 +303,7 @@
         name="open_step",
     )(*(pltpu.with_memory_space_constraint(array, pltpu.HBM) for array in inputs))
     cost, plan, row_mass, col_mass, row_dual, col_dual = held
+    work = pl.CostEstimate(flops=6 * rows * cols, bytes_accessed=0, transcendentals=0)
     for step in range(1, ITERS):
         came = swap(given)
         sent = pl.pallas_call(
@@ -312,42 +325,64 @@
             name="reduce_step",
         )(*near(got))
         theirs = swap(mine)
-        operands = near(
-            mine, theirs, own_row, weight, cost, plan, row_mass, col_mass, row_dual, col_dual
-        )
-        if step < ITERS - 1:
-            plan, given, kept, weight, row_dual, col_dual = pl.pallas_call(
-                functools.partial(middle_kernel, sizes),
-                out_shape=(big, give, keep, state, one, many),
-                in_specs=[VM] * 10,
-                out_specs=(VM,) * 6,
-                scratch_shapes=[spread],
-                compiler_params=ROOM,
-                name="middle_step",
-            )(*operands)
-        else:
-            plan, sent, row_sent, weight, row_dual, col_dual = pl.pallas_call(
-                functools.partial(close_kernel, sizes),
-                out_shape=(
-                    jax.ShapeDtypeStruct((rows, cols), jnp.float32),
-                    vm(wide, tiles, LANES), one, state, one, many,
-                ),
-                in_specs=[VM] * 10,
-                out_specs=(HB,) + (VM,) * 5,
-                scratch_shapes=[spread, big, pltpu.SemaphoreType.DMA((CHUNKS,))],
-                compiler_params=ROOM,
-                name="close_step",
-            )(*operands)
-    got = exchange(sent, WIDE)
+        plan, given, row_sums, moved_sums, row_all, weight, row_dual, col_dual = pl.pallas_call(
+            functools.partial(give_kernel, sizes),
+            out_shape=(big, give, spread, state, spread, state, one, many),
+            in_specs=[VM] * 9,
+            out_specs=(VM,) * 8,
+            input_output_aliases={5: 0},
+            compiler_params=ROOM,
+            cost_estimate=work,
+            name="give_step",
+        )(*near(mine, theirs, own_row, weight, cost, plan, col_mass, row_dual, col_dual))
+        plan, kept, row_sent = pl.pallas_call(
+            functools.partial(keep_kernel, sizes),
+            out_shape=(big, keep, one),
+            in_specs=[VM] * 9,
+            out_specs=(VM,) * 3,
+            input_output_aliases={2: 0},
+            compiler_params=ROOM,
+            cost_estimate=work,
+            name="keep_step",
+        )(*near(weight, cost, plan, row_mass, col_mass, row_all, col_dual, row_sums, moved_sums))
+    came = swap(given)
+    sent = pl.pallas_call(
+        functools.partial(last_build_kernel, sizes),
+        out_shape=vm(chips, 1, half * LANES),
+        in_specs=[VM] * 2,
+        out_specs=VM,
+        compiler_params=ROOM,
+        name="last_build_step",
+    )(*near(kept, came))
+    got = exchange(sent, PLANE)
     row_got = lax.all_gather(row_sent, "narrow")
+    plan, stored = pl.pallas_call(
+        store_kernel,
+        out_shape=(jax.ShapeDtypeStruct((rows, cols), jnp.float32), one),
+        in_specs=[VM],
+        out_specs=(HB, VM),
+        scratch_shapes=[pltpu.SemaphoreType.DMA],
+        compiler_params=ROOM,
+        cost_estimate=work,
+        name="store_step",
+    )(*near(plan))
+    mine, row_left = pl.pallas_call(
+        functools.partial(last_reduce_kernel, sizes),
+        out_shape=(give, one),
+        in_specs=[VM] * 3,
+        out_specs=(VM, VM),
+        compiler_params=ROOM,
+        name="last_reduce_step",
+    )(*near(got, row_got, stored))
+    theirs = swap(mine)
     row_dual, col_dual = pl.pallas_call(
         functools.partial(finish_kernel, sizes),
         out_shape=tuple(jax.ShapeDtypeStruct(s.shape, s.dtype) for s in (one, many)),
-        in_specs=[VM] * 5,
+        in_specs=[VM] * 6,
         out_specs=(VM, VM),
         compiler_params=ROOM,
         name="finish_step",
-    )(*near(got), row_got, weight, row_dual, col_dual)
+    )(*near(mine, theirs, row_left, weight, row_dual, col_dual))
     return (plan, row_dual.reshape(rows), col_dual.reshape(cols))
 
 

time: 97.9 us -> 101 us (1.032)
  Pallas kernels: 9.69 us -> 17.3 us
  waiting for transfers between devices: 10.2 us -> 4.16 us
  blocking collectives: 64.2 us -> 65.5 us
    pallas_call x3 -> x9, Pallas kernels: 5.86 us -> 13.5 us  [the longest x3 6.15 us: shards(): pl.pallas_call(functools.partial(keep_kernel, sizes), out_shape=(big, kee...]
    all_to_all x1, waiting for transfers between devices: 5.27 us -> 0.01 us  [exchange(): return lax.all_to_all(array, axes, split_axis=0, concat_axis=0, tiled=True)]
    all_to_all x3, blocking collectives: 57.7 us -> 59.3 us  [exchange(): return lax.all_to_all(array, axes, split_axis=0, concat_axis=0, tiled=True)]
    ppermute x6 -> x8, starting transfers between devices: 8.91 us -> 9.88 us  [swap(): return lax.ppermute(array, CORE, [(0, 1), (1, 0)])]
    ppermute x6 -> x8, waiting for transfers between devices: 4.98 us -> 4.15 us  [swap(): return lax.ppermute(array, CORE, [(0, 1), (1, 0)])]
  transfers between devices with their start and end apart: 7 -> 9, of which waited for: 7 -> 5; matrix products, arithmetic and copies ran while one was open for 0% -> 0% of each run, Pallas kernels for 0% -> 7%
where the time goes in v4:
time: 101 us
  blocking collectives  65.5 us (65%)
  Pallas kernels  17.3 us (17%)
  starting transfers between devices  13.4 us (13%)
  waiting for transfers between devices  4.16 us (4%)
    all_to_all x3, blocking collectives, exchange(): return lax.all_to_all(array, axes, split_axis=0, concat_axis=0, tiled=True)  59.3 us
    ppermute x8, starting transfers between devices, swap(): return lax.ppermute(array, CORE, [(0, 1), (1, 0)])  9.88 us
    pallas_call x3, Pallas kernels, shards(): pl.pallas_call(functools.partial(keep_kernel, sizes), out_shape=(big, kee...  6.15 us
    all_gather x1, blocking collectives, shards(): row_got = lax.all_gather(row_sent, 'narrow')  6.13 us
    pallas_call x3, Pallas kernels, shards(): pl.pallas_call(functools.partial(give_kernel, sizes), out_shape=(big, giv...  5.3 us
    ppermute x8, waiting for transfers between devices, swap(): return lax.ppermute(array, CORE, [(0, 1), (1, 0)])  4.15 us
    all_to_all x1, starting transfers between devices, exchange(): return lax.all_to_all(array, axes, split_axis=0, concat_axis=0, tiled=True)  3.51 us
    pallas_call x1, Pallas kernels, shards(): pl.pallas_call(functools.partial(open_kernel, sizes), out_shape=(big, big...  2.76 us
  transfers between devices with their start and end apart: 9, of which 5 were waited for; matrix products, arithmetic and copies ran while one was open for 0% of the time, Pallas kernels for 7%

profile of v4, /device:TPU:1, one launch (start us, length us, event | category | flops | bytes accessed | tf_op | source)
XLA Modules:
  0.0 101.0 jit_solution(3429336488380444022)
XLA Ops:
  0.6 2.8 %open_step.1 = (f32[128,4096]{1,0:T(8,128)S(1)}, f32[128,4096]{1,0:T(8,128)S(1)}, f32[1,128]{1,0:T(1,128)S(1)}, f32[1,4096]{1,0:T(1,128)S(1)}, f32[1,128]{1,0:T(...) custom-call(f32[128,4096]{1,0:T(8,128)} %refs_0_.1, ...), custom_call_target="tpu_custom_call" | custom-call | tf_op jit(solution)/shard_map/open_step/pallas_call | solution.py:296
  3.4 1.5 %collective-permute-start = (f32[1,2048]{1,0:T(1,128)S(1)}, f32[1,2048]{1,0:T(1,128)S(1)}, u32[]{:S(2)}, u32[]{:S(2)}) collective-permute-start(f32[1,2048]{1,0:T(1,128)S(1)} %get-tuple-element.56), channel_id=1, source_target_pairs={{0,4},{4,0},{1,5},{5,1},{2,6},{6,2},{3,7},{7,3},{8,12},{12,8},{9,1... | collective-permute-start | bytes 24584 | tf_op jit(solution)/shard_map/ppermute | solution.py:27
  4.9 0.8 collective-permute-done.came
  5.7 0.1 build_step.3
  5.7 24.2 %all_to_all.20.got = f32[64,1,2304]{2,1,0:T(1,128)S(1)} all-to-all(f32[64,1,2304]{2,1,0:T(1,128)S(1)} %build_step.3), channel_id=1, replica_groups=mesh['wide_0'=4,'wide_1'=4,'wide_2'=2,'narrow'=4] {'wide_1','narrow','wi..., dimensions={0} | all-to-all | bytes 1179648 | tf_op jit(solution)/shard_map/all_to_all | solution.py:23
  30.0 0.1 reduce_step.3
  30.1 1.9 %collective-permute-start.1 = (f32[1,2304]{1,0:T(1,128)S(1)}, f32[1,2304]{1,0:T(1,128)S(1)}, u32[]{:S(2)}, u32[]{:S(2)}) collective-permute-start(f32[1,2304]{1,0:T(1,128)S(1)} %get-tuple-element.57.mine), channel_id=1, source_target_pairs={{0,4},{4,0},{1,5},{5,1},{2,6},{6,2},{3,7},{7,3},{8,12},{12,8},{9,1... | collective-permute-start | bytes 27656 | tf_op jit(solution)/shard_map/ppermute | solution.py:27
  32.0 0.8 collective-permute-done.1.theirs
  32.8 1.8 %give_step.3 = (f32[128,4096]{1,0:T(8,128)S(1)}, f32[1,2048]{1,0:T(1,128)S(1)}, f32[128,128]{1,0:T(8,128)S(1)}, f32[8,128]{1,0:T(8,128)S(1)}, f32[128,128]{1,0:T...) custom-call(f32[1,2304]{1,0:T(1,128)S(1)} %get-tuple-element.57.mine, ...), custom_call_target="tpu_custom_call", output_to_operand_aliasing={{0}: (5, {})} | custom-call | flops 3145728 | tf_op jit(solution)/shard_map/give_step/pallas_call | solution.py:328
  34.6 0.4 collective-permute-start.2
  35.0 2.2 %keep_step.3 = (f32[128,4096]{1,0:T(8,128)S(1)}, f32[1,2304]{1,0:T(1,128)S(1)}, f32[1,128]{1,0:T(1,128)}) custom-call(f32[8,128]{1,0:T(8,128)S(1)} %get-tuple-element.65.weight, f32[128,4096]{1,0:T(8,128)S(1)} %get-tuple-element.60.cost, f32[128,4096]{1,0:T(8,128)S(1)} %get-tuple-element.66.plan, ...), custom_call_target="tpu_custom_call", output_to_operand_aliasing={{0}: (2, {})} | custom-call | flops 3145728 | tf_op jit(solution)/shard_map/keep_step/pallas_call | solution.py:338
  37.2 0.0 collective-permute-done.2.came
  37.2 0.1 build_step.4
  37.3 17.6 %all_to_all.21.got = f32[64,1,2304]{2,1,0:T(1,128)S(1)} all-to-all(f32[64,1,2304]{2,1,0:T(1,128)S(1)} %build_step.4), channel_id=1, replica_groups=mesh['wide_0'=4,'wide_1'=4,'wide_2'=2,'narrow'=4] {'wide_1','narrow','wi..., dimensions={0} | all-to-all | bytes 1179648 | tf_op jit(solution)/shard_map/all_to_all | solution.py:23
  54.8 0.1 reduce_step.4
  54.9 1.7 %collective-permute-start.3 = (f32[1,2304]{1,0:T(1,128)S(1)}, f32[1,2304]{1,0:T(1,128)S(1)}, u32[]{:S(2)}, u32[]{:S(2)}) collective-permute-start(f32[1,2304]{1,0:T(1,128)S(1)} %get-tuple-element.74.mine), channel_id=1, source_target_pairs={{0,4},{4,0},{1,5},{5,1},{2,6},{6,2},{3,7},{7,3},{8,12},{12,8},{9,1... | collective-permute-start | bytes 27656 | tf_op jit(solution)/shard_map/ppermute | solution.py:27
  56.6 0.8 collective-permute-done.3.theirs
  57.5 1.8 %give_step.4 = (f32[128,4096]{1,0:T(8,128)S(1)}, f32[1,2048]{1,0:T(1,128)S(1)}, f32[128,128]{1,0:T(8,128)S(1)}, f32[8,128]{1,0:T(8,128)S(1)}, f32[128,128]{1,0:T...) custom-call(f32[1,2304]{1,0:T(1,128)S(1)} %get-tuple-element.74.mine, ...), custom_call_target="tpu_custom_call", output_to_operand_aliasing={{0}: (5, {})} | custom-call | flops 3145728 | tf_op jit(solution)/shard_map/give_step/pallas_call | solution.py:328
  59.2 0.4 collective-permute-start.4
  59.7 2.2 %keep_step.4 = (f32[128,4096]{1,0:T(8,128)S(1)}, f32[1,2304]{1,0:T(1,128)S(1)}, f32[1,128]{1,0:T(1,128)}) custom-call(f32[8,128]{1,0:T(8,128)S(1)} %get-tuple-element.78.weight, f32[128,4096]{1,0:T(8,128)S(1)} %get-tuple-element.60.cost, f32[128,4096]{1,0:T(8,128)S(1)} %get-tuple-element.79.plan, ...), custom_call_target="tpu_custom_call", output_to_operand_aliasing={{0}: (2, {})} | custom-call | flops 3145728 | tf_op jit(solution)/shard_map/keep_step/pallas_call | solution.py:338
  61.9 0.0 collective-permute-done.4.came
  61.9 0.1 build_step.5
  61.9 17.6 %all_to_all.22.got = f32[64,1,2304]{2,1,0:T(1,128)S(1)} all-to-all(f32[64,1,2304]{2,1,0:T(1,128)S(1)} %build_step.5), channel_id=1, replica_groups=mesh['wide_0'=4,'wide_1'=4,'wide_2'=2,'narrow'=4] {'wide_1','narrow','wi..., dimensions={0} | all-to-all | bytes 1179648 | tf_op jit(solution)/shard_map/all_to_all | solution.py:23
  79.5 0.1 reduce_step.5
  79.6 1.7 %collective-permute-start.5 = (f32[1,2304]{1,0:T(1,128)S(1)}, f32[1,2304]{1,0:T(1,128)S(1)}, u32[]{:S(2)}, u32[]{:S(2)}) collective-permute-start(f32[1,2304]{1,0:T(1,128)S(1)} %get-tuple-element.86.mine), channel_id=1, source_target_pairs={{0,4},{4,0},{1,5},{5,1},{2,6},{6,2},{3,7},{7,3},{8,12},{12,8},{9,1... | collective-permute-start | bytes 27656 | tf_op jit(solution)/shard_map/ppermute | solution.py:27
  81.3 0.8 collective-permute-done.5.theirs
  82.1 1.8 %give_step.5 = (f32[128,4096]{1,0:T(8,128)S(1)}, f32[1,2048]{1,0:T(1,128)S(1)}, f32[128,128]{1,0:T(8,128)S(1)}, f32[8,128]{1,0:T(8,128)S(1)}, f32[128,128]{1,0:T...) custom-call(f32[1,2304]{1,0:T(1,128)S(1)} %get-tuple-element.86.mine, ...), custom_call_target="tpu_custom_call", output_to_operand_aliasing={{0}: (5, {})} | custom-call | flops 3145728 | tf_op jit(solution)/shard_map/give_step/pallas_call | solution.py:328
  83.9 0.4 collective-permute-start.6
  84.3 1.7 %keep_step.5 = (f32[128,4096]{1,0:T(8,128)S(1)}, f32[1,2304]{1,0:T(1,128)S(1)}, f32[1,128]{1,0:T(1,128)S(1)}) custom-call(f32[8,128]{1,0:T(8,128)S(1)} %get-tuple-element.90.weight, f32[128,4096]{1,0:T(8,128)S(1)} %get-tuple-element.60.cost, f32[128,4096]{1,0:T(8,128)S(1)} %get-tuple-element.91.plan, ...), custom_call_target="tpu_custom_call", output_to_operand_aliasing={{0}: (2, {})} | custom-call | flops 3145728 | tf_op jit(solution)/shard_map/keep_step/pallas_call | solution.py:338
  86.0 0.0 collective-permute-done.6.came
  86.1 0.7 last_build_step.1
  86.7 3.5 %all-to-all-start.3 = ((f32[16,1,2048]{2,1,0:T(1,128)}), f32[16,1,2048]{2,1,0:T(1,128)S(1)}, u32[]{:S(2)}, u32[]{:S(2)}) async-start(f32[16,1,2048]{2,1,0:T(1,128)} %last_build_step.1), calls=%async_computation.3 | async-start | bytes 262144 | tf_op jit(solution)/shard_map/all_to_all | solution.py:23
  90.2 1.3 %store_step.1 = (f32[128,4096]{1,0:T(8,128)}, f32[1,128]{1,0:T(1,128)S(1)}) custom-call(f32[128,4096]{1,0:T(8,128)S(1)} %get-tuple-element.96.plan), custom_call_target="tpu_custom_call" | custom-call | flops 3145728 | tf_op jit(solution)/shard_map/store_step/pallas_call | solution.py:359
  91.6 6.1 %all-gather.1.row_got = f32[4,1,128]{2,1,0:T(1,128)S(1)} all-gather(f32[1,1,128]{2,1,0:T(1,128)S(1)} %bitcast.7), channel_id=2, replica_groups=mesh['wide_0'=4,'wide_1'=4,'wide_2'=2,'narrow'=4] {'narrow'}, dimensions={0}, use_global_device_ids=true | all-gather | bytes 2560 | tf_op jit(solution)/shard_map/all_gather | solution.py:358
  97.7 0.0 all-to-all-done.3.got
  97.7 1.7 %collective-permute-start.7 = (f32[1,2048]{1,0:T(1,128)S(1)}, f32[1,2048]{1,0:T(1,128)S(1)}, u32[]{:S(2)}, u32[]{:S(2)}) collective-permute-start(f32[1,2048]{1,0:T(1,128)S(1)} %get-tuple-element.102.mine), channel_id=1, source_target_pairs={{0,4},{4,0},{1,5},{5,1},{2,6},{6,2},{3,7},{7,3},{8,12},{12,8},{9,1... | collective-permute-start | bytes 24584 | tf_op jit(solution)/shard_map/ppermute | solution.py:27
  99.5 0.8 collective-permute-done.7.theirs
  100.3 0.7 finish_step.1
  (1 shorter events, 0.0 us)
Async XLA Ops:
  3.4 2.3 %collective-permute-start = (f32[1,2048]{1,0:T(1,128)S(1)}, f32[1,2048]{1,0:T(1,128)S(1)}, u32[]{:S(2)}, u32[]{:S(2)}) collective-permute-start(f32[1,2048]{1,0:T(1,128)S(1)} %get-tuple-element.56), channel_id=1, source_target_pairs={{0,4},{4,0},{1,5},{5,1},{2,6},{6,2},{3,7},{7,3},{8,12},{12,8},{9,1... | collective-permute-start | bytes 24584 | tf_op jit(solution)/shard_map/ppermute | solution.py:27
  30.1 2.7 %collective-permute-start.1 = (f32[1,2304]{1,0:T(1,128)S(1)}, f32[1,2304]{1,0:T(1,128)S(1)}, u32[]{:S(2)}, u32[]{:S(2)}) collective-permute-start(f32[1,2304]{1,0:T(1,128)S(1)} %get-tuple-element.57.mine), channel_id=1, source_target_pairs={{0,4},{4,0},{1,5},{5,1},{2,6},{6,2},{3,7},{7,3},{8,12},{12,8},{9,1... | collective-permute-start | bytes 27656 | tf_op jit(solution)/shard_map/ppermute | solution.py:27
  34.6 2.6 %collective-permute-start.2 = (f32[1,2048]{1,0:T(1,128)S(1)}, f32[1,2048]{1,0:T(1,128)S(1)}, u32[]{:S(2)}, u32[]{:S(2)}) collective-permute-start(f32[1,2048]{1,0:T(1,128)S(1)} %get-tuple-element.73), channel_id=1, source_target_pairs={{0,4},{4,0},{1,5},{5,1},{2,6},{6,2},{3,7},{7,3},{8,12},{12,8},{9,1... | collective-permute-start | bytes 24584 | tf_op jit(solution)/shard_map/ppermute | solution.py:27
  54.9 2.6 %collective-permute-start.3 = (f32[1,2304]{1,0:T(1,128)S(1)}, f32[1,2304]{1,0:T(1,128)S(1)}, u32[]{:S(2)}, u32[]{:S(2)}) collective-permute-start(f32[1,2304]{1,0:T(1,128)S(1)} %get-tuple-element.74.mine), channel_id=1, source_target_pairs={{0,4},{4,0},{1,5},{5,1},{2,6},{6,2},{3,7},{7,3},{8,12},{12,8},{9,1... | collective-permute-start | bytes 27656 | tf_op jit(solution)/shard_map/ppermute | solution.py:27
  59.2 2.6 %collective-permute-start.4 = (f32[1,2048]{1,0:T(1,128)S(1)}, f32[1,2048]{1,0:T(1,128)S(1)}, u32[]{:S(2)}, u32[]{:S(2)}) collective-permute-start(f32[1,2048]{1,0:T(1,128)S(1)} %get-tuple-element.85), channel_id=1, source_target_pairs={{0,4},{4,0},{1,5},{5,1},{2,6},{6,2},{3,7},{7,3},{8,12},{12,8},{9,1... | collective-permute-start | bytes 24584 | tf_op jit(solution)/shard_map/ppermute | solution.py:27
  79.6 2.6 %collective-permute-start.5 = (f32[1,2304]{1,0:T(1,128)S(1)}, f32[1,2304]{1,0:T(1,128)S(1)}, u32[]{:S(2)}, u32[]{:S(2)}) collective-permute-start(f32[1,2304]{1,0:T(1,128)S(1)} %get-tuple-element.86.mine), channel_id=1, source_target_pairs={{0,4},{4,0},{1,5},{5,1},{2,6},{6,2},{3,7},{7,3},{8,12},{12,8},{9,1... | collective-permute-start | bytes 27656 | tf_op jit(solution)/shard_map/ppermute | solution.py:27
  83.9 2.1 %collective-permute-start.6 = (f32[1,2048]{1,0:T(1,128)S(1)}, f32[1,2048]{1,0:T(1,128)S(1)}, u32[]{:S(2)}, u32[]{:S(2)}) collective-permute-start(f32[1,2048]{1,0:T(1,128)S(1)} %get-tuple-element.99), channel_id=1, source_target_pairs={{0,4},{4,0},{1,5},{5,1},{2,6},{6,2},{3,7},{7,3},{8,12},{12,8},{9,1... | collective-permute-start | bytes 24584 | tf_op jit(solution)/shard_map/ppermute | solution.py:27
  86.7 11.0 %all-to-all-start.3 = ((f32[16,1,2048]{2,1,0:T(1,128)}), f32[16,1,2048]{2,1,0:T(1,128)S(1)}, u32[]{:S(2)}, u32[]{:S(2)}) async-start(f32[16,1,2048]{2,1,0:T(1,128)} %last_build_step.1), calls=%async_computation.3 | async-start | bytes 262144 | tf_op jit(solution)/shard_map/all_to_all | solution.py:23
  97.7 2.6 %collective-permute-start.7 = (f32[1,2048]{1,0:T(1,128)S(1)}, f32[1,2048]{1,0:T(1,128)S(1)}, u32[]{:S(2)}, u32[]{:S(2)}) collective-permute-start(f32[1,2048]{1,0:T(1,128)S(1)} %get-tuple-element.102.mine), channel_id=1, source_target_pairs={{0,4},{4,0},{1,5},{5,1},{2,6},{6,2},{3,7},{7,3},{8,12},{12,8},{9,1... | collective-permute-start | bytes 24584 | tf_op jit(solution)/shard_map/ppermute | solution.py:27

commit v5 on v4

--- a/solution.py
+++ b/solution.py
@@ -15,8 +15,8 @@
 CHUNKS = 4
 CORE = "wide_2"
 WIDE = ("wide_0", "wide_1", "wide_2")
-CHIPS = ("wide_1", "narrow", "wide_0")
-PLANE = ("wide_1", "wide_0")
+COLUMN = ("wide_2", "narrow")
+PLANE = ("wide_0", "wide_1")
 
 
 def exchange(array, axes):
@@ -43,21 +43,34 @@
     return slice(n * LANES, (n + size) * LANES)
 
 
-def dual_update(mine, theirs, own_row, weight, row_dual, col_dual, new_weight, new_row, new_col, sizes):
-    base, half = sizes[1], sizes[2]
+def dual_update(
+    got, weight, row_dual, col_dual, new_weight, new_row, new_col, rows_held, sizes
+):
+    narrow, base, half, chips = sizes
     core = lax.axis_index(CORE)
-    left_square = total(mine[:, tile_of(half)]) + total(theirs[:, tile_of(half)])
-    moved = total(mine[:, tile_of(half + 1)]) + total(theirs[:, tile_of(half + 1)])
+    place = lax.axis_index("wide_0") * lax.axis_size("wide_1") + lax.axis_index("wide_1")
+    squares, rest = None, None
+    for c in range(2):
+        rows, other = got[c * narrow, :, tile_of(half, chips)], got[c * narrow, :, tile_of(half + chips, 2)]
+        for n in range(c * narrow + 1, (c + 1) * narrow):
+            rows = rows + got[n, :, tile_of(half, chips)]
+            other = other + got[n, :, tile_of(half + chips, 2)]
+        rows_held[c] = rows
+        squares = rows * rows if squares is None else squares + rows * rows
+        rest = other if rest is None else rest + other
+    left_square = total(squares) + total(rest[:, tile_of(0)])
+    moved = total(rest[:, tile_of(1)])
     old = weight[...]
     dual_step = base * old
     dual_moved = dual_step * dual_step * left_square
     fresh_weight = jnp.sqrt(old * jnp.sqrt((dual_moved + 1.0) / (moved + 1.0)))
     new_weight[...] = fresh_weight
-    new_row[...] = row_dual[...] + dual_step[0:1, :] * own_row[...]
+    new_row[...] = row_dual[...] + dual_step[0:1, :] * rows_held[core, :, span(place, 1)]
     scale = jnp.broadcast_to(dual_step[0:1, 0:1], (1, half * LANES))
-    for side, part in ((core, mine), (1 - core, theirs)):
-        lanes = span(side * half, half)
-        new_col[:, lanes] = col_dual[:, lanes] + scale * part[:, tile_of(0, half)]
+    column = lax.axis_index("narrow")
+    for c in range(2):
+        lanes = tile_of(c * half, half)
+        new_col[:, lanes] = col_dual[:, lanes] + scale * got[c * narrow + column, :, tile_of(0, half)]
     return base / fresh_weight
 
 
@@ -153,12 +166,12 @@
 
 
 def give_kernel(
-    sizes, mine, theirs, own_row, weight, cost, plan, col_mass, row_dual, col_dual,
-    fresh_plan, give, row_sums, moved_sums, row_all, new_weight, new_row, new_col,
+    sizes, got, weight, cost, plan, col_mass, row_dual, col_dual,
+    fresh_plan, give, row_sums, moved_sums, row_all, new_weight, new_row, new_col, rows_held,
 ):
     _, _, half, chips = sizes
     step = dual_update(
-        mine, theirs, own_row, weight, row_dual, col_dual, new_weight, new_row, new_col, sizes
+        got, weight, row_dual, col_dual, new_weight, new_row, new_col, rows_held, sizes
     )
     spread_rows(new_row[...], row_all)
     side = 1 - lax.axis_index(CORE)
@@ -171,8 +184,8 @@
 
 
 def keep_kernel(
-    sizes, weight, cost, plan, row_mass, col_mass, row_all, col_dual, row_sums, moved_sums,
-    fresh_plan, keep, row_share,
+    sizes, weight, cost, plan, half_plan, row_mass, col_mass, row_all, col_dual, row_sums,
+    moved_sums, fresh_plan, keep, row_share,
 ):
     _, base, half, chips = sizes
     side = lax.axis_index(CORE)
@@ -196,38 +209,25 @@
         sent[p, :, tile_of(half, 2)] = rest
 
 
-def reduce_kernel(sizes, got, mine, own_row, held, rows_held):
+def reduce_kernel(sizes, got, sent):
     narrow, base, half, chips = sizes
-    column = lax.axis_index("narrow")
-    across, along = lax.axis_index("wide_0"), lax.axis_index("wide_1")
-    wide_0 = lax.axis_size("wide_0")
-    peers = [
-        [(b * narrow + n) * wide_0 + a for b in range(chips // wide_0) for a in range(wide_0)]
-        for n in range(narrow)
-    ]
-    col_squares = jnp.zeros((1, half * LANES), jnp.float32)
-    moved = jnp.zeros((1, LANES), jnp.float32)
-    for n in range(narrow):
-        cols = got[peers[n][0]]
-        for p in peers[n][1:]:
-            cols = cols + got[p]
-        moved = moved + cols[:, tile_of(half + 1)]
-        cols = cols[:, tile_of(0, half)]
-        held[n] = cols
-        col_squares = col_squares + cols * cols
-    squares = jnp.zeros((1, LANES), jnp.float32)
-    for r in range(half):
-        squares = squares + col_squares[:, tile_of(r)]
+    cols = got[0]
+    for p in range(1, chips):
+        cols = cols + got[p]
+    moved = cols[:, tile_of(half + 1)]
+    cols = cols[:, tile_of(0, half)]
+    sent[0, :, tile_of(0, half)] = cols
+    cols = cols * cols
+    squares = cols[:, tile_of(0)]
+    for r in range(1, half):
+        squares = squares + cols[:, tile_of(r)]
     for p in range(chips):
-        row = got[peers[0][p], :, tile_of(half)]
-        for n in range(1, narrow):
-            row = row + got[peers[n][p], :, tile_of(half)]
-        rows_held[p] = row
-        squares = squares + row * row
-    mine[:, tile_of(0, half)] = held[column]
-    mine[:, tile_of(half)] = squares
-    mine[:, tile_of(half + 1)] = moved
-    own_row[...] = rows_held[along * wide_0 + across]
+        sent[0, :, tile_of(half + p)] = got[p, :, tile_of(half)]
+    sent[0, :, tile_of(half + chips)] = squares
+    sent[0, :, tile_of(half + chips + 1)] = moved
+    everything = sent[0]
+    for q in range(1, sent.shape[0]):
+        sent[q] = everything
 
 
 def last_build_kernel(sizes, keep, came, sent):
@@ -308,43 +308,45 @@
         came = swap(given)
         sent = pl.pallas_call(
             functools.partial(build_kernel, sizes),
-            out_shape=vm(chips * narrow, 1, (half + 2) * LANES),
+            out_shape=vm(chips, 1, (half + 2) * LANES),
             in_specs=[VM] * 2,
             out_specs=VM,
             compiler_params=ROOM,
             name="build_step",
         )(*near(kept, came))
-        got = exchange(sent, CHIPS)
-        mine, own_row = pl.pallas_call(
+        got = exchange(sent, PLANE)
+        sent = pl.pallas_call(
             functools.partial(reduce_kernel, sizes),
-            out_shape=(keep, one),
+            out_shape=vm(2 * narrow, 1, (half + chips + 2) * LANES),
             in_specs=[VM],
-            out_specs=(VM, VM),
-            scratch_shapes=[vm(narrow, 1, half * LANES), vm(chips, 1, rows)],
+            out_specs=VM,
             compiler_params=ROOM,
             name="reduce_step",
         )(*near(got))
-        theirs = swap(mine)
-        plan, given, row_sums, moved_sums, row_all, weight, row_dual, col_dual = pl.pallas_call(
+        got = exchange(sent, COLUMN)
+        half_plan, given, row_sums, moved_sums, row_all, weight, row_dual, col_dual = pl.pallas_call(
             functools.partial(give_kernel, sizes),
             out_shape=(big, give, spread, state, spread, state, one, many),
-            in_specs=[VM] * 9,
+            in_specs=[VM] * 7,
             out_specs=(VM,) * 8,
-            input_output_aliases={5: 0},
+            scratch_shapes=[vm(2, 1, chips * LANES)],
             compiler_params=ROOM,
             cost_estimate=work,
             name="give_step",
-        )(*near(mine, theirs, own_row, weight, cost, plan, col_mass, row_dual, col_dual))
+        )(*near(got, weight, cost, plan, col_mass, row_dual, col_dual))
         plan, kept, row_sent = pl.pallas_call(
             functools.partial(keep_kernel, sizes),
             out_shape=(big, keep, one),
-            in_specs=[VM] * 9,
+            in_specs=[VM] * 10,
             out_specs=(VM,) * 3,
-            input_output_aliases={2: 0},
+            input_output_aliases={3: 0},
             compiler_params=ROOM,
             cost_estimate=work,
             name="keep_step",
-        )(*near(weight, cost, plan, row_mass, col_mass, row_all, col_dual, row_sums, moved_sums))
+        )(*near(
+            weight, cost, plan, half_plan, row_mass, col_mass, row_all, col_dual, row_sums,
+            moved_sums,
+        ))
     came = swap(given)
     sent = pl.pallas_call(
         functools.partial(last_build_kernel, sizes),

time: 101 us -> 93.9 us (0.930)
  Pallas kernels: 17.3 us -> 10.9 us
  blocking collectives: 65.5 us -> 71.4 us
  starting transfers between devices: 13.4 us -> 8.56 us
  waiting for transfers between devices: 4.16 us -> 1.82 us
    all_to_all x3 -> x6, blocking collectives: 59.3 us -> 64.5 us  [exchange(): return lax.all_to_all(array, axes, split_axis=0, concat_axis=0, tiled=True)]
    ppermute x8 -> x5, starting transfers between devices: 9.88 us -> 5.05 us  [swap(): return lax.ppermute(array, CORE, [(0, 1), (1, 0)])]
    pallas_call x3, Pallas kernels: 5.3 us -> 2.21 us  [shards(): pl.pallas_call(functools.partial(give_kernel, sizes), out_shape=(big, giv...]
    pallas_call x3, Pallas kernels: 6.15 us -> 3.07 us  [shards(): pl.pallas_call(functools.partial(keep_kernel, sizes), out_shape=(big, kee...]
    ppermute x8 -> x5, waiting for transfers between devices: 4.15 us -> 1.81 us  [swap(): return lax.ppermute(array, CORE, [(0, 1), (1, 0)])]
  transfers between devices with their start and end apart: 9 -> 6, of which waited for: 5 -> 3; matrix products, arithmetic and copies ran while one was open for 0% -> 0% of each run, Pallas kernels for 7% -> 5%
where the time goes in v5:
time: 93.9 us; the launch traced here: 93.5 us
  blocking collectives  71.4 us (76%)
  Pallas kernels  10.9 us (12%)
  starting transfers between devices  8.56 us (9%)
  waiting for transfers between devices  1.82 us (2%)
    all_to_all x6, blocking collectives, exchange(): return lax.all_to_all(array, axes, split_axis=0, concat_axis=0, tiled=True)  64.5 us
    all_gather x1, blocking collectives, shards(): row_got = lax.all_gather(row_sent, 'narrow')  6.96 us
    ppermute x5, starting transfers between devices, swap(): return lax.ppermute(array, CORE, [(0, 1), (1, 0)])  5.05 us
    all_to_all x1, starting transfers between devices, exchange(): return lax.all_to_all(array, axes, split_axis=0, concat_axis=0, tiled=True)  3.51 us
    pallas_call x3, Pallas kernels, shards(): pl.pallas_call(functools.partial(keep_kernel, sizes), out_shape=(big, kee...  3.07 us
    pallas_call x1, Pallas kernels, shards(): pl.pallas_call(functools.partial(open_kernel, sizes), out_shape=(big, big...  2.76 us
    pallas_call x3, Pallas kernels, shards(): pl.pallas_call(functools.partial(give_kernel, sizes), out_shape=(big, giv...  2.21 us
  transfers between devices with their start and end apart: 6, of which 3 were waited for; matrix products, arithmetic and copies ran while one was open for 0% of the time, Pallas kernels for 5%

profile of v5, /device:TPU:1, one launch (start us, length us, event | category | flops | bytes accessed | tf_op | source)
XLA Modules:
  0.0 93.5 jit_solution(5152690101319432349)
XLA Ops:
  0.6 2.8 %open_step.1 = (f32[128,4096]{1,0:T(8,128)S(1)}, f32[128,4096]{1,0:T(8,128)S(1)}, f32[1,128]{1,0:T(1,128)S(1)}, f32[1,4096]{1,0:T(1,128)S(1)}, f32[1,128]{1,0:T(...) custom-call(f32[128,4096]{1,0:T(8,128)} %refs_0_.1, ...), custom_call_target="tpu_custom_call" | custom-call | tf_op jit(solution)/shard_map/open_step/pallas_call | solution.py:296
  3.4 1.5 %collective-permute-start = (f32[1,2048]{1,0:T(1,128)S(1)}, f32[1,2048]{1,0:T(1,128)S(1)}, u32[]{:S(2)}, u32[]{:S(2)}) collective-permute-start(f32[1,2048]{1,0:T(1,128)S(1)} %get-tuple-element.50), channel_id=1, source_target_pairs={{0,4},{4,0},{1,5},{5,1},{2,6},{6,2},{3,7},{7,3},{8,12},{12,8},{9,1... | collective-permute-start | bytes 24584 | tf_op jit(solution)/shard_map/ppermute | solution.py:27
  4.9 0.8 collective-permute-done.came
  5.7 14.2 %all_to_all.35.got = f32[16,1,2304]{2,1,0:T(1,128)S(1)} all-to-all(f32[16,1,2304]{2,1,0:T(1,128)S(1)} %build_step.3), channel_id=1, replica_groups=mesh['wide_0'=4,'wide_1'=4,'wide_2'=2,'narrow'=4] {'wide_0','wide_1'}, dimensions={0} | all-to-all | bytes 294912 | tf_op jit(solution)/shard_map/all_to_all | solution.py:23
  20.0 11.3 %all_to_all.36.got = f32[8,1,4352]{2,1,0:T(1,128)S(1)} all-to-all(f32[8,1,4352]{2,1,0:T(1,128)S(1)} %reduce_step.3), channel_id=1, replica_groups=mesh['wide_0'=4,'wide_1'=4,'wide_2'=2,'narrow'=4] {'wide_2','narrow'}, dimensions={0} | all-to-all | bytes 278528 | tf_op jit(solution)/shard_map/all_to_all | solution.py:23
  31.3 0.7 give_step.3
  32.0 0.5 collective-permute-start.1
  32.5 1.2 %keep_step.3 = (f32[128,4096]{1,0:T(8,128)S(1)}, f32[1,2304]{1,0:T(1,128)S(1)}, f32[1,128]{1,0:T(1,128)}) custom-call(f32[8,128]{1,0:T(8,128)S(1)} %get-tuple-element.57.weight, f32[128,4096]{1,0:T(8,128)S(1)} %get-tuple-element.52.cost, f32[128,4096]{1,0:T(8,128)S(1)} %get-tuple-element.53.plan, ...), custom_call_target="tpu_custom_call", output_to_operand_aliasing={{0}: (3, {})} | custom-call | flops 3145728 | tf_op jit(solution)/shard_map/keep_step/pallas_call | solution.py:337
  33.7 0.0 collective-permute-done.1.came
  33.7 10.0 %all_to_all.37.got = f32[16,1,2304]{2,1,0:T(1,128)S(1)} all-to-all(f32[16,1,2304]{2,1,0:T(1,128)S(1)} %build_step.4), channel_id=1, replica_groups=mesh['wide_0'=4,'wide_1'=4,'wide_2'=2,'narrow'=4] {'wide_0','wide_1'}, dimensions={0} | all-to-all | bytes 294912 | tf_op jit(solution)/shard_map/all_to_all | solution.py:23
  43.7 9.6 %all_to_all.38.got = f32[8,1,4352]{2,1,0:T(1,128)S(1)} all-to-all(f32[8,1,4352]{2,1,0:T(1,128)S(1)} %reduce_step.4), channel_id=1, replica_groups=mesh['wide_0'=4,'wide_1'=4,'wide_2'=2,'narrow'=4] {'wide_2','narrow'}, dimensions={0} | all-to-all | bytes 278528 | tf_op jit(solution)/shard_map/all_to_all | solution.py:23
  53.3 0.7 give_step.4
  54.1 0.5 collective-permute-start.2
  54.6 1.2 %keep_step.4 = (f32[128,4096]{1,0:T(8,128)S(1)}, f32[1,2304]{1,0:T(1,128)S(1)}, f32[1,128]{1,0:T(1,128)}) custom-call(f32[8,128]{1,0:T(8,128)S(1)} %get-tuple-element.68.weight, f32[128,4096]{1,0:T(8,128)S(1)} %get-tuple-element.52.cost, f32[128,4096]{1,0:T(8,128)S(1)} %get-tuple-element.66.plan, ...), custom_call_target="tpu_custom_call", output_to_operand_aliasing={{0}: (3, {})} | custom-call | flops 3145728 | tf_op jit(solution)/shard_map/keep_step/pallas_call | solution.py:337
  55.8 0.0 collective-permute-done.2.came
  55.8 9.8 %all_to_all.39.got = f32[16,1,2304]{2,1,0:T(1,128)S(1)} all-to-all(f32[16,1,2304]{2,1,0:T(1,128)S(1)} %build_step.5), channel_id=1, replica_groups=mesh['wide_0'=4,'wide_1'=4,'wide_2'=2,'narrow'=4] {'wide_0','wide_1'}, dimensions={0} | all-to-all | bytes 294912 | tf_op jit(solution)/shard_map/all_to_all | solution.py:23
  65.6 9.6 %all_to_all.40.got = f32[8,1,4352]{2,1,0:T(1,128)S(1)} all-to-all(f32[8,1,4352]{2,1,0:T(1,128)S(1)} %reduce_step.5), channel_id=1, replica_groups=mesh['wide_0'=4,'wide_1'=4,'wide_2'=2,'narrow'=4] {'wide_2','narrow'}, dimensions={0} | all-to-all | bytes 278528 | tf_op jit(solution)/shard_map/all_to_all | solution.py:23
  75.2 0.7 give_step.5
  76.0 0.5 collective-permute-start.3
  76.5 0.7 keep_step.5
  77.1 0.2 collective-permute-done.3.came
  77.3 0.7 last_build_step.1
  77.9 3.5 %all-to-all-start.6 = ((f32[16,1,2048]{2,1,0:T(1,128)}), f32[16,1,2048]{2,1,0:T(1,128)S(1)}, u32[]{:S(2)}, u32[]{:S(2)}) async-start(f32[16,1,2048]{2,1,0:T(1,128)} %last_build_step.1), calls=%async_computation.6 | async-start | bytes 262144 | tf_op jit(solution)/shard_map/all_to_all | solution.py:23
  81.5 1.3 %store_step.1 = (f32[128,4096]{1,0:T(8,128)}, f32[1,128]{1,0:T(1,128)S(1)}) custom-call(f32[128,4096]{1,0:T(8,128)S(1)} %get-tuple-element.84.plan), custom_call_target="tpu_custom_call" | custom-call | flops 3145728 | tf_op jit(solution)/shard_map/store_step/pallas_call | solution.py:361
  82.8 7.0 %all-gather.1.row_got = f32[4,1,128]{2,1,0:T(1,128)S(1)} all-gather(f32[1,1,128]{2,1,0:T(1,128)S(1)} %bitcast.7), channel_id=2, replica_groups=mesh['wide_0'=4,'wide_1'=4,'wide_2'=2,'narrow'=4] {'narrow'}, dimensions={0}, use_global_device_ids=true | all-gather | bytes 2560 | tf_op jit(solution)/shard_map/all_gather | solution.py:360
  89.8 0.0 all-to-all-done.6.got
  89.8 2.1 %collective-permute-start.4 = (f32[1,2048]{1,0:T(1,128)S(1)}, f32[1,2048]{1,0:T(1,128)S(1)}, u32[]{:S(2)}, u32[]{:S(2)}) collective-permute-start(f32[1,2048]{1,0:T(1,128)S(1)} %get-tuple-element.90.mine), channel_id=1, source_target_pairs={{0,4},{4,0},{1,5},{5,1},{2,6},{6,2},{3,7},{7,3},{8,12},{12,8},{9,1... | collective-permute-start | bytes 24584 | tf_op jit(solution)/shard_map/ppermute | solution.py:27
  91.9 0.8 collective-permute-done.4.theirs
  92.8 0.7 finish_step.1
  (7 shorter events, 0.2 us)
Async XLA Ops:
  3.4 2.3 %collective-permute-start = (f32[1,2048]{1,0:T(1,128)S(1)}, f32[1,2048]{1,0:T(1,128)S(1)}, u32[]{:S(2)}, u32[]{:S(2)}) collective-permute-start(f32[1,2048]{1,0:T(1,128)S(1)} %get-tuple-element.50), channel_id=1, source_target_pairs={{0,4},{4,0},{1,5},{5,1},{2,6},{6,2},{3,7},{7,3},{8,12},{12,8},{9,1... | collective-permute-start | bytes 24584 | tf_op jit(solution)/shard_map/ppermute | solution.py:27
  32.0 1.7 %collective-permute-start.1 = (f32[1,2048]{1,0:T(1,128)S(1)}, f32[1,2048]{1,0:T(1,128)S(1)}, u32[]{:S(2)}, u32[]{:S(2)}) collective-permute-start(f32[1,2048]{1,0:T(1,128)S(1)} %get-tuple-element.65), channel_id=1, source_target_pairs={{0,4},{4,0},{1,5},{5,1},{2,6},{6,2},{3,7},{7,3},{8,12},{12,8},{9,1... | collective-permute-start | bytes 24584 | tf_op jit(solution)/shard_map/ppermute | solution.py:27
  54.1 1.7 %collective-permute-start.2 = (f32[1,2048]{1,0:T(1,128)S(1)}, f32[1,2048]{1,0:T(1,128)S(1)}, u32[]{:S(2)}, u32[]{:S(2)}) collective-permute-start(f32[1,2048]{1,0:T(1,128)S(1)} %get-tuple-element.75), channel_id=1, source_target_pairs={{0,4},{4,0},{1,5},{5,1},{2,6},{6,2},{3,7},{7,3},{8,12},{12,8},{9,1... | collective-permute-start | bytes 24584 | tf_op jit(solution)/shard_map/ppermute | solution.py:27
  76.0 1.3 %collective-permute-start.3 = (f32[1,2048]{1,0:T(1,128)S(1)}, f32[1,2048]{1,0:T(1,128)S(1)}, u32[]{:S(2)}, u32[]{:S(2)}) collective-permute-start(f32[1,2048]{1,0:T(1,128)S(1)} %get-tuple-element.87), channel_id=1, source_target_pairs={{0,4},{4,0},{1,5},{5,1},{2,6},{6,2},{3,7},{7,3},{8,12},{12,8},{9,1... | collective-permute-start | bytes 24584 | tf_op jit(solution)/shard_map/ppermute | solution.py:27
  77.9 11.8 %all-to-all-start.6 = ((f32[16,1,2048]{2,1,0:T(1,128)}), f32[16,1,2048]{2,1,0:T(1,128)S(1)}, u32[]{:S(2)}, u32[]{:S(2)}) async-start(f32[16,1,2048]{2,1,0:T(1,128)} %last_build_step.1), calls=%async_computation.6 | async-start | bytes 262144 | tf_op jit(solution)/shard_map/all_to_all | solution.py:23
  89.8 3.0 %collective-permute-start.4 = (f32[1,2048]{1,0:T(1,128)S(1)}, f32[1,2048]{1,0:T(1,128)S(1)}, u32[]{:S(2)}, u32[]{:S(2)}) collective-permute-start(f32[1,2048]{1,0:T(1,128)S(1)} %get-tuple-element.90.mine), channel_id=1, source_target_pairs={{0,4},{4,0},{1,5},{5,1},{2,6},{6,2},{3,7},{7,3},{8,12},{12,8},{9,1... | collective-permute-start | bytes 24584 | tf_op jit(solution)/shard_map/ppermute | solution.py:27

commit v6 on v5

--- a/solution.py
+++ b/solution.py
@@ -12,7 +12,9 @@
 ITERS = 4
 LANES = 128
 GROUP = 8
-CHUNKS = 4
+CHUNKS = 2
+WIDTH = 2
+MOVED = 2
 CORE = "wide_2"
 WIDE = ("wide_0", "wide_1", "wide_2")
 COLUMN = ("wide_2", "narrow")
@@ -78,27 +80,32 @@
     first, count = tiles
     groups = len(state[0])
 
-    def tile(n, state):
-        rows, moved = list(state[0]), state[1]
-        j = first + n
-        lanes = span(j, 1)
-        col = jnp.broadcast_to(col_dual[:, lanes], (GROUP, LANES))
-        cols = None
+    def some(m, state):
+        rows, moved = list(state[0]), list(state[1])
+        cols = [[None, None] for _ in range(WIDTH)]
+        lanes = [span(first + WIDTH * m + w, 1) for w in range(WIDTH)]
+        duals = [jnp.broadcast_to(col_dual[:, lanes[w]], (GROUP, LANES)) for w in range(WIDTH)]
         for g in range(groups):
             part = slice(g * GROUP, (g + 1) * GROUP)
-            old = plan[part, lanes]
-            gap = cost[part, lanes] - row_all[part, :] - col
-            fresh = jnp.maximum(old - step * gap, 0.0)
-            change = fresh - old
-            extrap = fresh + change
-            fresh_plan[part, lanes] = fresh
-            rows[g] = rows[g] + extrap
-            cols = extrap if cols is None else cols + extrap
-            moved = moved + change * change
-        done(n, j, down(cols))
-        return tuple(rows), moved
-
-    return lax.fori_loop(0, count, tile, state, unroll=2)
+            both = None
+            for w in range(WIDTH):
+                old = plan[part, lanes[w]]
+                gap = cost[part, lanes[w]] - row_all[part, :] - duals[w]
+                fresh = jnp.maximum(old - step * gap, 0.0)
+                change = fresh - old
+                extrap = fresh + change
+                fresh_plan[part, lanes[w]] = fresh
+                both = extrap if both is None else both + extrap
+                sums = cols[w]
+                sums[g % 2] = extrap if sums[g % 2] is None else sums[g % 2] + extrap
+                at = (g * WIDTH + w) % len(moved)
+                moved[at] = moved[at] + change * change
+            rows[g] = rows[g] + both
+        for w in range(WIDTH):
+            done(WIDTH * m + w, first + WIDTH * m + w, down(cols[w][0] + cols[w][1]))
+        return tuple(rows), tuple(moved)
+
+    return lax.fori_loop(0, count // WIDTH, some, state)
 
 
 def spread_rows(row_dual, row_all):
@@ -111,7 +118,7 @@
 
 def zeros(row_all):
     zero = jnp.zeros((GROUP, LANES), jnp.float32)
-    return tuple(zero for _ in range(row_all.shape[0] // GROUP)), zero
+    return tuple(zero for _ in range(row_all.shape[0] // GROUP)), (zero,) * MOVED
 
 
 def into(target, col_mass, wide):
@@ -124,45 +131,53 @@
 def tail(keep, row_mass, state, sizes):
     narrow, _, half, _ = sizes
     keep[:, tile_of(half)] = row_mass[...] * (1.0 / narrow) - gather_rows(state[0])
-    keep[:, tile_of(half + 1)] = down(state[1])
+    keep[:, tile_of(half + 1)] = down(sum(state[1][1:], state[1][0]))
 
 
 def open_kernel(sizes, *refs):
     narrow, base, half, chips = sizes
-    sources, targets, (give, keep, weight, row_all, sems) = refs[:6], refs[6:12], refs[12:]
+    sources, targets = refs[:6], refs[6:12]
+    fresh_plan, give, row_sums, moved_sums, row_all, weight, sems = refs[12:]
     cost, plan, row_mass, col_mass, row_dual, col_dual = targets
     core = lax.axis_index(CORE)
-    tiles = 2 * half // CHUNKS
+    tiles = half // CHUNKS
     weight[...] = jnp.full((GROUP, LANES), base, jnp.float32)
     small = [pltpu.make_async_copy(sources[n], targets[n], sems.at[n, 0]) for n in range(2, 6)]
     for copy in small:
         copy.start()
-    firsts, copies = [], []
-    for k in range(CHUNKS):
-        side = 1 - core if k < CHUNKS // 2 else core
-        firsts.append(side * half + (k % (CHUNKS // 2)) * tiles)
-        lanes = span(firsts[k], tiles)
+    big = []
+    for k in range(CHUNKS + 1):
+        first = (1 - core) * half + k * tiles if k < CHUNKS else core * half
+        lanes = span(first, tiles if k < CHUNKS else half)
         for n in range(2):
             copy = pltpu.make_async_copy(
                 sources[n].at[:, lanes], targets[n].at[:, lanes], sems.at[n, k]
             )
             copy.start()
-            copies.append(copy)
+            big.append(copy)
     for copy in small:
         copy.wait()
     spread_rows(row_dual[...], row_all)
     state = zeros(row_all)
+    put = into(give, col_mass, 2 * chips)
     for k in range(CHUNKS):
-        copies[2 * k].wait()
-        copies[2 * k + 1].wait()
-        target = give if k < CHUNKS // 2 else keep
-        shift = (k % (CHUNKS // 2)) * tiles
-        put = into(target, col_mass, 2 * chips)
+        big[2 * k].wait()
+        big[2 * k + 1].wait()
+        shift = k * tiles
         state = sweep(
-            jnp.float32(1.0), cost, plan, plan, row_all, col_dual, (firsts[k], tiles), state,
-            lambda n, j, cols, put=put, shift=shift: put(n + shift, j, cols),
+            jnp.float32(1.0), cost, plan, fresh_plan, row_all, col_dual,
+            ((1 - core) * half + shift, tiles), state,
+            lambda n, j, cols, shift=shift: put(n + shift, j, cols),
         )
-    tail(keep, row_mass, state, sizes)
+    hold(state, row_sums, moved_sums)
+    for copy in big[2 * CHUNKS :]:
+        copy.wait()
+
+
+def hold(state, row_sums, moved_sums):
+    row_sums[...] = jnp.concatenate(state[0], axis=0)
+    for n in range(MOVED):
+        moved_sums[n] = state[1][n]
 
 
 def give_kernel(
@@ -175,29 +190,31 @@
     )
     spread_rows(new_row[...], row_all)
     side = 1 - lax.axis_index(CORE)
-    rows, moved = sweep(
+    state = sweep(
         step, cost, plan, fresh_plan, row_all, new_col, (side * half, half), zeros(row_all),
         into(give, col_mass, 2 * chips),
     )
-    row_sums[...] = jnp.concatenate(rows, axis=0)
-    moved_sums[...] = moved
+    hold(state, row_sums, moved_sums)
 
 
 def keep_kernel(
     sizes, weight, cost, plan, half_plan, row_mass, col_mass, row_all, col_dual, row_sums,
-    moved_sums, fresh_plan, keep, row_share,
+    moved_sums, fresh_plan, keep, *row_share,
 ):
     _, base, half, chips = sizes
     side = lax.axis_index(CORE)
     rows = row_sums[...]
     groups = row_all.shape[0] // GROUP
-    state = tuple(rows[g * GROUP : (g + 1) * GROUP] for g in range(groups)), moved_sums[...]
+    state = tuple(rows[g * GROUP : (g + 1) * GROUP] for g in range(groups)), tuple(
+        moved_sums[n] for n in range(MOVED)
+    )
     state = sweep(
         base / weight[...], cost, plan, fresh_plan, row_all, col_dual, (side * half, half), state,
         into(keep, col_mass, 2 * chips),
     )
     tail(keep, row_mass, state, sizes)
-    row_share[...] = keep[:, tile_of(half)]
+    for share in row_share:
+        share[...] = keep[:, tile_of(half)]
 
 
 def build_kernel(sizes, keep, came, sent):
@@ -236,14 +253,14 @@
         sent[p] = cols
 
 
-def store_kernel(plan, plan_out, stored, sem):
+def store_kernel(plan, after, plan_out, stored, sem):
     copy = pltpu.make_async_copy(plan, plan_out, sem)
     copy.start()
-    stored[...] = jnp.zeros_like(stored)
+    stored[...] = after[:, tile_of(0)]
     copy.wait()
 
 
-def last_reduce_kernel(sizes, got, row_got, stored, mine, row_left):
+def last_reduce_kernel(sizes, got, row_got, mine, row_left):
     cols = got[0]
     for p in range(1, got.shape[0]):
         cols = cols + got[p]
@@ -254,7 +271,9 @@
     row_left[...] = rows
 
 
-def finish_kernel(sizes, mine, theirs, row_left, weight, row_dual, col_dual, row_out, col_out):
+def finish_kernel(
+    sizes, mine, theirs, stored, row_left, weight, row_dual, col_dual, row_out, col_out
+):
     _, base, half, _ = sizes
     core = lax.axis_index(CORE)
     step = base * weight[0:1, :]
@@ -292,18 +311,39 @@
     give, keep = vm(1, half * LANES), vm(1, (half + 2) * LANES)
     spread = vm(rows, LANES)
 
+    work = pl.CostEstimate(flops=6 * rows * cols, bytes_accessed=0, transcendentals=0)
+    sums = vm(MOVED, GROUP, LANES)
+
+    def keep_step(last, *operands):
+        share = (one,) if last else ()
+        return pl.pallas_call(
+            functools.partial(keep_kernel, sizes),
+            out_shape=(big, keep) + share,
+            in_specs=[VM] * 10,
+            out_specs=(VM,) * (2 + len(share)),
+            input_output_aliases={3: 0},
+            compiler_params=ROOM,
+            cost_estimate=work,
+            name="keep_step",
+        )(*near(*operands))
+
     inputs = (cost, plan, row_mass, col_mass, row_dual, col_dual)
-    *held, given, kept, weight = pl.pallas_call(
+    outputs = pl.pallas_call(
         functools.partial(open_kernel, sizes),
-        out_shape=(big, big, one, many, one, many, give, keep, state),
+        out_shape=(big, big, one, many, one, many, big, give, spread, sums, spread, state),
         in_specs=[HB] * 6,
-        out_specs=(VM,) * 9,
-        scratch_shapes=[spread, pltpu.SemaphoreType.DMA((6, CHUNKS))],
+        out_specs=(VM,) * 12,
+        scratch_shapes=[pltpu.SemaphoreType.DMA((6, CHUNKS + 1))],
         compiler_params=ROOM,
+        cost_estimate=work,
         name="open_step",
     )(*(pltpu.with_memory_space_constraint(array, pltpu.HBM) for array in inputs))
-    cost, plan, row_mass, col_mass, row_dual, col_dual = held
-    work = pl.CostEstimate(flops=6 * rows * cols, bytes_accessed=0, transcendentals=0)
+    cost, plan, row_mass, col_mass, row_dual, col_dual = outputs[:6]
+    half_plan, given, row_sums, moved_sums, row_all, weight = outputs[6:]
+    plan, kept = keep_step(
+        False, weight, cost, plan, half_plan, row_mass, col_mass, row_all, col_dual, row_sums,
+        moved_sums,
+    )
     for step in range(1, ITERS):
         came = swap(given)
         sent = pl.pallas_call(
@@ -326,7 +366,7 @@
         got = exchange(sent, COLUMN)
         half_plan, given, row_sums, moved_sums, row_all, weight, row_dual, col_dual = pl.pallas_call(
             functools.partial(give_kernel, sizes),
-            out_shape=(big, give, spread, state, spread, state, one, many),
+            out_shape=(big, give, spread, sums, spread, state, one, many),
             in_specs=[VM] * 7,
             out_specs=(VM,) * 8,
             scratch_shapes=[vm(2, 1, chips * LANES)],
@@ -334,19 +374,10 @@
             cost_estimate=work,
             name="give_step",
         )(*near(got, weight, cost, plan, col_mass, row_dual, col_dual))
-        plan, kept, row_sent = pl.pallas_call(
-            functools.partial(keep_kernel, sizes),
-            out_shape=(big, keep, one),
-            in_specs=[VM] * 10,
-            out_specs=(VM,) * 3,
-            input_output_aliases={3: 0},
-            compiler_params=ROOM,
-            cost_estimate=work,
-            name="keep_step",
-        )(*near(
-            weight, cost, plan, half_plan, row_mass, col_mass, row_all, col_dual, row_sums,
-            moved_sums,
-        ))
+        plan, kept, *row_sent = keep_step(
+            step == ITERS - 1, weight, cost, plan, half_plan, row_mass, col_mass, row_all,
+            col_dual, row_sums, moved_sums,
+        )
     came = swap(given)
     sent = pl.pallas_call(
         functools.partial(last_build_kernel, sizes),
@@ -357,34 +388,34 @@
         name="last_build_step",
     )(*near(kept, came))
     got = exchange(sent, PLANE)
-    row_got = lax.all_gather(row_sent, "narrow")
+    row_got = lax.all_gather(row_sent[0], "narrow")
+    mine, row_left = pl.pallas_call(
+        functools.partial(last_reduce_kernel, sizes),
+        out_shape=(give, one),
+        in_specs=[VM] * 2,
+        out_specs=(VM, VM),
+        compiler_params=ROOM,
+        name="last_reduce_step",
+    )(*near(got, row_got))
+    theirs = swap(mine)
     plan, stored = pl.pallas_call(
         store_kernel,
         out_shape=(jax.ShapeDtypeStruct((rows, cols), jnp.float32), one),
-        in_specs=[VM],
+        in_specs=[VM] * 2,
         out_specs=(HB, VM),
         scratch_shapes=[pltpu.SemaphoreType.DMA],
         compiler_params=ROOM,
         cost_estimate=work,
         name="store_step",
-    )(*near(plan))
-    mine, row_left = pl.pallas_call(
-        functools.partial(last_reduce_kernel, sizes),
-        out_shape=(give, one),
-        in_specs=[VM] * 3,
-        out_specs=(VM, VM),
-        compiler_params=ROOM,
-        name="last_reduce_step",
-    )(*near(got, row_got, stored))
-    theirs = swap(mine)
+    )(*near(plan, mine))
     row_dual, col_dual = pl.pallas_call(
         functools.partial(finish_kernel, sizes),
         out_shape=tuple(jax.ShapeDtypeStruct(s.shape, s.dtype) for s in (one, many)),
-        in_specs=[VM] * 6,
+        in_specs=[VM] * 7,
         out_specs=(VM, VM),
         compiler_params=ROOM,
         name="finish_step",
-    )(*near(mine, theirs, row_left, weight, row_dual, col_dual))
+    )(*near(mine, theirs, stored, row_left, weight, row_dual, col_dual))
     return (plan, row_dual.reshape(rows), col_dual.reshape(cols))
 
 

time: 93.9 us -> 92.5 us (0.985)
  waiting for transfers between devices: 1.82 us -> 0.67 us
    ppermute x5, waiting for transfers between devices: 1.81 us -> 0.66 us  [swap(): return lax.ppermute(array, CORE, [(0, 1), (1, 0)])]
    pallas_call x3 -> x4, Pallas kernels: 3.07 us -> 2.62 us  [keep_step(): pl.pallas_call(functools.partial(keep_kernel, sizes), out_shape=(big, kee...]
  transfers between devices with their start and end apart: 6 -> 6, of which waited for: 3 -> 4; matrix products, arithmetic and copies ran while one was open for 0% -> 0% of each run, Pallas kernels for 5% -> 4%
where the time goes in v6:
time: 92.5 us; the launch traced here: 92.1 us
  blocking collectives  71.9 us (78%)
  Pallas kernels  10.1 us (11%)
  starting transfers between devices  8.69 us (9%)
    all_to_all x6, blocking collectives, exchange(): return lax.all_to_all(array, axes, split_axis=0, concat_axis=0, tiled=True)  64.9 us
    all_gather x1, blocking collectives, shards(): row_got = lax.all_gather(row_sent[0], 'narrow')  6.96 us
    ppermute x5, starting transfers between devices, swap(): return lax.ppermute(array, CORE, [(0, 1), (1, 0)])  5.17 us
    all_to_all x1, starting transfers between devices, exchange(): return lax.all_to_all(array, axes, split_axis=0, concat_axis=0, tiled=True)  3.51 us
    pallas_call x4, Pallas kernels, keep_step(): pl.pallas_call(functools.partial(keep_kernel, sizes), out_shape=(big, kee...  2.62 us
    pallas_call x1, Pallas kernels, shards(): pl.pallas_call(functools.partial(open_kernel, sizes), out_shape=(big, big...  2.41 us
    pallas_call x3, Pallas kernels, shards(): pl.pallas_call(functools.partial(give_kernel, sizes), out_shape=(big, giv...  2.21 us
  transfers between devices with their start and end apart: 6, of which 4 were waited for; matrix products, arithmetic and copies ran while one was open for 0% of the time, Pallas kernels for 4%

profile of v6, /device:TPU:1, one launch (start us, length us, event | category | flops | bytes accessed | tf_op | source)
XLA Modules:
  0.0 92.1 jit_solution(3079344299367508956)
XLA Ops:
  0.6 2.4 %open_step.1 = (f32[128,4096]{1,0:T(8,128)S(1)}, f32[128,4096]{1,0:T(8,128)S(1)}, f32[1,128]{1,0:T(1,128)S(1)}, f32[1,4096]{1,0:T(1,128)S(1)}, f32[1,128]{1,0:T(...) custom-call(f32[128,4096]{1,0:T(8,128)} %refs_0_.1, ...), custom_call_target="tpu_custom_call" | custom-call | flops 3145728 | tf_op jit(solution)/shard_map/open_step/pallas_call | solution.py:331
  3.0 1.5 %collective-permute-start = (f32[1,2048]{1,0:T(1,128)S(1)}, f32[1,2048]{1,0:T(1,128)S(1)}, u32[]{:S(2)}, u32[]{:S(2)}) collective-permute-start(f32[1,2048]{1,0:T(1,128)S(1)} %get-tuple-element.65), channel_id=1, source_target_pairs={{0,4},{4,0},{1,5},{5,1},{2,6},{6,2},{3,7},{7,3},{8,12},{12,8},{9,1... | collective-permute-start | bytes 24584 | tf_op jit(solution)/shard_map/ppermute | solution.py:29
  4.5 0.7 keep_step.4
  5.2 0.2 collective-permute-done.came
  5.4 14.2 %all_to_all.35.got = f32[16,1,2304]{2,1,0:T(1,128)S(1)} all-to-all(f32[16,1,2304]{2,1,0:T(1,128)S(1)} %build_step.3), channel_id=1, replica_groups=mesh['wide_0'=4,'wide_1'=4,'wide_2'=2,'narrow'=4] {'wide_0','wide_1'}, dimensions={0} | all-to-all | bytes 294912 | tf_op jit(solution)/shard_map/all_to_all | solution.py:25
  19.6 11.3 %all_to_all.36.got = f32[8,1,4352]{2,1,0:T(1,128)S(1)} all-to-all(f32[8,1,4352]{2,1,0:T(1,128)S(1)} %reduce_step.3), channel_id=1, replica_groups=mesh['wide_0'=4,'wide_1'=4,'wide_2'=2,'narrow'=4] {'wide_2','narrow'}, dimensions={0} | all-to-all | bytes 278528 | tf_op jit(solution)/shard_map/all_to_all | solution.py:25
  30.9 0.7 give_step.3
  31.7 0.5 collective-permute-start.1
  32.1 0.7 keep_step.5
  32.8 0.2 collective-permute-done.1.came
  33.0 9.9 %all_to_all.37.got = f32[16,1,2304]{2,1,0:T(1,128)S(1)} all-to-all(f32[16,1,2304]{2,1,0:T(1,128)S(1)} %build_step.4), channel_id=1, replica_groups=mesh['wide_0'=4,'wide_1'=4,'wide_2'=2,'narrow'=4] {'wide_0','wide_1'}, dimensions={0} | all-to-all | bytes 294912 | tf_op jit(solution)/shard_map/all_to_all | solution.py:25
  42.9 9.8 %all_to_all.38.got = f32[8,1,4352]{2,1,0:T(1,128)S(1)} all-to-all(f32[8,1,4352]{2,1,0:T(1,128)S(1)} %reduce_step.4), channel_id=1, replica_groups=mesh['wide_0'=4,'wide_1'=4,'wide_2'=2,'narrow'=4] {'wide_2','narrow'}, dimensions={0} | all-to-all | bytes 278528 | tf_op jit(solution)/shard_map/all_to_all | solution.py:25
  52.7 0.7 give_step.4
  53.5 0.5 collective-permute-start.2
  53.9 0.7 keep_step.6
  54.6 0.2 collective-permute-done.2.came
  54.8 9.9 %all_to_all.39.got = f32[16,1,2304]{2,1,0:T(1,128)S(1)} all-to-all(f32[16,1,2304]{2,1,0:T(1,128)S(1)} %build_step.5), channel_id=1, replica_groups=mesh['wide_0'=4,'wide_1'=4,'wide_2'=2,'narrow'=4] {'wide_0','wide_1'}, dimensions={0} | all-to-all | bytes 294912 | tf_op jit(solution)/shard_map/all_to_all | solution.py:25
  64.7 9.8 %all_to_all.40.got = f32[8,1,4352]{2,1,0:T(1,128)S(1)} all-to-all(f32[8,1,4352]{2,1,0:T(1,128)S(1)} %reduce_step.5), channel_id=1, replica_groups=mesh['wide_0'=4,'wide_1'=4,'wide_2'=2,'narrow'=4] {'wide_2','narrow'}, dimensions={0} | all-to-all | bytes 278528 | tf_op jit(solution)/shard_map/all_to_all | solution.py:25
  74.5 0.7 give_step.5
  75.3 0.5 collective-permute-start.3
  75.7 0.7 keep_step.7
  76.4 0.2 collective-permute-done.3.came
  76.6 0.7 last_build_step.1
  77.2 3.5 %all-to-all-start.6 = ((f32[16,1,2048]{2,1,0:T(1,128)}), f32[16,1,2048]{2,1,0:T(1,128)S(1)}, u32[]{:S(2)}, u32[]{:S(2)}) async-start(f32[16,1,2048]{2,1,0:T(1,128)} %last_build_step.1), calls=%async_computation.6 | async-start | bytes 262144 | tf_op jit(solution)/shard_map/all_to_all | solution.py:25
  80.8 7.0 %all-gather.1.row_got = f32[4,1,128]{2,1,0:T(1,128)S(1)} all-gather(f32[1,1,128]{2,1,0:T(1,128)S(1)} %bitcast.7), channel_id=2, replica_groups=mesh['wide_0'=4,'wide_1'=4,'wide_2'=2,'narrow'=4] {'narrow'}, dimensions={0}, use_global_device_ids=true | all-gather | bytes 2560 | tf_op jit(solution)/shard_map/all_gather | solution.py:391
  87.7 0.0 all-to-all-done.6.got
  87.8 2.3 %collective-permute-start.4 = (f32[1,2048]{1,0:T(1,128)S(1)}, f32[1,2048]{1,0:T(1,128)S(1)}, u32[]{:S(2)}, u32[]{:S(2)}) collective-permute-start(f32[1,2048]{1,0:T(1,128)S(1)} %get-tuple-element.98.after.mine), channel_id=1, source_target_pairs={{0,4},{4,0},{1,5},{5,1},{2,6},{6,2},{3,7},{7,3},{8,12},{12,8},{9,1... | collective-permute-start | bytes 24584 | tf_op jit(solution)/shard_map/ppermute | solution.py:29
  90.0 1.3 %store_step.1 = (f32[128,4096]{1,0:T(8,128)}, f32[1,128]{1,0:T(1,128)S(1)}) custom-call(f32[128,4096]{1,0:T(8,128)S(1)} %get-tuple-element.94.plan, f32[1,2048]{1,0:T(1,128)S(1)} %get-tuple-element.98.after.mine), custom_call_target="tpu_custom_call" | custom-call | flops 3145728 | tf_op jit(solution)/shard_map/store_step/pallas_call | solution.py:401
  91.4 0.0 collective-permute-done.4.theirs
  91.4 0.7 finish_step.1
  (7 shorter events, 0.2 us)
Async XLA Ops:
  3.0 2.3 %collective-permute-start = (f32[1,2048]{1,0:T(1,128)S(1)}, f32[1,2048]{1,0:T(1,128)S(1)}, u32[]{:S(2)}, u32[]{:S(2)}) collective-permute-start(f32[1,2048]{1,0:T(1,128)S(1)} %get-tuple-element.65), channel_id=1, source_target_pairs={{0,4},{4,0},{1,5},{5,1},{2,6},{6,2},{3,7},{7,3},{8,12},{12,8},{9,1... | collective-permute-start | bytes 24584 | tf_op jit(solution)/shard_map/ppermute | solution.py:29
  31.7 1.3 %collective-permute-start.1 = (f32[1,2048]{1,0:T(1,128)S(1)}, f32[1,2048]{1,0:T(1,128)S(1)}, u32[]{:S(2)}, u32[]{:S(2)}) collective-permute-start(f32[1,2048]{1,0:T(1,128)S(1)} %get-tuple-element.75), channel_id=1, source_target_pairs={{0,4},{4,0},{1,5},{5,1},{2,6},{6,2},{3,7},{7,3},{8,12},{12,8},{9,1... | collective-permute-start | bytes 24584 | tf_op jit(solution)/shard_map/ppermute | solution.py:29
  53.5 1.3 %collective-permute-start.2 = (f32[1,2048]{1,0:T(1,128)S(1)}, f32[1,2048]{1,0:T(1,128)S(1)}, u32[]{:S(2)}, u32[]{:S(2)}) collective-permute-start(f32[1,2048]{1,0:T(1,128)S(1)} %get-tuple-element.85), channel_id=1, source_target_pairs={{0,4},{4,0},{1,5},{5,1},{2,6},{6,2},{3,7},{7,3},{8,12},{12,8},{9,1... | collective-permute-start | bytes 24584 | tf_op jit(solution)/shard_map/ppermute | solution.py:29
  75.3 1.3 %collective-permute-start.3 = (f32[1,2048]{1,0:T(1,128)S(1)}, f32[1,2048]{1,0:T(1,128)S(1)}, u32[]{:S(2)}, u32[]{:S(2)}) collective-permute-start(f32[1,2048]{1,0:T(1,128)S(1)} %get-tuple-element.96), channel_id=1, source_target_pairs={{0,4},{4,0},{1,5},{5,1},{2,6},{6,2},{3,7},{7,3},{8,12},{12,8},{9,1... | collective-permute-start | bytes 24584 | tf_op jit(solution)/shard_map/ppermute | solution.py:29
  77.2 10.5 %all-to-all-start.6 = ((f32[16,1,2048]{2,1,0:T(1,128)}), f32[16,1,2048]{2,1,0:T(1,128)S(1)}, u32[]{:S(2)}, u32[]{:S(2)}) async-start(f32[16,1,2048]{2,1,0:T(1,128)} %last_build_step.1), calls=%async_computation.6 | async-start | bytes 262144 | tf_op jit(solution)/shard_map/all_to_all | solution.py:25
  87.8 3.6 %collective-permute-start.4 = (f32[1,2048]{1,0:T(1,128)S(1)}, f32[1,2048]{1,0:T(1,128)S(1)}, u32[]{:S(2)}, u32[]{:S(2)}) collective-permute-start(f32[1,2048]{1,0:T(1,128)S(1)} %get-tuple-element.98.after.mine), channel_id=1, source_target_pairs={{0,4},{4,0},{1,5},{5,1},{2,6},{6,2},{3,7},{7,3},{8,12},{12,8},{9,1... | collective-permute-start | bytes 24584 | tf_op jit(solution)/shard_map/ppermute | solution.py:29

commit v7 on v6

--- a/solution.py
+++ b/solution.py
@@ -8,6 +8,7 @@
 from jax.experimental.pallas import tpu as pltpu
 from jax.sharding import Mesh
 from jax.sharding import PartitionSpec as P
+
 
 ITERS = 4
 LANES = 128
@@ -45,35 +46,39 @@
     return slice(n * LANES, (n + size) * LANES)
 
 
-def dual_update(
-    got, weight, row_dual, col_dual, new_weight, new_row, new_col, rows_held, sizes
-):
-    narrow, base, half, chips = sizes
+def collect_kernel(sizes, got, weight, row_dual, new_weight, new_row, row_all, rows_held):
+    narrow, base, _, chips = sizes
     core = lax.axis_index(CORE)
     place = lax.axis_index("wide_0") * lax.axis_size("wide_1") + lax.axis_index("wide_1")
     squares, rest = None, None
     for c in range(2):
-        rows, other = got[c * narrow, :, tile_of(half, chips)], got[c * narrow, :, tile_of(half + chips, 2)]
+        part = got[c * narrow]
         for n in range(c * narrow + 1, (c + 1) * narrow):
-            rows = rows + got[n, :, tile_of(half, chips)]
-            other = other + got[n, :, tile_of(half + chips, 2)]
+            part = part + got[n]
+        rows, other = part[:, tile_of(0, chips)], part[:, tile_of(chips, 2)]
         rows_held[c] = rows
         squares = rows * rows if squares is None else squares + rows * rows
         rest = other if rest is None else rest + other
-    left_square = total(squares) + total(rest[:, tile_of(0)])
-    moved = total(rest[:, tile_of(1)])
+    lanes = rest[:, tile_of(0)]
+    for p in range(chips):
+        lanes = lanes + squares[:, tile_of(p)]
+    left_square, moved = total(lanes), total(rest[:, tile_of(1)])
     old = weight[...]
     dual_step = base * old
     dual_moved = dual_step * dual_step * left_square
-    fresh_weight = jnp.sqrt(old * jnp.sqrt((dual_moved + 1.0) / (moved + 1.0)))
-    new_weight[...] = fresh_weight
-    new_row[...] = row_dual[...] + dual_step[0:1, :] * rows_held[core, :, span(place, 1)]
-    scale = jnp.broadcast_to(dual_step[0:1, 0:1], (1, half * LANES))
-    column = lax.axis_index("narrow")
-    for c in range(2):
-        lanes = tile_of(c * half, half)
-        new_col[:, lanes] = col_dual[:, lanes] + scale * got[c * narrow + column, :, tile_of(0, half)]
-    return base / fresh_weight
+    new_weight[...] = jnp.sqrt(old * jnp.sqrt((dual_moved + 1.0) / (moved + 1.0)))
+    row = row_dual[...] + dual_step[0:1, :] * rows_held[core, :, span(place, 1)]
+    new_row[...] = row
+    spread_rows(row, row_all)
+
+
+def col_update(mine, theirs, weight, col_dual, new_col, sizes):
+    base, half = sizes[1], sizes[2]
+    core = lax.axis_index(CORE)
+    scale = jnp.broadcast_to((base * weight[...])[0:1, 0:1], (1, half * LANES))
+    for side, part in ((core, mine), (1 - core, theirs)):
+        lanes = span(side * half, half)
+        new_col[:, lanes] = col_dual[:, lanes] + scale * part[...]
 
 
 def sweep(step, cost, plan, fresh_plan, row_all, col_dual, tiles, state, done):
@@ -135,10 +140,10 @@
 
 
 def open_kernel(sizes, *refs):
-    narrow, base, half, chips = sizes
+    _, base, half, chips = sizes
     sources, targets = refs[:6], refs[6:12]
     fresh_plan, give, row_sums, moved_sums, row_all, weight, sems = refs[12:]
-    cost, plan, row_mass, col_mass, row_dual, col_dual = targets
+    cost, plan, _, col_mass, row_dual, col_dual = targets
     core = lax.axis_index(CORE)
     tiles = half // CHUNKS
     weight[...] = jnp.full((GROUP, LANES), base, jnp.float32)
@@ -181,28 +186,31 @@
 
 
 def give_kernel(
-    sizes, got, weight, cost, plan, col_mass, row_dual, col_dual,
-    fresh_plan, give, row_sums, moved_sums, row_all, new_weight, new_row, new_col, rows_held,
+    sizes, mine, theirs, weight, new_weight, cost, plan, col_mass, row_all, col_dual,
+    fresh_plan, give, row_sums, moved_sums, new_col,
 ):
-    _, _, half, chips = sizes
-    step = dual_update(
-        got, weight, row_dual, col_dual, new_weight, new_row, new_col, rows_held, sizes
-    )
-    spread_rows(new_row[...], row_all)
+    _, base, half, chips = sizes
+    col_update(mine, theirs, weight, col_dual, new_col, sizes)
     side = 1 - lax.axis_index(CORE)
     state = sweep(
-        step, cost, plan, fresh_plan, row_all, new_col, (side * half, half), zeros(row_all),
-        into(give, col_mass, 2 * chips),
+        base / new_weight[...], cost, plan, fresh_plan, row_all, new_col, (side * half, half),
+        zeros(row_all), into(give, col_mass, 2 * chips),
     )
     hold(state, row_sums, moved_sums)
 
 
 def keep_kernel(
     sizes, weight, cost, plan, half_plan, row_mass, col_mass, row_all, col_dual, row_sums,
-    moved_sums, fresh_plan, keep, *row_share,
+    moved_sums, fresh_plan, keep, *last,
 ):
     _, base, half, chips = sizes
     side = lax.axis_index(CORE)
+    copy = None
+    if last:
+        row_share, plan_out, sem = last
+        lanes = span((1 - side) * half, half)
+        copy = pltpu.make_async_copy(fresh_plan.at[:, lanes], plan_out.at[:, lanes], sem)
+        copy.start()
     rows = row_sums[...]
     groups = row_all.shape[0] // GROUP
     state = tuple(rows[g * GROUP : (g + 1) * GROUP] for g in range(groups)), tuple(
@@ -213,8 +221,9 @@
         into(keep, col_mass, 2 * chips),
     )
     tail(keep, row_mass, state, sizes)
-    for share in row_share:
-        share[...] = keep[:, tile_of(half)]
+    if last:
+        row_share[...] = keep[:, tile_of(half)]
+        copy.wait()
 
 
 def build_kernel(sizes, keep, came, sent):
@@ -226,22 +235,22 @@
         sent[p, :, tile_of(half, 2)] = rest
 
 
-def reduce_kernel(sizes, got, sent):
-    narrow, base, half, chips = sizes
+def reduce_kernel(sizes, got, mine, sent):
+    _, _, half, chips = sizes
     cols = got[0]
     for p in range(1, chips):
         cols = cols + got[p]
     moved = cols[:, tile_of(half + 1)]
     cols = cols[:, tile_of(0, half)]
-    sent[0, :, tile_of(0, half)] = cols
+    mine[...] = cols
     cols = cols * cols
     squares = cols[:, tile_of(0)]
     for r in range(1, half):
         squares = squares + cols[:, tile_of(r)]
     for p in range(chips):
-        sent[0, :, tile_of(half + p)] = got[p, :, tile_of(half)]
-    sent[0, :, tile_of(half + chips)] = squares
-    sent[0, :, tile_of(half + chips + 1)] = moved
+        sent[0, :, tile_of(p)] = got[p, :, tile_of(half)]
+    sent[0, :, tile_of(chips)] = squares
+    sent[0, :, tile_of(chips + 1)] = moved
     everything = sent[0]
     for q in range(1, sent.shape[0]):
         sent[q] = everything
@@ -253,14 +262,16 @@
         sent[p] = cols
 
 
-def store_kernel(plan, after, plan_out, stored, sem):
-    copy = pltpu.make_async_copy(plan, plan_out, sem)
+def store_kernel(sizes, plan, after, plan_part, plan_out, stored, sem):
+    half = sizes[2]
+    lanes = span(lax.axis_index(CORE) * half, half)
+    copy = pltpu.make_async_copy(plan.at[:, lanes], plan_out.at[:, lanes], sem)
     copy.start()
     stored[...] = after[:, tile_of(0)]
     copy.wait()
 
 
-def last_reduce_kernel(sizes, got, row_got, mine, row_left):
+def last_reduce_kernel(got, row_got, mine, row_left):
     cols = got[0]
     for p in range(1, got.shape[0]):
         cols = cols + got[p]
@@ -274,14 +285,8 @@
 def finish_kernel(
     sizes, mine, theirs, stored, row_left, weight, row_dual, col_dual, row_out, col_out
 ):
-    _, base, half, _ = sizes
-    core = lax.axis_index(CORE)
-    step = base * weight[0:1, :]
-    row_out[...] = row_dual[...] + step * row_left[...]
-    scale = jnp.broadcast_to(step[:, 0:1], (1, half * LANES))
-    for side, part in ((core, mine), (1 - core, theirs)):
-        lanes = span(side * half, half)
-        col_out[:, lanes] = col_dual[:, lanes] + scale * part[...]
+    row_out[...] = row_dual[...] + sizes[1] * weight[0:1, :] * row_left[...]
+    col_update(mine, theirs, weight, col_dual, col_out, sizes)
 
 
 VM = pl.BlockSpec(memory_space=pltpu.VMEM)
@@ -304,9 +309,6 @@
     def vm(*shape):
         return pltpu.VMEM(shape, jnp.float32)
 
-    def near(*arrays):
-        return [pltpu.with_memory_space_constraint(array, pltpu.VMEM) for array in arrays]
-
     big, state, one, many = vm(rows, cols), vm(GROUP, LANES), vm(1, rows), vm(1, cols)
     give, keep = vm(1, half * LANES), vm(1, (half + 2) * LANES)
     spread = vm(rows, LANES)
@@ -314,18 +316,32 @@
     work = pl.CostEstimate(flops=6 * rows * cols, bytes_accessed=0, transcendentals=0)
     sums = vm(MOVED, GROUP, LANES)
 
+    whole = jax.ShapeDtypeStruct((rows, cols), jnp.float32)
+
+    def call(kernel, out_shape, *operands, **options):
+        place = pltpu.VMEM
+        single = not isinstance(out_shape, tuple)
+        specs = tuple(HB if o is whole else VM for o in ((out_shape,) if single else out_shape))
+        held = options.pop("held", ())
+        return pl.pallas_call(
+            kernel,
+            out_shape=out_shape,
+            in_specs=[HB if o in held else VM for o in range(len(operands))],
+            out_specs=specs[0] if single else specs,
+            compiler_params=ROOM,
+            **options,
+        )(*(
+            pltpu.with_memory_space_constraint(o, pltpu.HBM if n in held else place)
+            for n, o in enumerate(operands)
+        ))
+
     def keep_step(last, *operands):
-        share = (one,) if last else ()
-        return pl.pallas_call(
-            functools.partial(keep_kernel, sizes),
-            out_shape=(big, keep) + share,
-            in_specs=[VM] * 10,
-            out_specs=(VM,) * (2 + len(share)),
-            input_output_aliases={3: 0},
-            compiler_params=ROOM,
-            cost_estimate=work,
-            name="keep_step",
-        )(*near(*operands))
+        extra = (one, whole) if last else ()
+        return call(
+            functools.partial(keep_kernel, sizes), (big, keep) + extra, *operands,
+            input_output_aliases={3: 0}, cost_estimate=work,
+            scratch_shapes=[pltpu.SemaphoreType.DMA] if last else [],
+        )
 
     inputs = (cost, plan, row_mass, col_mass, row_dual, col_dual)
     outputs = pl.pallas_call(
@@ -344,79 +360,49 @@
         False, weight, cost, plan, half_plan, row_mass, col_mass, row_all, col_dual, row_sums,
         moved_sums,
     )
+    own = functools.partial
     for step in range(1, ITERS):
         came = swap(given)
-        sent = pl.pallas_call(
-            functools.partial(build_kernel, sizes),
-            out_shape=vm(chips, 1, (half + 2) * LANES),
-            in_specs=[VM] * 2,
-            out_specs=VM,
-            compiler_params=ROOM,
-            name="build_step",
-        )(*near(kept, came))
+        sent = call(own(build_kernel, sizes), vm(chips, 1, (half + 2) * LANES), kept, came)
         got = exchange(sent, PLANE)
-        sent = pl.pallas_call(
-            functools.partial(reduce_kernel, sizes),
-            out_shape=vm(2 * narrow, 1, (half + chips + 2) * LANES),
-            in_specs=[VM],
-            out_specs=VM,
-            compiler_params=ROOM,
-            name="reduce_step",
-        )(*near(got))
+        mine, sent = call(
+            own(reduce_kernel, sizes),
+            (give, vm(2 * narrow, 1, (chips + 2) * LANES)), got,
+        )
+        theirs = swap(mine)
         got = exchange(sent, COLUMN)
-        half_plan, given, row_sums, moved_sums, row_all, weight, row_dual, col_dual = pl.pallas_call(
-            functools.partial(give_kernel, sizes),
-            out_shape=(big, give, spread, sums, spread, state, one, many),
-            in_specs=[VM] * 7,
-            out_specs=(VM,) * 8,
-            scratch_shapes=[vm(2, 1, chips * LANES)],
-            compiler_params=ROOM,
+        new_weight, row_dual, row_all = call(
+            own(collect_kernel, sizes), (state, one, spread),
+            got, weight, row_dual, scratch_shapes=[vm(2, 1, chips * LANES)],
+        )
+        half_plan, given, row_sums, moved_sums, col_dual = call(
+            own(give_kernel, sizes), (big, give, spread, sums, many),
+            mine, theirs, weight, new_weight, cost, plan, col_mass, row_all, col_dual,
             cost_estimate=work,
-            name="give_step",
-        )(*near(got, weight, cost, plan, col_mass, row_dual, col_dual))
-        plan, kept, *row_sent = keep_step(
+        )
+        weight = new_weight
+        plan, kept, *tail_parts = keep_step(
             step == ITERS - 1, weight, cost, plan, half_plan, row_mass, col_mass, row_all,
             col_dual, row_sums, moved_sums,
         )
+    row_sent, plan_part = tail_parts
     came = swap(given)
-    sent = pl.pallas_call(
-        functools.partial(last_build_kernel, sizes),
-        out_shape=vm(chips, 1, half * LANES),
-        in_specs=[VM] * 2,
-        out_specs=VM,
-        compiler_params=ROOM,
-        name="last_build_step",
-    )(*near(kept, came))
+    sent = call(own(last_build_kernel, sizes), vm(chips, 1, half * LANES), kept, came)
     got = exchange(sent, PLANE)
-    row_got = lax.all_gather(row_sent[0], "narrow")
-    mine, row_left = pl.pallas_call(
-        functools.partial(last_reduce_kernel, sizes),
-        out_shape=(give, one),
-        in_specs=[VM] * 2,
-        out_specs=(VM, VM),
-        compiler_params=ROOM,
-        name="last_reduce_step",
-    )(*near(got, row_got))
+    row_got = lax.all_gather(row_sent, "narrow")
+    mine, row_left = call(last_reduce_kernel, (give, one), got, row_got)
     theirs = swap(mine)
-    plan, stored = pl.pallas_call(
-        store_kernel,
-        out_shape=(jax.ShapeDtypeStruct((rows, cols), jnp.float32), one),
-        in_specs=[VM] * 2,
-        out_specs=(HB, VM),
-        scratch_shapes=[pltpu.SemaphoreType.DMA],
-        compiler_params=ROOM,
+    plan, stored = call(
+        own(store_kernel, sizes), (whole, one), plan, mine, plan_part,
+        held=(2,), input_output_aliases={2: 0}, scratch_shapes=[pltpu.SemaphoreType.DMA],
         cost_estimate=work,
-        name="store_step",
-    )(*near(plan, mine))
-    row_dual, col_dual = pl.pallas_call(
-        functools.partial(finish_kernel, sizes),
-        out_shape=tuple(jax.ShapeDtypeStruct(s.shape, s.dtype) for s in (one, many)),
-        in_specs=[VM] * 7,
-        out_specs=(VM, VM),
-        compiler_params=ROOM,
-        name="finish_step",
-    )(*near(mine, theirs, stored, row_left, weight, row_dual, col_dual))
-    return (plan, row_dual.reshape(rows), col_dual.reshape(cols))
+    )
+    row_out, col_out = call(
+        own(finish_kernel, sizes),
+        tuple(jax.ShapeDtypeStruct(o.shape, o.dtype) for o in (one, many)),
+        mine, theirs, stored, row_left, weight, row_dual, col_dual,
+    )
+    return (plan, row_out.reshape(rows), col_out.reshape(cols))
 
 
 def solution(mesh):

time: 92.5 us -> 105 us (1.14)
  blocking collectives: 71.9 us -> 41 us
  starting transfers between devices: 8.69 us -> 24 us
  waiting for transfers between devices: 0.67 us -> 14.6 us
  local copies, waits for them, and re-layouts: 0 us -> 11.7 us
  Pallas kernels: 10.1 us -> 12.1 us
    all_to_all x6 -> x3, blocking collectives: 64.9 us -> 34 us  [exchange(): return lax.all_to_all(array, axes, split_axis=0, concat_axis=0, tiled=True)]
    all_to_all x1 -> x4, starting transfers between devices: 3.51 us -> 19.2 us  [exchange(): return lax.all_to_all(array, axes, split_axis=0, concat_axis=0, tiled=True)]
    all_to_all x1 -> x4, waiting for transfers between devices: 0.01 us -> 14.6 us  [exchange(): return lax.all_to_all(array, axes, split_axis=0, concat_axis=0, tiled=True)]
    unnamed x0 -> x16, local copies, waits for them, and re-layouts: none -> 11.7 us
    pallas_call x17 -> x20, Pallas kernels: 7.72 us -> 9.71 us  [call(): pl.pallas_call(kernel, out_shape=out_shape, in_specs=[HB if o in held els...]
    ppermute x5 -> x8, starting transfers between devices: 5.17 us -> 4.76 us  [swap(): return lax.ppermute(array, CORE, [(0, 1), (1, 0)])]
  transfers between devices with their start and end apart: 6 -> 12, of which waited for: 4 -> 3; matrix products, arithmetic and copies ran while one was open for 0% -> 0% of each run, Pallas kernels for 4% -> 4%
where the time goes in v7:
time: 105 us; the launch traced here: 104 us
  blocking collectives  41 us (39%)
  starting transfers between devices  24 us (23%)
  waiting for transfers between devices  14.6 us (14%)
  Pallas kernels  12.1 us (12%)
  local copies, waits for them, and re-layouts  11.7 us (11%)
    all_to_all x3, blocking collectives, exchange(): return lax.all_to_all(array, axes, split_axis=0, concat_axis=0, tiled=True)  34 us
    all_to_all x4, starting transfers between devices, exchange(): return lax.all_to_all(array, axes, split_axis=0, concat_axis=0, tiled=True)  19.2 us
    all_to_all x4, waiting for transfers between devices, exchange(): return lax.all_to_all(array, axes, split_axis=0, concat_axis=0, tiled=True)  14.6 us
    unnamed x16, local copies, waits for them, and re-layouts  11.7 us
    pallas_call x20, Pallas kernels, call(): pl.pallas_call(kernel, out_shape=out_shape, in_specs=[HB if o in held els...  9.71 us
    all_gather x1, blocking collectives, shards(): row_got = lax.all_gather(row_sent, 'narrow')  6.99 us
    ppermute x8, starting transfers between devices, swap(): return lax.ppermute(array, CORE, [(0, 1), (1, 0)])  4.76 us
    pallas_call x1, Pallas kernels, shards(): pl.pallas_call(functools.partial(open_kernel, sizes), out_shape=(big, big...  2.41 us
  transfers between devices with their start and end apart: 12, of which 3 were waited for; matrix products, arithmetic and copies ran while one was open for 0% of the time, Pallas kernels for 4%

profile of v7, /device:TPU:1, one launch (start us, length us, event | category | flops | bytes accessed | tf_op | source)
XLA Modules:
  0.0 104.2 jit_solution(3479698087183806743)
XLA Ops:
  0.6 2.4 %open_step.1 = (f32[128,4096]{1,0:T(8,128)S(1)}, f32[128,4096]{1,0:T(8,128)S(1)}, f32[1,128]{1,0:T(1,128)S(1)}, f32[1,4096]{1,0:T(1,128)S(1)}, f32[1,128]{1,0:T(...) custom-call(f32[128,4096]{1,0:T(8,128)} %refs_0_.1, ...), custom_call_target="tpu_custom_call" | custom-call | flops 3145728 | tf_op jit(solution)/shard_map/open_step/pallas_call | solution.py:347
  3.0 1.5 %collective-permute-start = (f32[1,2048]{1,0:T(1,128)S(1)}, f32[1,2048]{1,0:T(1,128)S(1)}, u32[]{:S(2)}, u32[]{:S(2)}) collective-permute-start(f32[1,2048]{1,0:T(1,128)S(1)} %get-tuple-element.72), channel_id=1, source_target_pairs={{0,4},{4,0},{1,5},{5,1},{2,6},{6,2},{3,7},{7,3},{8,12},{12,8},{9,1... | collective-permute-start | bytes 24584 | tf_op jit(solution)/shard_map/ppermute | solution.py:30
  4.5 0.7 shard_map.85
  5.2 0.0 copy-start
  5.2 1.3 %copy-done = f32[128,4096]{1,0:T(8,128)} copy-done((f32[128,4096]{1,0:T(8,128)}, f32[128,4096]{1,0:T(8,128)S(1)}, u32[]{:S(2)}) %copy-start) | copy-done | bytes 2097176
  6.5 14.4 %all_to_all.35.got = f32[16,1,2304]{2,1,0:T(1,128)S(1)} all-to-all(f32[16,1,2304]{2,1,0:T(1,128)S(1)} %shard_map.86), channel_id=1, replica_groups=mesh['wide_0'=4,'wide_1'=4,'wide_2'=2,'narrow'=4] {'wide_0','wide_1'}, dimensions={0} | all-to-all | bytes 294912 | tf_op jit(solution)/shard_map/all_to_all | solution.py:26
  20.9 0.7 shard_map.87
  21.6 6.0 %all-to-all-start.1 = ((f32[8,1,2304]{2,1,0:T(1,128)}), f32[8,1,2304]{2,1,0:T(1,128)S(1)}, u32[]{:S(2)}, u32[]{:S(2)}) async-start(f32[8,1,2304]{2,1,0:T(1,128)} %get-tuple-element.73), calls=%async_computation.1 | async-start | bytes 147456 | tf_op jit(solution)/shard_map/all_to_all | solution.py:26
  27.6 5.0 %all-to-all-done.1.got = f32[8,1,2304]{2,1,0:T(1,128)S(1)} async-done(((f32[8,1,2304]{2,1,0:T(1,128)}), f32[8,1,2304]{2,1,0:T(1,128)S(1)}, u32[]{:S(2)}, u32[]{:S(2)}) %all-to-all-start.1) | async-done | bytes 73760 | tf_op jit(solution)/shard_map/all_to_all | solution.py:26
  32.5 0.1 shard_map.88
  32.7 0.0 copy-start.1
  32.7 1.6 %copy-done.1 = f32[128,4096]{1,0:T(8,128)S(1)} copy-done((f32[128,4096]{1,0:T(8,128)S(1)}, f32[128,4096]{1,0:T(8,128)}, u32[]{:S(2)}) %copy-start.1) | copy-done | bytes 2097176
  34.3 0.7 shard_map.89
  34.9 0.5 collective-permute-start.2
  35.4 0.7 shard_map.90
  36.1 0.0 copy-start.2
  36.1 1.3 %copy-done.2 = f32[128,4096]{1,0:T(8,128)} copy-done((f32[128,4096]{1,0:T(8,128)}, f32[128,4096]{1,0:T(8,128)S(1)}, u32[]{:S(2)}) %copy-start.2) | copy-done | bytes 2097176
  37.4 9.8 %all_to_all.36.got = f32[16,1,2304]{2,1,0:T(1,128)S(1)} all-to-all(f32[16,1,2304]{2,1,0:T(1,128)S(1)} %shard_map.91), channel_id=1, replica_groups=mesh['wide_0'=4,'wide_1'=4,'wide_2'=2,'narrow'=4] {'wide_0','wide_1'}, dimensions={0} | all-to-all | bytes 294912 | tf_op jit(solution)/shard_map/all_to_all | solution.py:26
  47.2 0.7 shard_map.92
  47.9 4.9 %all-to-all-start.3 = ((f32[8,1,2304]{2,1,0:T(1,128)}), f32[8,1,2304]{2,1,0:T(1,128)S(1)}, u32[]{:S(2)}, u32[]{:S(2)}) async-start(f32[8,1,2304]{2,1,0:T(1,128)} %get-tuple-element.85), calls=%async_computation.3 | async-start | bytes 147456 | tf_op jit(solution)/shard_map/all_to_all | solution.py:26
  52.8 0.2 collective-permute-start.3
  52.9 4.8 %all-to-all-done.3.got = f32[8,1,2304]{2,1,0:T(1,128)S(1)} async-done(((f32[8,1,2304]{2,1,0:T(1,128)}), f32[8,1,2304]{2,1,0:T(1,128)S(1)}, u32[]{:S(2)}, u32[]{:S(2)}) %all-to-all-start.3) | async-done | bytes 73760 | tf_op jit(solution)/shard_map/all_to_all | solution.py:26
  57.7 0.1 shard_map.93
  57.9 0.0 copy-start.3
  57.9 1.6 %copy-done.3 = f32[128,4096]{1,0:T(8,128)S(1)} copy-done((f32[128,4096]{1,0:T(8,128)S(1)}, f32[128,4096]{1,0:T(8,128)}, u32[]{:S(2)}) %copy-start.3) | copy-done | bytes 2097176
  59.5 0.7 shard_map.94
  60.1 0.5 collective-permute-start.4
  60.6 0.7 shard_map.95
  61.3 0.0 copy-start.4
  61.3 1.3 %copy-done.4 = f32[128,4096]{1,0:T(8,128)} copy-done((f32[128,4096]{1,0:T(8,128)}, f32[128,4096]{1,0:T(8,128)S(1)}, u32[]{:S(2)}) %copy-start.4) | copy-done | bytes 2097176
  62.6 9.8 %all_to_all.37.got = f32[16,1,2304]{2,1,0:T(1,128)S(1)} all-to-all(f32[16,1,2304]{2,1,0:T(1,128)S(1)} %shard_map.96), channel_id=1, replica_groups=mesh['wide_0'=4,'wide_1'=4,'wide_2'=2,'narrow'=4] {'wide_0','wide_1'}, dimensions={0} | all-to-all | bytes 294912 | tf_op jit(solution)/shard_map/all_to_all | solution.py:26
  72.5 0.7 shard_map.97
  73.2 4.9 %all-to-all-start.5 = ((f32[8,1,2304]{2,1,0:T(1,128)}), f32[8,1,2304]{2,1,0:T(1,128)S(1)}, u32[]{:S(2)}, u32[]{:S(2)}) async-start(f32[8,1,2304]{2,1,0:T(1,128)} %get-tuple-element.97), calls=%async_computation.5 | async-start | bytes 147456 | tf_op jit(solution)/shard_map/all_to_all | solution.py:26
  78.0 0.2 collective-permute-start.5
  78.2 4.8 %all-to-all-done.5.got = f32[8,1,2304]{2,1,0:T(1,128)S(1)} async-done(((f32[8,1,2304]{2,1,0:T(1,128)}), f32[8,1,2304]{2,1,0:T(1,128)S(1)}, u32[]{:S(2)}, u32[]{:S(2)}) %all-to-all-start.5) | async-done | bytes 73760 | tf_op jit(solution)/shard_map/all_to_all | solution.py:26
  83.0 0.1 shard_map.98
  83.1 1.6 %copy-done.5 = f32[128,4096]{1,0:T(8,128)S(1)} copy-done((f32[128,4096]{1,0:T(8,128)S(1)}, f32[128,4096]{1,0:T(8,128)}, u32[]{:S(2)}) %copy-start.5) | copy-done | bytes 2097176
  84.7 0.7 shard_map.99
  85.4 0.5 collective-permute-start.6
  85.8 1.0 shard_map.100
  86.9 1.3 %copy-done.6 = f32[128,4096]{1,0:T(8,128)} copy-done((f32[128,4096]{1,0:T(8,128)}, f32[128,4096]{1,0:T(8,128)S(1)}, u32[]{:S(2)}) %copy-start.6) | copy-done | bytes 2097176
  88.2 0.7 shard_map.101
  88.9 3.5 %all-to-all-start.6 = ((f32[16,1,2048]{2,1,0:T(1,128)}), f32[16,1,2048]{2,1,0:T(1,128)S(1)}, u32[]{:S(2)}, u32[]{:S(2)}) async-start(f32[16,1,2048]{2,1,0:T(1,128)} %shard_map.101), calls=%async_computation.6 | async-start | bytes 262144 | tf_op jit(solution)/shard_map/all_to_all | solution.py:26
  92.4 7.0 %all-gather.1.row_got = f32[4,1,128]{2,1,0:T(1,128)S(1)} all-gather(f32[1,1,128]{2,1,0:T(1,128)S(1)} %bitcast.7), channel_id=2, replica_groups=mesh['wide_0'=4,'wide_1'=4,'wide_2'=2,'narrow'=4] {'narrow'}, dimensions={0}, use_global_device_ids=true | all-gather | bytes 2560 | tf_op jit(solution)/shard_map/all_gather | solution.py:392
  99.4 1.5 %collective-permute-start.7 = (f32[1,2048]{1,0:T(1,128)S(1)}, f32[1,2048]{1,0:T(1,128)S(1)}, u32[]{:S(2)}, u32[]{:S(2)}) collective-permute-start(f32[1,2048]{1,0:T(1,128)S(1)} %get-tuple-element.111.after.mine), channel_id=1, source_target_pairs={{0,4},{4,0},{1,5},{5,1},{2,6},{6,2},{3,7},{7,3},{8,12},{12,8},{9,1... | collective-permute-start | bytes 24584 | tf_op jit(solution)/shard_map/ppermute | solution.py:30
  100.9 1.6 %copy-done.7 = f32[128,4096]{1,0:T(8,128)S(1)} copy-done((f32[128,4096]{1,0:T(8,128)S(1)}, f32[128,4096]{1,0:T(8,128)}, u32[]{:S(2)}) %copy-start.7) | copy-done | bytes 2097176
  102.5 1.0 shard_map.103
  103.5 0.7 shard_map.104
  (17 shorter events, 0.1 us)
Async XLA Ops:
  3.0 3.5 %collective-permute-start = (f32[1,2048]{1,0:T(1,128)S(1)}, f32[1,2048]{1,0:T(1,128)S(1)}, u32[]{:S(2)}, u32[]{:S(2)}) collective-permute-start(f32[1,2048]{1,0:T(1,128)S(1)} %get-tuple-element.72), channel_id=1, source_target_pairs={{0,4},{4,0},{1,5},{5,1},{2,6},{6,2},{3,7},{7,3},{8,12},{12,8},{9,1... | collective-permute-start | bytes 24584 | tf_op jit(solution)/shard_map/ppermute | solution.py:30
  5.2 1.3 %copy-start = (f32[128,4096]{1,0:T(8,128)}, f32[128,4096]{1,0:T(8,128)S(1)}, u32[]{:S(2)}) copy-start(f32[128,4096]{1,0:T(8,128)S(1)} %get-tuple-element.76.plan) | copy-start | bytes 6291460
  21.6 11.0 %all-to-all-start.1 = ((f32[8,1,2304]{2,1,0:T(1,128)}), f32[8,1,2304]{2,1,0:T(1,128)S(1)}, u32[]{:S(2)}, u32[]{:S(2)}) async-start(f32[8,1,2304]{2,1,0:T(1,128)} %get-tuple-element.73), calls=%async_computation.1 | async-start | bytes 147456 | tf_op jit(solution)/shard_map/all_to_all | solution.py:26
  27.6 5.1 %collective-permute-start.1 = (f32[1,2048]{1,0:T(1,128)S(1)}, f32[1,2048]{1,0:T(1,128)S(1)}, u32[]{:S(2)}, u32[]{:S(2)}) collective-permute-start(f32[1,2048]{1,0:T(1,128)S(1)} %get-tuple-element.77.mine), channel_id=1, source_target_pairs={{0,4},{4,0},{1,5},{5,1},{2,6},{6,2},{3,7},{7,3},{8,12},{12,8},{9,1... | collective-permute-start | bytes 24584 | tf_op jit(solution)/shard_map/ppermute | solution.py:30
  32.7 1.6 %copy-start.1 = (f32[128,4096]{1,0:T(8,128)S(1)}, f32[128,4096]{1,0:T(8,128)}, u32[]{:S(2)}) copy-start(f32[128,4096]{1,0:T(8,128)} %copy-done) | copy-start | bytes 6291460
  34.9 2.5 %collective-permute-start.2 = (f32[1,2048]{1,0:T(1,128)S(1)}, f32[1,2048]{1,0:T(1,128)S(1)}, u32[]{:S(2)}, u32[]{:S(2)}) collective-permute-start(f32[1,2048]{1,0:T(1,128)S(1)} %get-tuple-element.84), channel_id=1, source_target_pairs={{0,4},{4,0},{1,5},{5,1},{2,6},{6,2},{3,7},{7,3},{8,12},{12,8},{9,1... | collective-permute-start | bytes 24584 | tf_op jit(solution)/shard_map/ppermute | solution.py:30
  36.1 1.3 %copy-start.2 = (f32[128,4096]{1,0:T(8,128)}, f32[128,4096]{1,0:T(8,128)S(1)}, u32[]{:S(2)}) copy-start(f32[128,4096]{1,0:T(8,128)S(1)} %get-tuple-element.88.plan) | copy-start | bytes 6291460
  47.9 9.8 %all-to-all-start.3 = ((f32[8,1,2304]{2,1,0:T(1,128)}), f32[8,1,2304]{2,1,0:T(1,128)S(1)}, u32[]{:S(2)}, u32[]{:S(2)}) async-start(f32[8,1,2304]{2,1,0:T(1,128)} %get-tuple-element.85), calls=%async_computation.3 | async-start | bytes 147456 | tf_op jit(solution)/shard_map/all_to_all | solution.py:26
  52.8 5.1 %collective-permute-start.3 = (f32[1,2048]{1,0:T(1,128)S(1)}, f32[1,2048]{1,0:T(1,128)S(1)}, u32[]{:S(2)}, u32[]{:S(2)}) collective-permute-start(f32[1,2048]{1,0:T(1,128)S(1)} %get-tuple-element.89.mine), channel_id=1, source_target_pairs={{0,4},{4,0},{1,5},{5,1},{2,6},{6,2},{3,7},{7,3},{8,12},{12,8},{9,1... | collective-permute-start | bytes 24584 | tf_op jit(solution)/shard_map/ppermute | solution.py:30
  57.9 1.6 %copy-start.3 = (f32[128,4096]{1,0:T(8,128)S(1)}, f32[128,4096]{1,0:T(8,128)}, u32[]{:S(2)}) copy-start(f32[128,4096]{1,0:T(8,128)} %copy-done.2) | copy-start | bytes 6291460
  60.1 2.5 %collective-permute-start.4 = (f32[1,2048]{1,0:T(1,128)S(1)}, f32[1,2048]{1,0:T(1,128)S(1)}, u32[]{:S(2)}, u32[]{:S(2)}) collective-permute-start(f32[1,2048]{1,0:T(1,128)S(1)} %get-tuple-element.96), channel_id=1, source_target_pairs={{0,4},{4,0},{1,5},{5,1},{2,6},{6,2},{3,7},{7,3},{8,12},{12,8},{9,1... | collective-permute-start | bytes 24584 | tf_op jit(solution)/shard_map/ppermute | solution.py:30
  61.3 1.3 %copy-start.4 = (f32[128,4096]{1,0:T(8,128)}, f32[128,4096]{1,0:T(8,128)S(1)}, u32[]{:S(2)}) copy-start(f32[128,4096]{1,0:T(8,128)S(1)} %get-tuple-element.100.plan) | copy-start | bytes 6291460
  73.2 9.8 %all-to-all-start.5 = ((f32[8,1,2304]{2,1,0:T(1,128)}), f32[8,1,2304]{2,1,0:T(1,128)S(1)}, u32[]{:S(2)}, u32[]{:S(2)}) async-start(f32[8,1,2304]{2,1,0:T(1,128)} %get-tuple-element.97), calls=%async_computation.5 | async-start | bytes 147456 | tf_op jit(solution)/shard_map/all_to_all | solution.py:26
  78.0 5.1 %collective-permute-start.5 = (f32[1,2048]{1,0:T(1,128)S(1)}, f32[1,2048]{1,0:T(1,128)S(1)}, u32[]{:S(2)}, u32[]{:S(2)}) collective-permute-start(f32[1,2048]{1,0:T(1,128)S(1)} %get-tuple-element.101.mine), channel_id=1, source_target_pairs={{0,4},{4,0},{1,5},{5,1},{2,6},{6,2},{3,7},{7,3},{8,12},{12,8},{9,1... | collective-permute-start | bytes 24584 | tf_op jit(solution)/shard_map/ppermute | solution.py:30
  83.1 1.6 %copy-start.5 = (f32[128,4096]{1,0:T(8,128)S(1)}, f32[128,4096]{1,0:T(8,128)}, u32[]{:S(2)}) copy-start(f32[128,4096]{1,0:T(8,128)} %copy-done.4) | copy-start | bytes 6291460
  85.4 2.8 %collective-permute-start.6 = (f32[1,2048]{1,0:T(1,128)S(1)}, f32[1,2048]{1,0:T(1,128)S(1)}, u32[]{:S(2)}, u32[]{:S(2)}) collective-permute-start(f32[1,2048]{1,0:T(1,128)S(1)} %get-tuple-element.109), channel_id=1, source_target_pairs={{0,4},{4,0},{1,5},{5,1},{2,6},{6,2},{3,7},{7,3},{8,12},{12,8},{9,1... | collective-permute-start | bytes 24584 | tf_op jit(solution)/shard_map/ppermute | solution.py:30
  86.8 1.4 %copy-start.6 = (f32[128,4096]{1,0:T(8,128)}, f32[128,4096]{1,0:T(8,128)S(1)}, u32[]{:S(2)}) copy-start(f32[128,4096]{1,0:T(8,128)S(1)} %get-tuple-element.107.plan) | copy-start | bytes 6291460
  88.9 10.5 %all-to-all-start.6 = ((f32[16,1,2048]{2,1,0:T(1,128)}), f32[16,1,2048]{2,1,0:T(1,128)S(1)}, u32[]{:S(2)}, u32[]{:S(2)}) async-start(f32[16,1,2048]{2,1,0:T(1,128)} %shard_map.101), calls=%async_computation.6 | async-start | bytes 262144 | tf_op jit(solution)/shard_map/all_to_all | solution.py:26
  99.4 4.1 %collective-permute-start.7 = (f32[1,2048]{1,0:T(1,128)S(1)}, f32[1,2048]{1,0:T(1,128)S(1)}, u32[]{:S(2)}, u32[]{:S(2)}) collective-permute-start(f32[1,2048]{1,0:T(1,128)S(1)} %get-tuple-element.111.after.mine), channel_id=1, source_target_pairs={{0,4},{4,0},{1,5},{5,1},{2,6},{6,2},{3,7},{7,3},{8,12},{12,8},{9,1... | collective-permute-start | bytes 24584 | tf_op jit(solution)/shard_map/ppermute | solution.py:30
  100.9 1.6 %copy-start.7 = (f32[128,4096]{1,0:T(8,128)S(1)}, f32[128,4096]{1,0:T(8,128)}, u32[]{:S(2)}) copy-start(f32[128,4096]{1,0:T(8,128)} %copy-done.6) | copy-start | bytes 6291460

commit v8 on v7

--- a/solution.py
+++ b/solution.py
@@ -13,7 +13,7 @@
 ITERS = 4
 LANES = 128
 GROUP = 8
-CHUNKS = 2
+CHUNKS = 4
 WIDTH = 2
 MOVED = 2
 CORE = "wide_2"
@@ -158,7 +158,8 @@
             copy = pltpu.make_async_copy(
                 sources[n].at[:, lanes], targets[n].at[:, lanes], sems.at[n, k]
             )
-            copy.start()
+            if k < CHUNKS:
+                copy.start()
             big.append(copy)
     for copy in small:
         copy.wait()
@@ -168,6 +169,9 @@
     for k in range(CHUNKS):
         big[2 * k].wait()
         big[2 * k + 1].wait()
+        if k == 0:
+            for copy in big[2 * CHUNKS :]:
+                copy.start()
         shift = k * tiles
         state = sweep(
             jnp.float32(1.0), cost, plan, fresh_plan, row_all, col_dual,
@@ -271,15 +275,18 @@
     copy.wait()
 
 
-def last_reduce_kernel(got, row_got, mine, row_left):
+def row_kernel(*refs):
+    rows = refs[0][...]
+    for ref in refs[1:-1]:
+        rows = rows + ref[...]
+    refs[-1][...] = rows
+
+
+def last_reduce_kernel(got, mine):
     cols = got[0]
     for p in range(1, got.shape[0]):
         cols = cols + got[p]
     mine[...] = cols
-    rows = row_got[0]
-    for n in range(1, row_got.shape[0]):
-        rows = rows + row_got[n]
-    row_left[...] = rows
 
 
 def finish_kernel(
@@ -389,8 +396,12 @@
     came = swap(given)
     sent = call(own(last_build_kernel, sizes), vm(chips, 1, half * LANES), kept, came)
     got = exchange(sent, PLANE)
-    row_got = lax.all_gather(row_sent, "narrow")
-    mine, row_left = call(last_reduce_kernel, (give, one), got, row_got)
+    row_got = [
+        lax.ppermute(row_sent, "narrow", [(n, (n + k) % narrow) for n in range(narrow)])
+        for k in range(1, narrow)
+    ]
+    row_left = call(row_kernel, one, row_sent, *row_got)
+    mine = call(last_reduce_kernel, give, got)
     theirs = swap(mine)
     plan, stored = call(
         own(store_kernel, sizes), (whole, one), plan, mine, plan_part,

time: 105 us -> 108 us (1.029)
  waiting for transfers between devices: 14.6 us -> 18.2 us
  local copies, waits for them, and re-layouts: 11.7 us -> 8.71 us
  blocking collectives: 41 us -> 43.8 us
  starting transfers between devices: 24 us -> 22.8 us
    all_to_all x3 -> x4, blocking collectives: 34 us -> 43.8 us  [exchange(): return lax.all_to_all(array, axes, split_axis=0, concat_axis=0, tiled=True)]
    all_gather x1 -> x0, blocking collectives: 6.99 us -> none  [shards(): row_got = lax.all_gather(row_sent, 'narrow')]
    ppermute x0 -> x3, waiting for transfers between devices: none -> 3.63 us  [shards(): lax.ppermute(row_sent, 'narrow', [(n, (n + k) % narrow) for n in range(na...]
    all_to_all x4 -> x3, starting transfers between devices: 19.2 us -> 15.7 us  [exchange(): return lax.all_to_all(array, axes, split_axis=0, concat_axis=0, tiled=True)]
    unnamed x16 -> x12, local copies, waits for them, and re-layouts: 11.7 us -> 8.71 us
    ppermute x0 -> x3, starting transfers between devices: none -> 2.28 us  [shards(): lax.ppermute(row_sent, 'narrow', [(n, (n + k) % narrow) for n in range(na...]
    pallas_call x20 -> x21, Pallas kernels: 9.71 us -> 9.05 us  [call(): pl.pallas_call(kernel, out_shape=out_shape, in_specs=[HB if o in held els...]
    all_to_all x4 -> x3, waiting for transfers between devices: 14.6 us -> 14.6 us  [exchange(): return lax.all_to_all(array, axes, split_axis=0, concat_axis=0, tiled=True)]
  transfers between devices with their start and end apart: 12 -> 14, of which waited for: 3 -> 6; matrix products, arithmetic and copies ran while one was open for 0% -> 0% of each run, Pallas kernels for 4% -> 4%
where the time goes in v8:
time: 108 us; the launch traced here: 106 us
  blocking collectives  43.8 us (41%)
  starting transfers between devices  22.8 us (21%)
  waiting for transfers between devices  18.2 us (17%)
  Pallas kernels  12.1 us (11%)
  local copies, waits for them, and re-layouts  8.71 us (8%)
    all_to_all x4, blocking collectives, exchange(): return lax.all_to_all(array, axes, split_axis=0, concat_axis=0, tiled=True)  43.8 us
    all_to_all x3, starting transfers between devices, exchange(): return lax.all_to_all(array, axes, split_axis=0, concat_axis=0, tiled=True)  15.7 us
    all_to_all x3, waiting for transfers between devices, exchange(): return lax.all_to_all(array, axes, split_axis=0, concat_axis=0, tiled=True)  14.6 us
    pallas_call x21, Pallas kernels, call(): pl.pallas_call(kernel, out_shape=out_shape, in_specs=[HB if o in held els...  9.05 us
    unnamed x12, local copies, waits for them, and re-layouts  8.71 us
    ppermute x8, starting transfers between devices, swap(): return lax.ppermute(array, CORE, [(0, 1), (1, 0)])  4.84 us
    ppermute x3, waiting for transfers between devices, shards(): lax.ppermute(row_sent, 'narrow', [(n, (n + k) % narrow) for n in range(na...  3.63 us
    pallas_call x1, Pallas kernels, shards(): pl.pallas_call(functools.partial(open_kernel, sizes), out_shape=(big, big...  3.03 us
  transfers between devices with their start and end apart: 14, of which 6 were waited for; matrix products, arithmetic and copies ran while one was open for 0% of the time, Pallas kernels for 4%

profile of v8, /device:TPU:1, one launch (start us, length us, event | category | flops | bytes accessed | tf_op | source)
XLA Modules:
  0.0 106.5 jit_solution(3033885119820194273)
XLA Ops:
  0.6 3.0 %open_step.1 = (f32[128,4096]{1,0:T(8,128)S(1)}, f32[128,4096]{1,0:T(8,128)S(1)}, f32[1,128]{1,0:T(1,128)S(1)}, f32[1,4096]{1,0:T(1,128)S(1)}, f32[1,128]{1,0:T(...) custom-call(f32[128,4096]{1,0:T(8,128)} %refs_0_.1, ...), custom_call_target="tpu_custom_call" | custom-call | flops 3145728 | tf_op jit(solution)/shard_map/open_step/pallas_call | solution.py:354
  3.7 1.5 %collective-permute-start = (f32[1,2048]{1,0:T(1,128)S(1)}, f32[1,2048]{1,0:T(1,128)S(1)}, u32[]{:S(2)}, u32[]{:S(2)}) collective-permute-start(f32[1,2048]{1,0:T(1,128)S(1)} %get-tuple-element.70), channel_id=1, source_target_pairs={{0,4},{4,0},{1,5},{5,1},{2,6},{6,2},{3,7},{7,3},{8,12},{12,8},{9,1... | collective-permute-start | bytes 24584 | tf_op jit(solution)/shard_map/ppermute | solution.py:30
  5.1 0.7 shard_map.85
  5.8 0.0 copy-start
  5.8 1.3 %copy-done = f32[128,4096]{1,0:T(8,128)} copy-done((f32[128,4096]{1,0:T(8,128)}, f32[128,4096]{1,0:T(8,128)S(1)}, u32[]{:S(2)}) %copy-start) | copy-done | bytes 2097176
  7.1 14.4 %all_to_all.35.got = f32[16,1,2304]{2,1,0:T(1,128)S(1)} all-to-all(f32[16,1,2304]{2,1,0:T(1,128)S(1)} %shard_map.86), channel_id=1, replica_groups=mesh['wide_0'=4,'wide_1'=4,'wide_2'=2,'narrow'=4] {'wide_0','wide_1'}, dimensions={0} | all-to-all | bytes 294912 | tf_op jit(solution)/shard_map/all_to_all | solution.py:26
  21.5 0.7 shard_map.87
  22.2 6.0 %all-to-all-start.1 = ((f32[8,1,2304]{2,1,0:T(1,128)}), f32[8,1,2304]{2,1,0:T(1,128)S(1)}, u32[]{:S(2)}, u32[]{:S(2)}) async-start(f32[8,1,2304]{2,1,0:T(1,128)} %get-tuple-element.71), calls=%async_computation.1 | async-start | bytes 147456 | tf_op jit(solution)/shard_map/all_to_all | solution.py:26
  28.2 5.0 %all-to-all-done.1.got = f32[8,1,2304]{2,1,0:T(1,128)S(1)} async-done(((f32[8,1,2304]{2,1,0:T(1,128)}), f32[8,1,2304]{2,1,0:T(1,128)S(1)}, u32[]{:S(2)}, u32[]{:S(2)}) %all-to-all-start.1) | async-done | bytes 73760 | tf_op jit(solution)/shard_map/all_to_all | solution.py:26
  33.1 0.1 shard_map.88
  33.3 0.0 copy-start.1
  33.3 1.6 %copy-done.1 = f32[128,4096]{1,0:T(8,128)S(1)} copy-done((f32[128,4096]{1,0:T(8,128)S(1)}, f32[128,4096]{1,0:T(8,128)}, u32[]{:S(2)}) %copy-start.1) | copy-done | bytes 2097176
  34.9 0.7 shard_map.89
  35.5 0.5 collective-permute-start.2
  36.0 0.7 shard_map.90
  36.7 1.3 %copy-done.2 = f32[128,4096]{1,0:T(8,128)} copy-done((f32[128,4096]{1,0:T(8,128)}, f32[128,4096]{1,0:T(8,128)S(1)}, u32[]{:S(2)}) %copy-start.2) | copy-done | bytes 2097176
  38.0 9.8 %all_to_all.36.got = f32[16,1,2304]{2,1,0:T(1,128)S(1)} all-to-all(f32[16,1,2304]{2,1,0:T(1,128)S(1)} %shard_map.91), channel_id=1, replica_groups=mesh['wide_0'=4,'wide_1'=4,'wide_2'=2,'narrow'=4] {'wide_0','wide_1'}, dimensions={0} | all-to-all | bytes 294912 | tf_op jit(solution)/shard_map/all_to_all | solution.py:26
  47.8 0.7 shard_map.92
  48.5 4.9 %all-to-all-start.3 = ((f32[8,1,2304]{2,1,0:T(1,128)}), f32[8,1,2304]{2,1,0:T(1,128)S(1)}, u32[]{:S(2)}, u32[]{:S(2)}) async-start(f32[8,1,2304]{2,1,0:T(1,128)} %get-tuple-element.83), calls=%async_computation.3 | async-start | bytes 147456 | tf_op jit(solution)/shard_map/all_to_all | solution.py:26
  53.4 0.2 collective-permute-start.3
  53.5 4.8 %all-to-all-done.3.got = f32[8,1,2304]{2,1,0:T(1,128)S(1)} async-done(((f32[8,1,2304]{2,1,0:T(1,128)}), f32[8,1,2304]{2,1,0:T(1,128)S(1)}, u32[]{:S(2)}, u32[]{:S(2)}) %all-to-all-start.3) | async-done | bytes 73760 | tf_op jit(solution)/shard_map/all_to_all | solution.py:26
  58.3 0.1 shard_map.93
  58.5 0.0 copy-start.3
  58.5 1.6 %copy-done.3 = f32[128,4096]{1,0:T(8,128)S(1)} copy-done((f32[128,4096]{1,0:T(8,128)S(1)}, f32[128,4096]{1,0:T(8,128)}, u32[]{:S(2)}) %copy-start.3) | copy-done | bytes 2097176
  60.1 0.7 shard_map.94
  60.7 0.5 collective-permute-start.4
  61.2 0.7 shard_map.95
  61.9 0.0 copy-start.4
  61.9 1.3 %copy-done.4 = f32[128,4096]{1,0:T(8,128)} copy-done((f32[128,4096]{1,0:T(8,128)}, f32[128,4096]{1,0:T(8,128)S(1)}, u32[]{:S(2)}) %copy-start.4) | copy-done | bytes 2097176
  63.2 9.8 %all_to_all.37.got = f32[16,1,2304]{2,1,0:T(1,128)S(1)} all-to-all(f32[16,1,2304]{2,1,0:T(1,128)S(1)} %shard_map.96), channel_id=1, replica_groups=mesh['wide_0'=4,'wide_1'=4,'wide_2'=2,'narrow'=4] {'wide_0','wide_1'}, dimensions={0} | all-to-all | bytes 294912 | tf_op jit(solution)/shard_map/all_to_all | solution.py:26
  73.1 0.7 shard_map.97
  73.7 4.9 %all-to-all-start.5 = ((f32[8,1,2304]{2,1,0:T(1,128)}), f32[8,1,2304]{2,1,0:T(1,128)S(1)}, u32[]{:S(2)}, u32[]{:S(2)}) async-start(f32[8,1,2304]{2,1,0:T(1,128)} %get-tuple-element.95), calls=%async_computation.5 | async-start | bytes 147456 | tf_op jit(solution)/shard_map/all_to_all | solution.py:26
  78.6 0.2 collective-permute-start.5
  78.8 4.8 %all-to-all-done.5.got = f32[8,1,2304]{2,1,0:T(1,128)S(1)} async-done(((f32[8,1,2304]{2,1,0:T(1,128)}), f32[8,1,2304]{2,1,0:T(1,128)S(1)}, u32[]{:S(2)}, u32[]{:S(2)}) %all-to-all-start.5) | async-done | bytes 73760 | tf_op jit(solution)/shard_map/all_to_all | solution.py:26
  83.6 0.1 shard_map.98
  83.7 1.6 %copy-done.5 = f32[128,4096]{1,0:T(8,128)S(1)} copy-done((f32[128,4096]{1,0:T(8,128)S(1)}, f32[128,4096]{1,0:T(8,128)}, u32[]{:S(2)}) %copy-start.5) | copy-done | bytes 2097176
  85.3 0.7 shard_map.99
  86.0 0.5 collective-permute-start.6
  86.4 1.0 shard_map.100
  87.5 9.8 %all_to_all.38.got = f32[16,1,2048]{2,1,0:T(1,128)S(1)} all-to-all(f32[16,1,2048]{2,1,0:T(1,128)S(1)} %shard_map.101), channel_id=1, replica_groups=mesh['wide_0'=4,'wide_1'=4,'wide_2'=2,'narrow'=4] {'wide_0','wide_1'}, dimensions={0} | all-to-all | bytes 262144 | tf_op jit(solution)/shard_map/all_to_all | solution.py:26
  97.3 1.6 %collective-permute-start.7 = (f32[1,2048]{1,0:T(1,128)S(1)}, f32[1,2048]{1,0:T(1,128)S(1)}, u32[]{:S(2)}, u32[]{:S(2)}) collective-permute-start(f32[1,2048]{1,0:T(1,128)S(1)} %shard_map.102.after.mine), channel_id=1, source_target_pairs={{0,4},{4,0},{1,5},{5,1},{2,6},{6,2},{3,7},{7,3},{8,12},{12,8},{9,1... | collective-permute-start | bytes 24584 | tf_op jit(solution)/shard_map/ppermute | solution.py:30
  98.9 1.2 %collective-permute-start.10 = (f32[1,128]{1,0:T(1,128)S(1)}, f32[1,128]{1,0:T(1,128)S(1)}, u32[]{:S(2)}, u32[]{:S(2)}) collective-permute-start(f32[1,128]{1,0:T(1,128)S(1)} %get-tuple-element.111.refs_0_), channel_id=1, source_target_pairs={{0,3},{1,0},{2,1},{3,2},{4,7},{5,4},{6,5},{7,6},{8,11},{9,8},{10,9... | collective-permute-start | bytes 1544 | tf_op jit(solution)/shard_map/ppermute | solution.py:400
  100.1 1.1 %collective-permute-start.9 = (f32[1,128]{1,0:T(1,128)S(1)}, f32[1,128]{1,0:T(1,128)S(1)}, u32[]{:S(2)}, u32[]{:S(2)}) collective-permute-start(f32[1,128]{1,0:T(1,128)S(1)} %get-tuple-element.111.refs_0_), channel_id=1, source_target_pairs={{0,2},{1,3},{2,0},{3,1},{4,6},{5,7},{6,4},{7,5},{8,10},{9,11},{10,... | collective-permute-start | bytes 1544 | tf_op jit(solution)/shard_map/ppermute | solution.py:400
  101.2 0.1 collective-permute-done.10.refs_3_
  101.3 2.7 %collective-permute-done.9.refs_2_ = f32[1,128]{1,0:T(1,128)S(1)} collective-permute-done((f32[1,128]{1,0:T(1,128)S(1)}, f32[1,128]{1,0:T(1,128)S(1)}, u32[]{:S(2)}, u32[]{:S(2)}) %collective-permute-start.9) | collective-permute-done | bytes 544 | tf_op jit(solution)/shard_map/ppermute | solution.py:400
  104.0 0.8 collective-permute-done.8.refs_1_
  104.8 1.0 shard_map.103
  105.8 0.7 shard_map.105
  (18 shorter events, 0.1 us)
Async XLA Ops:
  3.7 3.5 %collective-permute-start = (f32[1,2048]{1,0:T(1,128)S(1)}, f32[1,2048]{1,0:T(1,128)S(1)}, u32[]{:S(2)}, u32[]{:S(2)}) collective-permute-start(f32[1,2048]{1,0:T(1,128)S(1)} %get-tuple-element.70), channel_id=1, source_target_pairs={{0,4},{4,0},{1,5},{5,1},{2,6},{6,2},{3,7},{7,3},{8,12},{12,8},{9,1... | collective-permute-start | bytes 24584 | tf_op jit(solution)/shard_map/ppermute | solution.py:30
  5.8 1.3 %copy-start = (f32[128,4096]{1,0:T(8,128)}, f32[128,4096]{1,0:T(8,128)S(1)}, u32[]{:S(2)}) copy-start(f32[128,4096]{1,0:T(8,128)S(1)} %get-tuple-element.74.plan) | copy-start | bytes 6291460
  22.2 11.0 %all-to-all-start.1 = ((f32[8,1,2304]{2,1,0:T(1,128)}), f32[8,1,2304]{2,1,0:T(1,128)S(1)}, u32[]{:S(2)}, u32[]{:S(2)}) async-start(f32[8,1,2304]{2,1,0:T(1,128)} %get-tuple-element.71), calls=%async_computation.1 | async-start | bytes 147456 | tf_op jit(solution)/shard_map/all_to_all | solution.py:26
  28.2 5.1 %collective-permute-start.1 = (f32[1,2048]{1,0:T(1,128)S(1)}, f32[1,2048]{1,0:T(1,128)S(1)}, u32[]{:S(2)}, u32[]{:S(2)}) collective-permute-start(f32[1,2048]{1,0:T(1,128)S(1)} %get-tuple-element.75.mine), channel_id=1, source_target_pairs={{0,4},{4,0},{1,5},{5,1},{2,6},{6,2},{3,7},{7,3},{8,12},{12,8},{9,1... | collective-permute-start | bytes 24584 | tf_op jit(solution)/shard_map/ppermute | solution.py:30
  33.3 1.6 %copy-start.1 = (f32[128,4096]{1,0:T(8,128)S(1)}, f32[128,4096]{1,0:T(8,128)}, u32[]{:S(2)}) copy-start(f32[128,4096]{1,0:T(8,128)} %copy-done) | copy-start | bytes 6291460
  35.5 2.5 %collective-permute-start.2 = (f32[1,2048]{1,0:T(1,128)S(1)}, f32[1,2048]{1,0:T(1,128)S(1)}, u32[]{:S(2)}, u32[]{:S(2)}) collective-permute-start(f32[1,2048]{1,0:T(1,128)S(1)} %get-tuple-element.82), channel_id=1, source_target_pairs={{0,4},{4,0},{1,5},{5,1},{2,6},{6,2},{3,7},{7,3},{8,12},{12,8},{9,1... | collective-permute-start | bytes 24584 | tf_op jit(solution)/shard_map/ppermute | solution.py:30
  36.7 1.3 %copy-start.2 = (f32[128,4096]{1,0:T(8,128)}, f32[128,4096]{1,0:T(8,128)S(1)}, u32[]{:S(2)}) copy-start(f32[128,4096]{1,0:T(8,128)S(1)} %get-tuple-element.86.plan) | copy-start | bytes 6291460
  48.5 9.8 %all-to-all-start.3 = ((f32[8,1,2304]{2,1,0:T(1,128)}), f32[8,1,2304]{2,1,0:T(1,128)S(1)}, u32[]{:S(2)}, u32[]{:S(2)}) async-start(f32[8,1,2304]{2,1,0:T(1,128)} %get-tuple-element.83), calls=%async_computation.3 | async-start | bytes 147456 | tf_op jit(solution)/shard_map/all_to_all | solution.py:26
  53.4 5.1 %collective-permute-start.3 = (f32[1,2048]{1,0:T(1,128)S(1)}, f32[1,2048]{1,0:T(1,128)S(1)}, u32[]{:S(2)}, u32[]{:S(2)}) collective-permute-start(f32[1,2048]{1,0:T(1,128)S(1)} %get-tuple-element.87.mine), channel_id=1, source_target_pairs={{0,4},{4,0},{1,5},{5,1},{2,6},{6,2},{3,7},{7,3},{8,12},{12,8},{9,1... | collective-permute-start | bytes 24584 | tf_op jit(solution)/shard_map/ppermute | solution.py:30
  58.5 1.6 %copy-start.3 = (f32[128,4096]{1,0:T(8,128)S(1)}, f32[128,4096]{1,0:T(8,128)}, u32[]{:S(2)}) copy-start(f32[128,4096]{1,0:T(8,128)} %copy-done.2) | copy-start | bytes 6291460
  60.7 2.5 %collective-permute-start.4 = (f32[1,2048]{1,0:T(1,128)S(1)}, f32[1,2048]{1,0:T(1,128)S(1)}, u32[]{:S(2)}, u32[]{:S(2)}) collective-permute-start(f32[1,2048]{1,0:T(1,128)S(1)} %get-tuple-element.94), channel_id=1, source_target_pairs={{0,4},{4,0},{1,5},{5,1},{2,6},{6,2},{3,7},{7,3},{8,12},{12,8},{9,1... | collective-permute-start | bytes 24584 | tf_op jit(solution)/shard_map/ppermute | solution.py:30
  61.9 1.3 %copy-start.4 = (f32[128,4096]{1,0:T(8,128)}, f32[128,4096]{1,0:T(8,128)S(1)}, u32[]{:S(2)}) copy-start(f32[128,4096]{1,0:T(8,128)S(1)} %get-tuple-element.98.plan) | copy-start | bytes 6291460
  73.7 9.8 %all-to-all-start.5 = ((f32[8,1,2304]{2,1,0:T(1,128)}), f32[8,1,2304]{2,1,0:T(1,128)S(1)}, u32[]{:S(2)}, u32[]{:S(2)}) async-start(f32[8,1,2304]{2,1,0:T(1,128)} %get-tuple-element.95), calls=%async_computation.5 | async-start | bytes 147456 | tf_op jit(solution)/shard_map/all_to_all | solution.py:26
  78.6 5.1 %collective-permute-start.5 = (f32[1,2048]{1,0:T(1,128)S(1)}, f32[1,2048]{1,0:T(1,128)S(1)}, u32[]{:S(2)}, u32[]{:S(2)}) collective-permute-start(f32[1,2048]{1,0:T(1,128)S(1)} %get-tuple-element.99.mine), channel_id=1, source_target_pairs={{0,4},{4,0},{1,5},{5,1},{2,6},{6,2},{3,7},{7,3},{8,12},{12,8},{9,1... | collective-permute-start | bytes 24584 | tf_op jit(solution)/shard_map/ppermute | solution.py:30
  83.7 1.6 %copy-start.5 = (f32[128,4096]{1,0:T(8,128)S(1)}, f32[128,4096]{1,0:T(8,128)}, u32[]{:S(2)}) copy-start(f32[128,4096]{1,0:T(8,128)} %copy-done.4) | copy-start | bytes 6291460
  86.0 1.5 %collective-permute-start.6 = (f32[1,2048]{1,0:T(1,128)S(1)}, f32[1,2048]{1,0:T(1,128)S(1)}, u32[]{:S(2)}, u32[]{:S(2)}) collective-permute-start(f32[1,2048]{1,0:T(1,128)S(1)} %get-tuple-element.107), channel_id=1, source_target_pairs={{0,4},{4,0},{1,5},{5,1},{2,6},{6,2},{3,7},{7,3},{8,12},{12,8},{9,1... | collective-permute-start | bytes 24584 | tf_op jit(solution)/shard_map/ppermute | solution.py:30
  97.3 8.5 %collective-permute-start.7 = (f32[1,2048]{1,0:T(1,128)S(1)}, f32[1,2048]{1,0:T(1,128)S(1)}, u32[]{:S(2)}, u32[]{:S(2)}) collective-permute-start(f32[1,2048]{1,0:T(1,128)S(1)} %shard_map.102.after.mine), channel_id=1, source_target_pairs={{0,4},{4,0},{1,5},{5,1},{2,6},{6,2},{3,7},{7,3},{8,12},{12,8},{9,1... | collective-permute-start | bytes 24584 | tf_op jit(solution)/shard_map/ppermute | solution.py:30
  98.9 2.4 %collective-permute-start.10 = (f32[1,128]{1,0:T(1,128)S(1)}, f32[1,128]{1,0:T(1,128)S(1)}, u32[]{:S(2)}, u32[]{:S(2)}) collective-permute-start(f32[1,128]{1,0:T(1,128)S(1)} %get-tuple-element.111.refs_0_), channel_id=1, source_target_pairs={{0,3},{1,0},{2,1},{3,2},{4,7},{5,4},{6,5},{7,6},{8,11},{9,8},{10,9... | collective-permute-start | bytes 1544 | tf_op jit(solution)/shard_map/ppermute | solution.py:400
  100.1 3.9 %collective-permute-start.9 = (f32[1,128]{1,0:T(1,128)S(1)}, f32[1,128]{1,0:T(1,128)S(1)}, u32[]{:S(2)}, u32[]{:S(2)}) collective-permute-start(f32[1,128]{1,0:T(1,128)S(1)} %get-tuple-element.111.refs_0_), channel_id=1, source_target_pairs={{0,2},{1,3},{2,0},{3,1},{4,6},{5,7},{6,4},{7,5},{8,10},{9,11},{10,... | collective-permute-start | bytes 1544 | tf_op jit(solution)/shard_map/ppermute | solution.py:400
  101.2 3.6 %collective-permute-start.8 = (f32[1,128]{1,0:T(1,128)S(1)}, f32[1,128]{1,0:T(1,128)S(1)}, u32[]{:S(2)}, u32[]{:S(2)}) collective-permute-start(f32[1,128]{1,0:T(1,128)S(1)} %get-tuple-element.111.refs_0_), channel_id=1, source_target_pairs={{0,1},{1,2},{2,3},{3,0},{4,5},{5,6},{6,7},{7,4},{8,9},{9,10},{10,1... | collective-permute-start | bytes 1544 | tf_op jit(solution)/shard_map/ppermute | solution.py:400

commit v9 on v8

--- a/solution.py
+++ b/solution.py
@@ -13,17 +13,35 @@
 ITERS = 4
 LANES = 128
 GROUP = 8
-CHUNKS = 4
+CHUNKS = 2
 WIDTH = 2
 MOVED = 2
 CORE = "wide_2"
 WIDE = ("wide_0", "wide_1", "wide_2")
 COLUMN = ("wide_2", "narrow")
-PLANE = ("wide_0", "wide_1")
-
-
-def exchange(array, axes):
-    return lax.all_to_all(array, axes, split_axis=0, concat_axis=0, tiled=True)
+
+
+def exchange(array, axes, groups=None):
+    return lax.all_to_all(
+        array, axes, split_axis=0, concat_axis=0, tiled=True, axis_index_groups=groups
+    )
+
+
+def crossed():
+    sizes = [lax.axis_size(axis) for axis in WIDE]
+    groups = []
+    for side in range(sizes[2]):
+        groups.append([
+            (a * sizes[1] + b) * sizes[2] + (side ^ (a * 2 // sizes[0]))
+            for a in range(sizes[0])
+            for b in range(sizes[1])
+        ])
+    return groups
+
+
+def own_side():
+    upper = (lax.axis_index("wide_0") * 2) // lax.axis_size("wide_0")
+    return (lax.axis_index(CORE) + upper) % 2
 
 
 def swap(array):
@@ -74,9 +92,9 @@
 
 def col_update(mine, theirs, weight, col_dual, new_col, sizes):
     base, half = sizes[1], sizes[2]
-    core = lax.axis_index(CORE)
+    own = own_side()
     scale = jnp.broadcast_to((base * weight[...])[0:1, 0:1], (1, half * LANES))
-    for side, part in ((core, mine), (1 - core, theirs)):
+    for side, part in ((own, mine), (1 - own, theirs)):
         lanes = span(side * half, half)
         new_col[:, lanes] = col_dual[:, lanes] + scale * part[...]
 
@@ -144,7 +162,7 @@
     sources, targets = refs[:6], refs[6:12]
     fresh_plan, give, row_sums, moved_sums, row_all, weight, sems = refs[12:]
     cost, plan, _, col_mass, row_dual, col_dual = targets
-    core = lax.axis_index(CORE)
+    own = own_side()
     tiles = half // CHUNKS
     weight[...] = jnp.full((GROUP, LANES), base, jnp.float32)
     small = [pltpu.make_async_copy(sources[n], targets[n], sems.at[n, 0]) for n in range(2, 6)]
@@ -152,14 +170,13 @@
         copy.start()
     big = []
     for k in range(CHUNKS + 1):
-        first = (1 - core) * half + k * tiles if k < CHUNKS else core * half
+        first = (1 - own) * half + k * tiles if k < CHUNKS else own * half
         lanes = span(first, tiles if k < CHUNKS else half)
         for n in range(2):
             copy = pltpu.make_async_copy(
                 sources[n].at[:, lanes], targets[n].at[:, lanes], sems.at[n, k]
             )
-            if k < CHUNKS:
-                copy.start()
+            copy.start()
             big.append(copy)
     for copy in small:
         copy.wait()
@@ -169,13 +186,10 @@
     for k in range(CHUNKS):
         big[2 * k].wait()
         big[2 * k + 1].wait()
-        if k == 0:
-            for copy in big[2 * CHUNKS :]:
-                copy.start()
         shift = k * tiles
         state = sweep(
             jnp.float32(1.0), cost, plan, fresh_plan, row_all, col_dual,
-            ((1 - core) * half + shift, tiles), state,
+            ((1 - own) * half + shift, tiles), state,
             lambda n, j, cols, shift=shift: put(n + shift, j, cols),
         )
     hold(state, row_sums, moved_sums)
@@ -195,7 +209,7 @@
 ):
     _, base, half, chips = sizes
     col_update(mine, theirs, weight, col_dual, new_col, sizes)
-    side = 1 - lax.axis_index(CORE)
+    side = 1 - own_side()
     state = sweep(
         base / new_weight[...], cost, plan, fresh_plan, row_all, new_col, (side * half, half),
         zeros(row_all), into(give, col_mass, 2 * chips),
@@ -208,7 +222,7 @@
     moved_sums, fresh_plan, keep, *last,
 ):
     _, base, half, chips = sizes
-    side = lax.axis_index(CORE)
+    side = own_side()
     copy = None
     if last:
         row_share, plan_out, sem = last
@@ -268,7 +282,7 @@
 
 def store_kernel(sizes, plan, after, plan_part, plan_out, stored, sem):
     half = sizes[2]
-    lanes = span(lax.axis_index(CORE) * half, half)
+    lanes = span(own_side() * half, half)
     copy = pltpu.make_async_copy(plan.at[:, lanes], plan_out.at[:, lanes], sem)
     copy.start()
     stored[...] = after[:, tile_of(0)]
@@ -371,7 +385,7 @@
     for step in range(1, ITERS):
         came = swap(given)
         sent = call(own(build_kernel, sizes), vm(chips, 1, (half + 2) * LANES), kept, came)
-        got = exchange(sent, PLANE)
+        got = exchange(sent, WIDE, crossed())
         mine, sent = call(
             own(reduce_kernel, sizes),
             (give, vm(2 * narrow, 1, (chips + 2) * LANES)), got,
@@ -395,7 +409,7 @@
     row_sent, plan_part = tail_parts
     came = swap(given)
     sent = call(own(last_build_kernel, sizes), vm(chips, 1, half * LANES), kept, came)
-    got = exchange(sent, PLANE)
+    got = exchange(sent, WIDE, crossed())
     row_got = [
         lax.ppermute(row_sent, "narrow", [(n, (n + k) % narrow) for n in range(narrow)])
         for k in range(1, narrow)

time: 108 us -> 107 us (level)
  blocking collectives: 43.8 us -> 49.6 us
  starting transfers between devices: 22.8 us -> 17.3 us
    all_to_all x4, blocking collectives: 43.8 us -> 49.6 us  [exchange(): lax.all_to_all(array, axes, split_axis=0, concat_axis=0, tiled=True, axis...]
    all_to_all x3, starting transfers between devices: 15.7 us -> 11.6 us  [exchange(): lax.all_to_all(array, axes, split_axis=0, concat_axis=0, tiled=True, axis...]
    ppermute x8, starting transfers between devices: 4.84 us -> 3.42 us  [swap(): return lax.ppermute(array, CORE, [(0, 1), (1, 0)])]
where the time goes in v9:
time: 107 us; the launch traced here: 106 us
  blocking collectives  49.6 us (46%)
  waiting for transfers between devices  18.2 us (17%)
  starting transfers between devices  17.3 us (16%)
  Pallas kernels  11.5 us (11%)
  local copies, waits for them, and re-layouts  8.71 us (8%)
    all_to_all x4, blocking collectives, exchange(): lax.all_to_all(array, axes, split_axis=0, concat_axis=0, tiled=True, axis...  49.6 us
    all_to_all x3, waiting for transfers between devices, exchange(): lax.all_to_all(array, axes, split_axis=0, concat_axis=0, tiled=True, axis...  14.6 us
    all_to_all x3, starting transfers between devices, exchange(): lax.all_to_all(array, axes, split_axis=0, concat_axis=0, tiled=True, axis...  11.6 us
    pallas_call x21, Pallas kernels, call(): pl.pallas_call(kernel, out_shape=out_shape, in_specs=[HB if o in held els...  9.05 us
    unnamed x12, local copies, waits for them, and re-layouts  8.71 us
    ppermute x3, waiting for transfers between devices, shards(): lax.ppermute(row_sent, 'narrow', [(n, (n + k) % narrow) for n in range(na...  3.63 us
    ppermute x8, starting transfers between devices, swap(): return lax.ppermute(array, CORE, [(0, 1), (1, 0)])  3.42 us
    pallas_call x1, Pallas kernels, shards(): pl.pallas_call(functools.partial(open_kernel, sizes), out_shape=(big, big...  2.41 us
  transfers between devices with their start and end apart: 14, of which 6 were waited for; matrix products, arithmetic and copies ran while one was open for 0% of the time, Pallas kernels for 4%

profile of v9, /device:TPU:1, one launch (start us, length us, event | category | flops | bytes accessed | tf_op | source)
XLA Modules:
  0.0 106.1 jit_solution(8512512978213509706)
XLA Ops:
  0.6 2.4 %open_step.1 = (f32[128,4096]{1,0:T(8,128)S(1)}, f32[128,4096]{1,0:T(8,128)S(1)}, f32[1,128]{1,0:T(1,128)S(1)}, f32[1,4096]{1,0:T(1,128)S(1)}, f32[1,128]{1,0:T(...) custom-call(f32[128,4096]{1,0:T(8,128)} %refs_0_.1, ...), custom_call_target="tpu_custom_call" | custom-call | flops 3145728 | tf_op jit(solution)/shard_map/open_step/pallas_call | solution.py:368
  3.0 1.5 %collective-permute-start = (f32[1,2048]{1,0:T(1,128)S(1)}, f32[1,2048]{1,0:T(1,128)S(1)}, u32[]{:S(2)}, u32[]{:S(2)}) collective-permute-start(f32[1,2048]{1,0:T(1,128)S(1)} %get-tuple-element.70), channel_id=1, source_target_pairs={{0,4},{4,0},{1,5},{5,1},{2,6},{6,2},{3,7},{7,3},{8,12},{12,8},{9,1... | collective-permute-start | bytes 24584 | tf_op jit(solution)/shard_map/ppermute | solution.py:48
  4.5 0.7 shard_map.85
  5.2 0.0 copy-start
  5.2 1.3 %copy-done = f32[128,4096]{1,0:T(8,128)} copy-done((f32[128,4096]{1,0:T(8,128)}, f32[128,4096]{1,0:T(8,128)S(1)}, u32[]{:S(2)}) %copy-start) | copy-done | bytes 2097176
  6.5 15.3 %all_to_all.35.got = f32[16,1,2304]{2,1,0:T(1,128)S(1)} all-to-all(f32[16,1,2304]{2,1,0:T(1,128)S(1)} %shard_map.86), channel_id=1, replica_groups={{0,8,16,24,32,40,48,56,68,76,84,92,100,108,116,124},{4,12,20,28,36,44,5..., dimensions={0} | all-to-all | bytes 294912 | tf_op jit(solution)/shard_map/all_to_all | solution.py:25
  21.8 0.7 shard_map.87
  22.5 4.8 %all-to-all-start.1 = ((f32[8,1,2304]{2,1,0:T(1,128)}), f32[8,1,2304]{2,1,0:T(1,128)S(1)}, u32[]{:S(2)}, u32[]{:S(2)}) async-start(f32[8,1,2304]{2,1,0:T(1,128)} %get-tuple-element.71), calls=%async_computation.1 | async-start | bytes 147456 | tf_op jit(solution)/shard_map/all_to_all | solution.py:25
  27.3 5.0 %all-to-all-done.1.got = f32[8,1,2304]{2,1,0:T(1,128)S(1)} async-done(((f32[8,1,2304]{2,1,0:T(1,128)}), f32[8,1,2304]{2,1,0:T(1,128)S(1)}, u32[]{:S(2)}, u32[]{:S(2)}) %all-to-all-start.1) | async-done | bytes 73760 | tf_op jit(solution)/shard_map/all_to_all | solution.py:25
  32.2 0.1 shard_map.88
  32.4 0.0 copy-start.1
  32.4 1.6 %copy-done.1 = f32[128,4096]{1,0:T(8,128)S(1)} copy-done((f32[128,4096]{1,0:T(8,128)S(1)}, f32[128,4096]{1,0:T(8,128)}, u32[]{:S(2)}) %copy-start.1) | copy-done | bytes 2097176
  34.0 0.7 shard_map.89
  34.6 0.5 collective-permute-start.2
  35.1 0.7 shard_map.90
  35.8 0.0 copy-start.2
  35.8 1.3 %copy-done.2 = f32[128,4096]{1,0:T(8,128)} copy-done((f32[128,4096]{1,0:T(8,128)}, f32[128,4096]{1,0:T(8,128)S(1)}, u32[]{:S(2)}) %copy-start.2) | copy-done | bytes 2097176
  37.1 11.4 %all_to_all.36.got = f32[16,1,2304]{2,1,0:T(1,128)S(1)} all-to-all(f32[16,1,2304]{2,1,0:T(1,128)S(1)} %shard_map.91), channel_id=1, replica_groups={{0,8,16,24,32,40,48,56,68,76,84,92,100,108,116,124},{4,12,20,28,36,44,5..., dimensions={0} | all-to-all | bytes 294912 | tf_op jit(solution)/shard_map/all_to_all | solution.py:25
  48.5 0.7 shard_map.92
  49.2 3.4 %all-to-all-start.3 = ((f32[8,1,2304]{2,1,0:T(1,128)}), f32[8,1,2304]{2,1,0:T(1,128)S(1)}, u32[]{:S(2)}, u32[]{:S(2)}) async-start(f32[8,1,2304]{2,1,0:T(1,128)} %get-tuple-element.83), calls=%async_computation.3 | async-start | bytes 147456 | tf_op jit(solution)/shard_map/all_to_all | solution.py:25
  52.6 0.2 collective-permute-start.3
  52.8 4.8 %all-to-all-done.3.got = f32[8,1,2304]{2,1,0:T(1,128)S(1)} async-done(((f32[8,1,2304]{2,1,0:T(1,128)}), f32[8,1,2304]{2,1,0:T(1,128)S(1)}, u32[]{:S(2)}, u32[]{:S(2)}) %all-to-all-start.3) | async-done | bytes 73760 | tf_op jit(solution)/shard_map/all_to_all | solution.py:25
  57.6 0.1 shard_map.93
  57.7 1.6 %copy-done.3 = f32[128,4096]{1,0:T(8,128)S(1)} copy-done((f32[128,4096]{1,0:T(8,128)S(1)}, f32[128,4096]{1,0:T(8,128)}, u32[]{:S(2)}) %copy-start.3) | copy-done | bytes 2097176
  59.3 0.7 shard_map.94
  60.0 0.5 collective-permute-start.4
  60.5 0.7 shard_map.95
  61.1 1.3 %copy-done.4 = f32[128,4096]{1,0:T(8,128)} copy-done((f32[128,4096]{1,0:T(8,128)}, f32[128,4096]{1,0:T(8,128)S(1)}, u32[]{:S(2)}) %copy-start.4) | copy-done | bytes 2097176
  62.5 11.5 %all_to_all.37.got = f32[16,1,2304]{2,1,0:T(1,128)S(1)} all-to-all(f32[16,1,2304]{2,1,0:T(1,128)S(1)} %shard_map.96), channel_id=1, replica_groups={{0,8,16,24,32,40,48,56,68,76,84,92,100,108,116,124},{4,12,20,28,36,44,5..., dimensions={0} | all-to-all | bytes 294912 | tf_op jit(solution)/shard_map/all_to_all | solution.py:25
  74.0 0.7 shard_map.97
  74.7 3.4 %all-to-all-start.5 = ((f32[8,1,2304]{2,1,0:T(1,128)}), f32[8,1,2304]{2,1,0:T(1,128)S(1)}, u32[]{:S(2)}, u32[]{:S(2)}) async-start(f32[8,1,2304]{2,1,0:T(1,128)} %get-tuple-element.95), calls=%async_computation.5 | async-start | bytes 147456 | tf_op jit(solution)/shard_map/all_to_all | solution.py:25
  78.1 0.2 collective-permute-start.5
  78.2 4.8 %all-to-all-done.5.got = f32[8,1,2304]{2,1,0:T(1,128)S(1)} async-done(((f32[8,1,2304]{2,1,0:T(1,128)}), f32[8,1,2304]{2,1,0:T(1,128)S(1)}, u32[]{:S(2)}, u32[]{:S(2)}) %all-to-all-start.5) | async-done | bytes 73760 | tf_op jit(solution)/shard_map/all_to_all | solution.py:25
  83.0 0.1 shard_map.98
  83.2 0.0 copy-start.5
  83.2 1.6 %copy-done.5 = f32[128,4096]{1,0:T(8,128)S(1)} copy-done((f32[128,4096]{1,0:T(8,128)S(1)}, f32[128,4096]{1,0:T(8,128)}, u32[]{:S(2)}) %copy-start.5) | copy-done | bytes 2097176
  84.8 0.7 shard_map.99
  85.4 0.5 collective-permute-start.6
  85.9 1.0 shard_map.100
  86.9 11.4 %all_to_all.38.got = f32[16,1,2048]{2,1,0:T(1,128)S(1)} all-to-all(f32[16,1,2048]{2,1,0:T(1,128)S(1)} %shard_map.101), channel_id=1, replica_groups={{0,8,16,24,32,40,48,56,68,76,84,92,100,108,116,124},{4,12,20,28,36,44,5..., dimensions={0} | all-to-all | bytes 262144 | tf_op jit(solution)/shard_map/all_to_all | solution.py:25
  98.3 0.2 collective-permute-start.7
  98.5 1.2 %collective-permute-start.10 = (f32[1,128]{1,0:T(1,128)S(1)}, f32[1,128]{1,0:T(1,128)S(1)}, u32[]{:S(2)}, u32[]{:S(2)}) collective-permute-start(f32[1,128]{1,0:T(1,128)S(1)} %get-tuple-element.111.refs_0_), channel_id=1, source_target_pairs={{0,3},{1,0},{2,1},{3,2},{4,7},{5,4},{6,5},{7,6},{8,11},{9,8},{10,9... | collective-permute-start | bytes 1544 | tf_op jit(solution)/shard_map/ppermute | solution.py:414
  99.7 1.1 %collective-permute-start.9 = (f32[1,128]{1,0:T(1,128)S(1)}, f32[1,128]{1,0:T(1,128)S(1)}, u32[]{:S(2)}, u32[]{:S(2)}) collective-permute-start(f32[1,128]{1,0:T(1,128)S(1)} %get-tuple-element.111.refs_0_), channel_id=1, source_target_pairs={{0,2},{1,3},{2,0},{3,1},{4,6},{5,7},{6,4},{7,5},{8,10},{9,11},{10,... | collective-permute-start | bytes 1544 | tf_op jit(solution)/shard_map/ppermute | solution.py:414
  100.8 0.1 collective-permute-done.10.refs_3_
  100.9 2.7 %collective-permute-done.9.refs_2_ = f32[1,128]{1,0:T(1,128)S(1)} collective-permute-done((f32[1,128]{1,0:T(1,128)S(1)}, f32[1,128]{1,0:T(1,128)S(1)}, u32[]{:S(2)}, u32[]{:S(2)}) %collective-permute-start.9) | collective-permute-done | bytes 544 | tf_op jit(solution)/shard_map/ppermute | solution.py:414
  103.6 0.8 collective-permute-done.8.refs_1_
  104.4 1.0 shard_map.103
  105.4 0.7 shard_map.105
  (18 shorter events, 0.1 us)
Async XLA Ops:
  3.0 3.5 %collective-permute-start = (f32[1,2048]{1,0:T(1,128)S(1)}, f32[1,2048]{1,0:T(1,128)S(1)}, u32[]{:S(2)}, u32[]{:S(2)}) collective-permute-start(f32[1,2048]{1,0:T(1,128)S(1)} %get-tuple-element.70), channel_id=1, source_target_pairs={{0,4},{4,0},{1,5},{5,1},{2,6},{6,2},{3,7},{7,3},{8,12},{12,8},{9,1... | collective-permute-start | bytes 24584 | tf_op jit(solution)/shard_map/ppermute | solution.py:48
  5.2 1.3 %copy-start = (f32[128,4096]{1,0:T(8,128)}, f32[128,4096]{1,0:T(8,128)S(1)}, u32[]{:S(2)}) copy-start(f32[128,4096]{1,0:T(8,128)S(1)} %get-tuple-element.74.plan) | copy-start | bytes 6291460
  22.5 9.7 %all-to-all-start.1 = ((f32[8,1,2304]{2,1,0:T(1,128)}), f32[8,1,2304]{2,1,0:T(1,128)S(1)}, u32[]{:S(2)}, u32[]{:S(2)}) async-start(f32[8,1,2304]{2,1,0:T(1,128)} %get-tuple-element.71), calls=%async_computation.1 | async-start | bytes 147456 | tf_op jit(solution)/shard_map/all_to_all | solution.py:25
  27.3 5.1 %collective-permute-start.1 = (f32[1,2048]{1,0:T(1,128)S(1)}, f32[1,2048]{1,0:T(1,128)S(1)}, u32[]{:S(2)}, u32[]{:S(2)}) collective-permute-start(f32[1,2048]{1,0:T(1,128)S(1)} %get-tuple-element.75.mine), channel_id=1, source_target_pairs={{0,4},{4,0},{1,5},{5,1},{2,6},{6,2},{3,7},{7,3},{8,12},{12,8},{9,1... | collective-permute-start | bytes 24584 | tf_op jit(solution)/shard_map/ppermute | solution.py:48
  32.4 1.6 %copy-start.1 = (f32[128,4096]{1,0:T(8,128)S(1)}, f32[128,4096]{1,0:T(8,128)}, u32[]{:S(2)}) copy-start(f32[128,4096]{1,0:T(8,128)} %copy-done) | copy-start | bytes 6291460
  34.6 2.5 %collective-permute-start.2 = (f32[1,2048]{1,0:T(1,128)S(1)}, f32[1,2048]{1,0:T(1,128)S(1)}, u32[]{:S(2)}, u32[]{:S(2)}) collective-permute-start(f32[1,2048]{1,0:T(1,128)S(1)} %get-tuple-element.82), channel_id=1, source_target_pairs={{0,4},{4,0},{1,5},{5,1},{2,6},{6,2},{3,7},{7,3},{8,12},{12,8},{9,1... | collective-permute-start | bytes 24584 | tf_op jit(solution)/shard_map/ppermute | solution.py:48
  35.8 1.3 %copy-start.2 = (f32[128,4096]{1,0:T(8,128)}, f32[128,4096]{1,0:T(8,128)S(1)}, u32[]{:S(2)}) copy-start(f32[128,4096]{1,0:T(8,128)S(1)} %get-tuple-element.86.plan) | copy-start | bytes 6291460
  49.2 8.4 %all-to-all-start.3 = ((f32[8,1,2304]{2,1,0:T(1,128)}), f32[8,1,2304]{2,1,0:T(1,128)S(1)}, u32[]{:S(2)}, u32[]{:S(2)}) async-start(f32[8,1,2304]{2,1,0:T(1,128)} %get-tuple-element.83), calls=%async_computation.3 | async-start | bytes 147456 | tf_op jit(solution)/shard_map/all_to_all | solution.py:25
  52.6 5.1 %collective-permute-start.3 = (f32[1,2048]{1,0:T(1,128)S(1)}, f32[1,2048]{1,0:T(1,128)S(1)}, u32[]{:S(2)}, u32[]{:S(2)}) collective-permute-start(f32[1,2048]{1,0:T(1,128)S(1)} %get-tuple-element.87.mine), channel_id=1, source_target_pairs={{0,4},{4,0},{1,5},{5,1},{2,6},{6,2},{3,7},{7,3},{8,12},{12,8},{9,1... | collective-permute-start | bytes 24584 | tf_op jit(solution)/shard_map/ppermute | solution.py:48
  57.7 1.6 %copy-start.3 = (f32[128,4096]{1,0:T(8,128)S(1)}, f32[128,4096]{1,0:T(8,128)}, u32[]{:S(2)}) copy-start(f32[128,4096]{1,0:T(8,128)} %copy-done.2) | copy-start | bytes 6291460
  60.0 2.5 %collective-permute-start.4 = (f32[1,2048]{1,0:T(1,128)S(1)}, f32[1,2048]{1,0:T(1,128)S(1)}, u32[]{:S(2)}, u32[]{:S(2)}) collective-permute-start(f32[1,2048]{1,0:T(1,128)S(1)} %get-tuple-element.94), channel_id=1, source_target_pairs={{0,4},{4,0},{1,5},{5,1},{2,6},{6,2},{3,7},{7,3},{8,12},{12,8},{9,1... | collective-permute-start | bytes 24584 | tf_op jit(solution)/shard_map/ppermute | solution.py:48
  61.1 1.3 %copy-start.4 = (f32[128,4096]{1,0:T(8,128)}, f32[128,4096]{1,0:T(8,128)S(1)}, u32[]{:S(2)}) copy-start(f32[128,4096]{1,0:T(8,128)S(1)} %get-tuple-element.98.plan) | copy-start | bytes 6291460
  74.7 8.4 %all-to-all-start.5 = ((f32[8,1,2304]{2,1,0:T(1,128)}), f32[8,1,2304]{2,1,0:T(1,128)S(1)}, u32[]{:S(2)}, u32[]{:S(2)}) async-start(f32[8,1,2304]{2,1,0:T(1,128)} %get-tuple-element.95), calls=%async_computation.5 | async-start | bytes 147456 | tf_op jit(solution)/shard_map/all_to_all | solution.py:25
  78.1 5.1 %collective-permute-start.5 = (f32[1,2048]{1,0:T(1,128)S(1)}, f32[1,2048]{1,0:T(1,128)S(1)}, u32[]{:S(2)}, u32[]{:S(2)}) collective-permute-start(f32[1,2048]{1,0:T(1,128)S(1)} %get-tuple-element.99.mine), channel_id=1, source_target_pairs={{0,4},{4,0},{1,5},{5,1},{2,6},{6,2},{3,7},{7,3},{8,12},{12,8},{9,1... | collective-permute-start | bytes 24584 | tf_op jit(solution)/shard_map/ppermute | solution.py:48
  83.2 1.6 %copy-start.5 = (f32[128,4096]{1,0:T(8,128)S(1)}, f32[128,4096]{1,0:T(8,128)}, u32[]{:S(2)}) copy-start(f32[128,4096]{1,0:T(8,128)} %copy-done.4) | copy-start | bytes 6291460
  85.4 1.5 %collective-permute-start.6 = (f32[1,2048]{1,0:T(1,128)S(1)}, f32[1,2048]{1,0:T(1,128)S(1)}, u32[]{:S(2)}, u32[]{:S(2)}) collective-permute-start(f32[1,2048]{1,0:T(1,128)S(1)} %get-tuple-element.107), channel_id=1, source_target_pairs={{0,4},{4,0},{1,5},{5,1},{2,6},{6,2},{3,7},{7,3},{8,12},{12,8},{9,1... | collective-permute-start | bytes 24584 | tf_op jit(solution)/shard_map/ppermute | solution.py:48
  98.3 7.1 %collective-permute-start.7 = (f32[1,2048]{1,0:T(1,128)S(1)}, f32[1,2048]{1,0:T(1,128)S(1)}, u32[]{:S(2)}, u32[]{:S(2)}) collective-permute-start(f32[1,2048]{1,0:T(1,128)S(1)} %shard_map.102.after.mine), channel_id=1, source_target_pairs={{0,4},{4,0},{1,5},{5,1},{2,6},{6,2},{3,7},{7,3},{8,12},{12,8},{9,1... | collective-permute-start | bytes 24584 | tf_op jit(solution)/shard_map/ppermute | solution.py:48
  98.5 2.4 %collective-permute-start.10 = (f32[1,128]{1,0:T(1,128)S(1)}, f32[1,128]{1,0:T(1,128)S(1)}, u32[]{:S(2)}, u32[]{:S(2)}) collective-permute-start(f32[1,128]{1,0:T(1,128)S(1)} %get-tuple-element.111.refs_0_), channel_id=1, source_target_pairs={{0,3},{1,0},{2,1},{3,2},{4,7},{5,4},{6,5},{7,6},{8,11},{9,8},{10,9... | collective-permute-start | bytes 1544 | tf_op jit(solution)/shard_map/ppermute | solution.py:414
  99.7 3.9 %collective-permute-start.9 = (f32[1,128]{1,0:T(1,128)S(1)}, f32[1,128]{1,0:T(1,128)S(1)}, u32[]{:S(2)}, u32[]{:S(2)}) collective-permute-start(f32[1,128]{1,0:T(1,128)S(1)} %get-tuple-element.111.refs_0_), channel_id=1, source_target_pairs={{0,2},{1,3},{2,0},{3,1},{4,6},{5,7},{6,4},{7,5},{8,10},{9,11},{10,... | collective-permute-start | bytes 1544 | tf_op jit(solution)/shard_map/ppermute | solution.py:414
  100.8 3.6 %collective-permute-start.8 = (f32[1,128]{1,0:T(1,128)S(1)}, f32[1,128]{1,0:T(1,128)S(1)}, u32[]{:S(2)}, u32[]{:S(2)}) collective-permute-start(f32[1,128]{1,0:T(1,128)S(1)} %get-tuple-element.111.refs_0_), channel_id=1, source_target_pairs={{0,1},{1,2},{2,3},{3,0},{4,5},{5,6},{6,7},{7,4},{8,9},{9,10},{10,1... | collective-permute-start | bytes 1544 | tf_op jit(solution)/shard_map/ppermute | solution.py:414

commit v10 on v9

--- a/solution.py
+++ b/solution.py
@@ -27,12 +27,16 @@
     )
 
 
+def turned(place, size):
+    return (4 * place + size) // (2 * size) % 2
+
+
 def crossed():
     sizes = [lax.axis_size(axis) for axis in WIDE]
     groups = []
     for side in range(sizes[2]):
         groups.append([
-            (a * sizes[1] + b) * sizes[2] + (side ^ (a * 2 // sizes[0]))
+            (a * sizes[1] + b) * sizes[2] + (side ^ turned(b, sizes[1]))
             for a in range(sizes[0])
             for b in range(sizes[1])
         ])
@@ -40,8 +44,7 @@
 
 
 def own_side():
-    upper = (lax.axis_index("wide_0") * 2) // lax.axis_size("wide_0")
-    return (lax.axis_index(CORE) + upper) % 2
+    return (lax.axis_index(CORE) + turned(lax.axis_index("wide_1"), lax.axis_size("wide_1"))) % 2
 
 
 def swap(array):
@@ -101,10 +104,10 @@
 
 def sweep(step, cost, plan, fresh_plan, row_all, col_dual, tiles, state, done):
     first, count = tiles
-    groups = len(state[0])
+    groups = row_all.shape[0] // GROUP
 
     def some(m, state):
-        rows, moved = list(state[0]), list(state[1])
+        rows, moved = (list(state[0]), list(state[1])) if state else ((), ())
         cols = [[None, None] for _ in range(WIDTH)]
         lanes = [span(first + WIDTH * m + w, 1) for w in range(WIDTH)]
         duals = [jnp.broadcast_to(col_dual[:, lanes[w]], (GROUP, LANES)) for w in range(WIDTH)]
@@ -118,17 +121,45 @@
                 change = fresh - old
                 extrap = fresh + change
                 fresh_plan[part, lanes[w]] = fresh
-                both = extrap if both is None else both + extrap
                 sums = cols[w]
                 sums[g % 2] = extrap if sums[g % 2] is None else sums[g % 2] + extrap
+                if state:
+                    both = extrap if both is None else both + extrap
+                    at = (g * WIDTH + w) % len(moved)
+                    moved[at] = moved[at] + change * change
+            if state:
+                rows[g] = rows[g] + both
+        for w in range(WIDTH):
+            done(WIDTH * m + w, first + WIDTH * m + w, down(cols[w][0] + cols[w][1]))
+        return tuple(rows), tuple(moved)
+
+    if state is None:
+        lax.fori_loop(0, count // WIDTH, lambda m, _: some(m, None) and 0, 0, unroll=True)
+        return None
+    return lax.fori_loop(0, count // WIDTH, some, state, unroll=True)
+
+
+def catch_up(plan, fresh_plan, tiles, state):
+    first, count = tiles
+    groups = len(state[0])
+
+    def some(m, state):
+        rows, moved = list(state[0]), list(state[1])
+        lanes = [span(first + WIDTH * m + w, 1) for w in range(WIDTH)]
+        for g in range(groups):
+            part = slice(g * GROUP, (g + 1) * GROUP)
+            both = None
+            for w in range(WIDTH):
+                fresh = fresh_plan[part, lanes[w]]
+                change = fresh - plan[part, lanes[w]]
+                extrap = fresh + change
+                both = extrap if both is None else both + extrap
                 at = (g * WIDTH + w) % len(moved)
                 moved[at] = moved[at] + change * change
             rows[g] = rows[g] + both
-        for w in range(WIDTH):
-            done(WIDTH * m + w, first + WIDTH * m + w, down(cols[w][0] + cols[w][1]))
         return tuple(rows), tuple(moved)
 
-    return lax.fori_loop(0, count // WIDTH, some, state)
+    return lax.fori_loop(0, count // WIDTH, some, state, unroll=True)
 
 
 def spread_rows(row_dual, row_all):
@@ -160,7 +191,7 @@
 def open_kernel(sizes, *refs):
     _, base, half, chips = sizes
     sources, targets = refs[:6], refs[6:12]
-    fresh_plan, give, row_sums, moved_sums, row_all, weight, sems = refs[12:]
+    fresh_plan, give, row_all, weight, sems = refs[12:]
     cost, plan, _, col_mass, row_dual, col_dual = targets
     own = own_side()
     tiles = half // CHUNKS
@@ -181,45 +212,36 @@
     for copy in small:
         copy.wait()
     spread_rows(row_dual[...], row_all)
-    state = zeros(row_all)
     put = into(give, col_mass, 2 * chips)
     for k in range(CHUNKS):
         big[2 * k].wait()
         big[2 * k + 1].wait()
         shift = k * tiles
-        state = sweep(
+        sweep(
             jnp.float32(1.0), cost, plan, fresh_plan, row_all, col_dual,
-            ((1 - own) * half + shift, tiles), state,
+            ((1 - own) * half + shift, tiles), None,
             lambda n, j, cols, shift=shift: put(n + shift, j, cols),
         )
-    hold(state, row_sums, moved_sums)
     for copy in big[2 * CHUNKS :]:
         copy.wait()
 
 
-def hold(state, row_sums, moved_sums):
-    row_sums[...] = jnp.concatenate(state[0], axis=0)
-    for n in range(MOVED):
-        moved_sums[n] = state[1][n]
-
-
 def give_kernel(
     sizes, mine, theirs, weight, new_weight, cost, plan, col_mass, row_all, col_dual,
-    fresh_plan, give, row_sums, moved_sums, new_col,
+    fresh_plan, give, new_col,
 ):
     _, base, half, chips = sizes
     col_update(mine, theirs, weight, col_dual, new_col, sizes)
     side = 1 - own_side()
-    state = sweep(
+    sweep(
         base / new_weight[...], cost, plan, fresh_plan, row_all, new_col, (side * half, half),
-        zeros(row_all), into(give, col_mass, 2 * chips),
-    )
-    hold(state, row_sums, moved_sums)
+        None, into(give, col_mass, 2 * chips),
+    )
 
 
 def keep_kernel(
-    sizes, weight, cost, plan, half_plan, row_mass, col_mass, row_all, col_dual, row_sums,
-    moved_sums, fresh_plan, keep, *last,
+    sizes, weight, cost, plan, half_plan, row_mass, col_mass, row_all, col_dual,
+    fresh_plan, keep, *last,
 ):
     _, base, half, chips = sizes
     side = own_side()
@@ -229,11 +251,7 @@
         lanes = span((1 - side) * half, half)
         copy = pltpu.make_async_copy(fresh_plan.at[:, lanes], plan_out.at[:, lanes], sem)
         copy.start()
-    rows = row_sums[...]
-    groups = row_all.shape[0] // GROUP
-    state = tuple(rows[g * GROUP : (g + 1) * GROUP] for g in range(groups)), tuple(
-        moved_sums[n] for n in range(MOVED)
-    )
+    state = catch_up(plan, fresh_plan, ((1 - side) * half, half), zeros(row_all))
     state = sweep(
         base / weight[...], cost, plan, fresh_plan, row_all, col_dual, (side * half, half), state,
         into(keep, col_mass, 2 * chips),
@@ -335,7 +353,6 @@
     spread = vm(rows, LANES)
 
     work = pl.CostEstimate(flops=6 * rows * cols, bytes_accessed=0, transcendentals=0)
-    sums = vm(MOVED, GROUP, LANES)
 
     whole = jax.ShapeDtypeStruct((rows, cols), jnp.float32)
 
@@ -367,19 +384,18 @@
     inputs = (cost, plan, row_mass, col_mass, row_dual, col_dual)
     outputs = pl.pallas_call(
         functools.partial(open_kernel, sizes),
-        out_shape=(big, big, one, many, one, many, big, give, spread, sums, spread, state),
+        out_shape=(big, big, one, many, one, many, big, give, spread, state),
         in_specs=[HB] * 6,
-        out_specs=(VM,) * 12,
+        out_specs=(VM,) * 10,
         scratch_shapes=[pltpu.SemaphoreType.DMA((6, CHUNKS + 1))],
         compiler_params=ROOM,
         cost_estimate=work,
         name="open_step",
     )(*(pltpu.with_memory_space_constraint(array, pltpu.HBM) for array in inputs))
     cost, plan, row_mass, col_mass, row_dual, col_dual = outputs[:6]
-    half_plan, given, row_sums, moved_sums, row_all, weight = outputs[6:]
+    half_plan, given, row_all, weight = outputs[6:]
     plan, kept = keep_step(
-        False, weight, cost, plan, half_plan, row_mass, col_mass, row_all, col_dual, row_sums,
-        moved_sums,
+        False, weight, cost, plan, half_plan, row_mass, col_mass, row_all, col_dual
     )
     own = functools.partial
     for step in range(1, ITERS):
@@ -396,15 +412,15 @@
             own(collect_kernel, sizes), (state, one, spread),
             got, weight, row_dual, scratch_shapes=[vm(2, 1, chips * LANES)],
         )
-        half_plan, given, row_sums, moved_sums, col_dual = call(
-            own(give_kernel, sizes), (big, give, spread, sums, many),
+        half_plan, given, col_dual = call(
+            own(give_kernel, sizes), (big, give, many),
             mine, theirs, weight, new_weight, cost, plan, col_mass, row_all, col_dual,
             cost_estimate=work,
         )
         weight = new_weight
         plan, kept, *tail_parts = keep_step(
             step == ITERS - 1, weight, cost, plan, half_plan, row_mass, col_mass, row_all,
-            col_dual, row_sums, moved_sums,
+            col_dual,
         )
     row_sent, plan_part = tail_parts
     came = swap(given)

time: 107 us -> 106 us (level)
  blocking collectives: 49.6 us -> 47.2 us
    all_to_all x4, blocking collectives: 49.6 us -> 47.2 us  [exchange(): lax.all_to_all(array, axes, split_axis=0, concat_axis=0, tiled=True, axis...]
  transfers between devices with their start and end apart: 14 -> 14, of which waited for: 6 -> 6; matrix products, arithmetic and copies ran while one was open for 0% -> 0% of each run, Pallas kernels for 4% -> 5%
where the time goes in v10:
time: 106 us; the launch traced here: 105 us
  blocking collectives  47.2 us (45%)
  starting transfers between devices  18.2 us (17%)
  waiting for transfers between devices  18.2 us (17%)
  Pallas kernels  11.8 us (11%)
  local copies, waits for them, and re-layouts  8.7 us (8%)
    all_to_all x4, blocking collectives, exchange(): lax.all_to_all(array, axes, split_axis=0, concat_axis=0, tiled=True, axis...  47.2 us
    all_to_all x3, waiting for transfers between devices, exchange(): lax.all_to_all(array, axes, split_axis=0, concat_axis=0, tiled=True, axis...  14.6 us
    all_to_all x3, starting transfers between devices, exchange(): lax.all_to_all(array, axes, split_axis=0, concat_axis=0, tiled=True, axis...  12.2 us
    pallas_call x21, Pallas kernels, call(): pl.pallas_call(kernel, out_shape=out_shape, in_specs=[HB if o in held els...  9.38 us
    unnamed x12, local copies, waits for them, and re-layouts  8.7 us
    ppermute x8, starting transfers between devices, swap(): return lax.ppermute(array, CORE, [(0, 1), (1, 0)])  3.69 us
    ppermute x3, waiting for transfers between devices, shards(): lax.ppermute(row_sent, 'narrow', [(n, (n + k) % narrow) for n in range(na...  3.63 us
    pallas_call x1, Pallas kernels, shards(): pl.pallas_call(functools.partial(open_kernel, sizes), out_shape=(big, big...  2.41 us
  transfers between devices with their start and end apart: 14, of which 6 were waited for; matrix products, arithmetic and copies ran while one was open for 0% of the time, Pallas kernels for 5%

profile of v10, /device:TPU:1, one launch (start us, length us, event | category | flops | bytes accessed | tf_op | source)
XLA Modules:
  0.0 104.9 jit_solution(4543345270429891629)
XLA Ops:
  0.6 2.4 %open_step.1 = (f32[128,4096]{1,0:T(8,128)S(1)}, f32[128,4096]{1,0:T(8,128)S(1)}, f32[1,128]{1,0:T(1,128)S(1)}, f32[1,4096]{1,0:T(1,128)S(1)}, f32[1,128]{1,0:T(...) custom-call(f32[128,4096]{1,0:T(8,128)} %refs_0_.1, ...), custom_call_target="tpu_custom_call" | custom-call | flops 3145728 | tf_op jit(solution)/shard_map/open_step/pallas_call | solution.py:385
  3.0 1.5 %collective-permute-start = (f32[1,2048]{1,0:T(1,128)S(1)}, f32[1,2048]{1,0:T(1,128)S(1)}, u32[]{:S(2)}, u32[]{:S(2)}) collective-permute-start(f32[1,2048]{1,0:T(1,128)S(1)} %get-tuple-element.60), channel_id=1, source_target_pairs={{0,4},{4,0},{1,5},{5,1},{2,6},{6,2},{3,7},{7,3},{8,12},{12,8},{9,1... | collective-permute-start | bytes 24584 | tf_op jit(solution)/shard_map/ppermute | solution.py:51
  4.5 0.8 shard_map.85
  5.3 1.3 %copy-done = f32[128,4096]{1,0:T(8,128)} copy-done((f32[128,4096]{1,0:T(8,128)}, f32[128,4096]{1,0:T(8,128)S(1)}, u32[]{:S(2)}) %copy-start) | copy-done | bytes 2097176
  6.6 15.3 %all_to_all.35.got = f32[16,1,2304]{2,1,0:T(1,128)S(1)} all-to-all(f32[16,1,2304]{2,1,0:T(1,128)S(1)} %shard_map.86), channel_id=1, replica_groups={{0,12,20,24,32,44,52,56,64,76,84,88,96,108,116,120},{4,8,16,28,36,40,48..., dimensions={0} | all-to-all | bytes 294912 | tf_op jit(solution)/shard_map/all_to_all | solution.py:25
  21.9 0.7 shard_map.87
  22.6 4.9 %all-to-all-start.1 = ((f32[8,1,2304]{2,1,0:T(1,128)}), f32[8,1,2304]{2,1,0:T(1,128)S(1)}, u32[]{:S(2)}, u32[]{:S(2)}) async-start(f32[8,1,2304]{2,1,0:T(1,128)} %get-tuple-element.61), calls=%async_computation.1 | async-start | bytes 147456 | tf_op jit(solution)/shard_map/all_to_all | solution.py:25
  27.5 0.0 collective-permute-start.1
  27.5 5.0 %all-to-all-done.1.got = f32[8,1,2304]{2,1,0:T(1,128)S(1)} async-done(((f32[8,1,2304]{2,1,0:T(1,128)}), f32[8,1,2304]{2,1,0:T(1,128)S(1)}, u32[]{:S(2)}, u32[]{:S(2)}) %all-to-all-start.1) | async-done | bytes 73760 | tf_op jit(solution)/shard_map/all_to_all | solution.py:25
  32.4 0.1 shard_map.88
  32.6 0.0 copy-start.1
  32.6 1.6 %copy-done.1 = f32[128,4096]{1,0:T(8,128)S(1)} copy-done((f32[128,4096]{1,0:T(8,128)S(1)}, f32[128,4096]{1,0:T(8,128)}, u32[]{:S(2)}) %copy-start.1) | copy-done | bytes 2097176
  34.2 0.4 shard_map.89
  34.6 0.5 collective-permute-start.2
  35.1 0.8 shard_map.90
  35.8 1.3 %copy-done.2 = f32[128,4096]{1,0:T(8,128)} copy-done((f32[128,4096]{1,0:T(8,128)}, f32[128,4096]{1,0:T(8,128)S(1)}, u32[]{:S(2)}) %copy-start.2) | copy-done | bytes 2097176
  37.2 10.7 %all_to_all.36.got = f32[16,1,2304]{2,1,0:T(1,128)S(1)} all-to-all(f32[16,1,2304]{2,1,0:T(1,128)S(1)} %shard_map.91), channel_id=1, replica_groups={{0,12,20,24,32,44,52,56,64,76,84,88,96,108,116,120},{4,8,16,28,36,40,48..., dimensions={0} | all-to-all | bytes 294912 | tf_op jit(solution)/shard_map/all_to_all | solution.py:25
  47.8 0.7 shard_map.92
  48.5 3.7 %all-to-all-start.3 = ((f32[8,1,2304]{2,1,0:T(1,128)}), f32[8,1,2304]{2,1,0:T(1,128)S(1)}, u32[]{:S(2)}, u32[]{:S(2)}) async-start(f32[8,1,2304]{2,1,0:T(1,128)} %get-tuple-element.71), calls=%async_computation.3 | async-start | bytes 147456 | tf_op jit(solution)/shard_map/all_to_all | solution.py:25
  52.2 0.2 collective-permute-start.3
  52.3 4.8 %all-to-all-done.3.got = f32[8,1,2304]{2,1,0:T(1,128)S(1)} async-done(((f32[8,1,2304]{2,1,0:T(1,128)}), f32[8,1,2304]{2,1,0:T(1,128)S(1)}, u32[]{:S(2)}, u32[]{:S(2)}) %all-to-all-start.3) | async-done | bytes 73760 | tf_op jit(solution)/shard_map/all_to_all | solution.py:25
  57.1 0.1 shard_map.93
  57.3 0.0 copy-start.3
  57.3 1.6 %copy-done.3 = f32[128,4096]{1,0:T(8,128)S(1)} copy-done((f32[128,4096]{1,0:T(8,128)S(1)}, f32[128,4096]{1,0:T(8,128)}, u32[]{:S(2)}) %copy-start.3) | copy-done | bytes 2097176
  58.9 0.4 shard_map.94
  59.3 0.5 collective-permute-start.4
  59.8 0.8 shard_map.95
  60.6 1.3 %copy-done.4 = f32[128,4096]{1,0:T(8,128)} copy-done((f32[128,4096]{1,0:T(8,128)}, f32[128,4096]{1,0:T(8,128)S(1)}, u32[]{:S(2)}) %copy-start.4) | copy-done | bytes 2097176
  61.9 10.7 %all_to_all.37.got = f32[16,1,2304]{2,1,0:T(1,128)S(1)} all-to-all(f32[16,1,2304]{2,1,0:T(1,128)S(1)} %shard_map.96), channel_id=1, replica_groups={{0,12,20,24,32,44,52,56,64,76,84,88,96,108,116,120},{4,8,16,28,36,40,48..., dimensions={0} | all-to-all | bytes 294912 | tf_op jit(solution)/shard_map/all_to_all | solution.py:25
  72.5 0.7 shard_map.97
  73.2 3.7 %all-to-all-start.5 = ((f32[8,1,2304]{2,1,0:T(1,128)}), f32[8,1,2304]{2,1,0:T(1,128)S(1)}, u32[]{:S(2)}, u32[]{:S(2)}) async-start(f32[8,1,2304]{2,1,0:T(1,128)} %get-tuple-element.81), calls=%async_computation.5 | async-start | bytes 147456 | tf_op jit(solution)/shard_map/all_to_all | solution.py:25
  76.9 0.2 collective-permute-start.5
  77.1 4.8 %all-to-all-done.5.got = f32[8,1,2304]{2,1,0:T(1,128)S(1)} async-done(((f32[8,1,2304]{2,1,0:T(1,128)}), f32[8,1,2304]{2,1,0:T(1,128)S(1)}, u32[]{:S(2)}, u32[]{:S(2)}) %all-to-all-start.5) | async-done | bytes 73760 | tf_op jit(solution)/shard_map/all_to_all | solution.py:25
  81.9 0.1 shard_map.98
  82.0 0.0 copy-start.5
  82.0 1.6 %copy-done.5 = f32[128,4096]{1,0:T(8,128)S(1)} copy-done((f32[128,4096]{1,0:T(8,128)S(1)}, f32[128,4096]{1,0:T(8,128)}, u32[]{:S(2)}) %copy-start.5) | copy-done | bytes 2097176
  83.6 0.4 shard_map.99
  84.0 0.5 collective-permute-start.6
  84.5 1.7 %shard_map.100 = (f32[128,4096]{1,0:T(8,128)S(1)}, f32[1,2304]{1,0:T(1,128)S(1)}, f32[1,128]{1,0:T(1,128)S(1)}, f32[128,4096]{1,0:T(8,128)}) custom-call(f32[8,128]{1,0:T(8,128)S(1)} %get-tuple-element.83.new_weight.weight, f32[128,4096]{1,0:T(8,128)S(1)} %get-tuple-element.52.cost, f32[128,4096]{1,0:T(8,128)S(1)} %copy-done.5, ...), custom_call_target="tpu_custom_call", output_to_operand_aliasing={{0}: (3, {})} | custom-call | flops 3145728 | tf_op jit(solution)/shard_map/pallas_call | solution.py:364
  86.2 10.6 %all_to_all.38.got = f32[16,1,2048]{2,1,0:T(1,128)S(1)} all-to-all(f32[16,1,2048]{2,1,0:T(1,128)S(1)} %shard_map.101), channel_id=1, replica_groups={{0,12,20,24,32,44,52,56,64,76,84,88,96,108,116,120},{4,8,16,28,36,40,48..., dimensions={0} | all-to-all | bytes 262144 | tf_op jit(solution)/shard_map/all_to_all | solution.py:25
  96.8 0.5 collective-permute-start.7
  97.3 1.2 %collective-permute-start.10 = (f32[1,128]{1,0:T(1,128)S(1)}, f32[1,128]{1,0:T(1,128)S(1)}, u32[]{:S(2)}, u32[]{:S(2)}) collective-permute-start(f32[1,128]{1,0:T(1,128)S(1)} %get-tuple-element.95.refs_0_), channel_id=1, source_target_pairs={{0,3},{1,0},{2,1},{3,2},{4,7},{5,4},{6,5},{7,6},{8,11},{9,8},{10,9... | collective-permute-start | bytes 1544 | tf_op jit(solution)/shard_map/ppermute | solution.py:430
  98.5 1.1 %collective-permute-start.9 = (f32[1,128]{1,0:T(1,128)S(1)}, f32[1,128]{1,0:T(1,128)S(1)}, u32[]{:S(2)}, u32[]{:S(2)}) collective-permute-start(f32[1,128]{1,0:T(1,128)S(1)} %get-tuple-element.95.refs_0_), channel_id=1, source_target_pairs={{0,2},{1,3},{2,0},{3,1},{4,6},{5,7},{6,4},{7,5},{8,10},{9,11},{10,... | collective-permute-start | bytes 1544 | tf_op jit(solution)/shard_map/ppermute | solution.py:430
  99.6 0.1 collective-permute-done.10.refs_3_
  99.7 2.7 %collective-permute-done.9.refs_2_ = f32[1,128]{1,0:T(1,128)S(1)} collective-permute-done((f32[1,128]{1,0:T(1,128)S(1)}, f32[1,128]{1,0:T(1,128)S(1)}, u32[]{:S(2)}, u32[]{:S(2)}) %collective-permute-start.9) | collective-permute-done | bytes 544 | tf_op jit(solution)/shard_map/ppermute | solution.py:430
  102.4 0.8 collective-permute-done.8.refs_1_
  103.2 1.0 shard_map.103
  104.2 0.7 shard_map.105
  (18 shorter events, 0.1 us)
Async XLA Ops:
  3.0 3.5 %collective-permute-start = (f32[1,2048]{1,0:T(1,128)S(1)}, f32[1,2048]{1,0:T(1,128)S(1)}, u32[]{:S(2)}, u32[]{:S(2)}) collective-permute-start(f32[1,2048]{1,0:T(1,128)S(1)} %get-tuple-element.60), channel_id=1, source_target_pairs={{0,4},{4,0},{1,5},{5,1},{2,6},{6,2},{3,7},{7,3},{8,12},{12,8},{9,1... | collective-permute-start | bytes 24584 | tf_op jit(solution)/shard_map/ppermute | solution.py:51
  5.3 1.3 %copy-start = (f32[128,4096]{1,0:T(8,128)}, f32[128,4096]{1,0:T(8,128)S(1)}, u32[]{:S(2)}) copy-start(f32[128,4096]{1,0:T(8,128)S(1)} %get-tuple-element.64.plan) | copy-start | bytes 6291460
  22.6 9.8 %all-to-all-start.1 = ((f32[8,1,2304]{2,1,0:T(1,128)}), f32[8,1,2304]{2,1,0:T(1,128)S(1)}, u32[]{:S(2)}, u32[]{:S(2)}) async-start(f32[8,1,2304]{2,1,0:T(1,128)} %get-tuple-element.61), calls=%async_computation.1 | async-start | bytes 147456 | tf_op jit(solution)/shard_map/all_to_all | solution.py:25
  27.5 5.1 %collective-permute-start.1 = (f32[1,2048]{1,0:T(1,128)S(1)}, f32[1,2048]{1,0:T(1,128)S(1)}, u32[]{:S(2)}, u32[]{:S(2)}) collective-permute-start(f32[1,2048]{1,0:T(1,128)S(1)} %get-tuple-element.65.mine), channel_id=1, source_target_pairs={{0,4},{4,0},{1,5},{5,1},{2,6},{6,2},{3,7},{7,3},{8,12},{12,8},{9,1... | collective-permute-start | bytes 24584 | tf_op jit(solution)/shard_map/ppermute | solution.py:51
  32.6 1.6 %copy-start.1 = (f32[128,4096]{1,0:T(8,128)S(1)}, f32[128,4096]{1,0:T(8,128)}, u32[]{:S(2)}) copy-start(f32[128,4096]{1,0:T(8,128)} %copy-done) | copy-start | bytes 6291460
  34.6 2.5 %collective-permute-start.2 = (f32[1,2048]{1,0:T(1,128)S(1)}, f32[1,2048]{1,0:T(1,128)S(1)}, u32[]{:S(2)}, u32[]{:S(2)}) collective-permute-start(f32[1,2048]{1,0:T(1,128)S(1)} %get-tuple-element.70), channel_id=1, source_target_pairs={{0,4},{4,0},{1,5},{5,1},{2,6},{6,2},{3,7},{7,3},{8,12},{12,8},{9,1... | collective-permute-start | bytes 24584 | tf_op jit(solution)/shard_map/ppermute | solution.py:51
  35.8 1.3 %copy-start.2 = (f32[128,4096]{1,0:T(8,128)}, f32[128,4096]{1,0:T(8,128)S(1)}, u32[]{:S(2)}) copy-start(f32[128,4096]{1,0:T(8,128)S(1)} %get-tuple-element.74.plan) | copy-start | bytes 6291460
  48.5 8.6 %all-to-all-start.3 = ((f32[8,1,2304]{2,1,0:T(1,128)}), f32[8,1,2304]{2,1,0:T(1,128)S(1)}, u32[]{:S(2)}, u32[]{:S(2)}) async-start(f32[8,1,2304]{2,1,0:T(1,128)} %get-tuple-element.71), calls=%async_computation.3 | async-start | bytes 147456 | tf_op jit(solution)/shard_map/all_to_all | solution.py:25
  52.2 5.1 %collective-permute-start.3 = (f32[1,2048]{1,0:T(1,128)S(1)}, f32[1,2048]{1,0:T(1,128)S(1)}, u32[]{:S(2)}, u32[]{:S(2)}) collective-permute-start(f32[1,2048]{1,0:T(1,128)S(1)} %get-tuple-element.75.mine), channel_id=1, source_target_pairs={{0,4},{4,0},{1,5},{5,1},{2,6},{6,2},{3,7},{7,3},{8,12},{12,8},{9,1... | collective-permute-start | bytes 24584 | tf_op jit(solution)/shard_map/ppermute | solution.py:51
  57.3 1.6 %copy-start.3 = (f32[128,4096]{1,0:T(8,128)S(1)}, f32[128,4096]{1,0:T(8,128)}, u32[]{:S(2)}) copy-start(f32[128,4096]{1,0:T(8,128)} %copy-done.2) | copy-start | bytes 6291460
  59.3 2.5 %collective-permute-start.4 = (f32[1,2048]{1,0:T(1,128)S(1)}, f32[1,2048]{1,0:T(1,128)S(1)}, u32[]{:S(2)}, u32[]{:S(2)}) collective-permute-start(f32[1,2048]{1,0:T(1,128)S(1)} %get-tuple-element.80), channel_id=1, source_target_pairs={{0,4},{4,0},{1,5},{5,1},{2,6},{6,2},{3,7},{7,3},{8,12},{12,8},{9,1... | collective-permute-start | bytes 24584 | tf_op jit(solution)/shard_map/ppermute | solution.py:51
  60.5 1.3 %copy-start.4 = (f32[128,4096]{1,0:T(8,128)}, f32[128,4096]{1,0:T(8,128)S(1)}, u32[]{:S(2)}) copy-start(f32[128,4096]{1,0:T(8,128)S(1)} %get-tuple-element.84.plan) | copy-start | bytes 6291460
  73.2 8.6 %all-to-all-start.5 = ((f32[8,1,2304]{2,1,0:T(1,128)}), f32[8,1,2304]{2,1,0:T(1,128)S(1)}, u32[]{:S(2)}, u32[]{:S(2)}) async-start(f32[8,1,2304]{2,1,0:T(1,128)} %get-tuple-element.81), calls=%async_computation.5 | async-start | bytes 147456 | tf_op jit(solution)/shard_map/all_to_all | solution.py:25
  76.9 5.1 %collective-permute-start.5 = (f32[1,2048]{1,0:T(1,128)S(1)}, f32[1,2048]{1,0:T(1,128)S(1)}, u32[]{:S(2)}, u32[]{:S(2)}) collective-permute-start(f32[1,2048]{1,0:T(1,128)S(1)} %get-tuple-element.85.mine), channel_id=1, source_target_pairs={{0,4},{4,0},{1,5},{5,1},{2,6},{6,2},{3,7},{7,3},{8,12},{12,8},{9,1... | collective-permute-start | bytes 24584 | tf_op jit(solution)/shard_map/ppermute | solution.py:51
  82.0 1.6 %copy-start.5 = (f32[128,4096]{1,0:T(8,128)S(1)}, f32[128,4096]{1,0:T(8,128)}, u32[]{:S(2)}) copy-start(f32[128,4096]{1,0:T(8,128)} %copy-done.4) | copy-start | bytes 6291460
  84.0 2.2 %collective-permute-start.6 = (f32[1,2048]{1,0:T(1,128)S(1)}, f32[1,2048]{1,0:T(1,128)S(1)}, u32[]{:S(2)}, u32[]{:S(2)}) collective-permute-start(f32[1,2048]{1,0:T(1,128)S(1)} %get-tuple-element.91), channel_id=1, source_target_pairs={{0,4},{4,0},{1,5},{5,1},{2,6},{6,2},{3,7},{7,3},{8,12},{12,8},{9,1... | collective-permute-start | bytes 24584 | tf_op jit(solution)/shard_map/ppermute | solution.py:51
  96.8 7.4 %collective-permute-start.7 = (f32[1,2048]{1,0:T(1,128)S(1)}, f32[1,2048]{1,0:T(1,128)S(1)}, u32[]{:S(2)}, u32[]{:S(2)}) collective-permute-start(f32[1,2048]{1,0:T(1,128)S(1)} %shard_map.102.after.mine), channel_id=1, source_target_pairs={{0,4},{4,0},{1,5},{5,1},{2,6},{6,2},{3,7},{7,3},{8,12},{12,8},{9,1... | collective-permute-start | bytes 24584 | tf_op jit(solution)/shard_map/ppermute | solution.py:51
  97.3 2.4 %collective-permute-start.10 = (f32[1,128]{1,0:T(1,128)S(1)}, f32[1,128]{1,0:T(1,128)S(1)}, u32[]{:S(2)}, u32[]{:S(2)}) collective-permute-start(f32[1,128]{1,0:T(1,128)S(1)} %get-tuple-element.95.refs_0_), channel_id=1, source_target_pairs={{0,3},{1,0},{2,1},{3,2},{4,7},{5,4},{6,5},{7,6},{8,11},{9,8},{10,9... | collective-permute-start | bytes 1544 | tf_op jit(solution)/shard_map/ppermute | solution.py:430
  98.5 3.9 %collective-permute-start.9 = (f32[1,128]{1,0:T(1,128)S(1)}, f32[1,128]{1,0:T(1,128)S(1)}, u32[]{:S(2)}, u32[]{:S(2)}) collective-permute-start(f32[1,128]{1,0:T(1,128)S(1)} %get-tuple-element.95.refs_0_), channel_id=1, source_target_pairs={{0,2},{1,3},{2,0},{3,1},{4,6},{5,7},{6,4},{7,5},{8,10},{9,11},{10,... | collective-permute-start | bytes 1544 | tf_op jit(solution)/shard_map/ppermute | solution.py:430
  99.6 3.6 %collective-permute-start.8 = (f32[1,128]{1,0:T(1,128)S(1)}, f32[1,128]{1,0:T(1,128)S(1)}, u32[]{:S(2)}, u32[]{:S(2)}) collective-permute-start(f32[1,128]{1,0:T(1,128)S(1)} %get-tuple-element.95.refs_0_), channel_id=1, source_target_pairs={{0,1},{1,2},{2,3},{3,0},{4,5},{5,6},{6,7},{7,4},{8,9},{9,10},{10,1... | collective-permute-start | bytes 1544 | tf_op jit(solution)/shard_map/ppermute | solution.py:430

commit v11 on v10

--- a/solution.py
+++ b/solution.py
@@ -36,15 +36,15 @@
     groups = []
     for side in range(sizes[2]):
         groups.append([
-            (a * sizes[1] + b) * sizes[2] + (side ^ turned(b, sizes[1]))
+            (a * sizes[1] + b) * sizes[2] + (side ^ turned(a, sizes[0]))
+            for b in range(sizes[1])
             for a in range(sizes[0])
-            for b in range(sizes[1])
         ])
     return groups
 
 
 def own_side():
-    return (lax.axis_index(CORE) + turned(lax.axis_index("wide_1"), lax.axis_size("wide_1"))) % 2
+    return (lax.axis_index(CORE) + turned(lax.axis_index("wide_0"), lax.axis_size("wide_0"))) % 2
 
 
 def swap(array):
@@ -70,7 +70,7 @@
 def collect_kernel(sizes, got, weight, row_dual, new_weight, new_row, row_all, rows_held):
     narrow, base, _, chips = sizes
     core = lax.axis_index(CORE)
-    place = lax.axis_index("wide_0") * lax.axis_size("wide_1") + lax.axis_index("wide_1")
+    place = lax.axis_index("wide_1") * lax.axis_size("wide_0") + lax.axis_index("wide_0")
     squares, rest = None, None
     for c in range(2):
         part = got[c * narrow]
@@ -102,7 +102,7 @@
         new_col[:, lanes] = col_dual[:, lanes] + scale * part[...]
 
 
-def sweep(step, cost, plan, fresh_plan, row_all, col_dual, tiles, state, done):
+def sweep(step, cost, plan, fresh_plan, row_all, col_dual, tiles, state, done, unroll=True):
     first, count = tiles
     groups = row_all.shape[0] // GROUP
 
@@ -134,12 +134,12 @@
         return tuple(rows), tuple(moved)
 
     if state is None:
-        lax.fori_loop(0, count // WIDTH, lambda m, _: some(m, None) and 0, 0, unroll=True)
+        lax.fori_loop(0, count // WIDTH, lambda m, _: some(m, None) and 0, 0, unroll=unroll)
         return None
-    return lax.fori_loop(0, count // WIDTH, some, state, unroll=True)
-
-
-def catch_up(plan, fresh_plan, tiles, state):
+    return lax.fori_loop(0, count // WIDTH, some, state, unroll=unroll)
+
+
+def catch_up(plan, fresh_plan, tiles, state, unroll=True):
     first, count = tiles
     groups = len(state[0])
 
@@ -159,7 +159,7 @@
             rows[g] = rows[g] + both
         return tuple(rows), tuple(moved)
 
-    return lax.fori_loop(0, count // WIDTH, some, state, unroll=True)
+    return lax.fori_loop(0, count // WIDTH, some, state, unroll=unroll)
 
 
 def spread_rows(row_dual, row_all):
@@ -251,10 +251,10 @@
         lanes = span((1 - side) * half, half)
         copy = pltpu.make_async_copy(fresh_plan.at[:, lanes], plan_out.at[:, lanes], sem)
         copy.start()
-    state = catch_up(plan, fresh_plan, ((1 - side) * half, half), zeros(row_all))
+    state = catch_up(plan, fresh_plan, ((1 - side) * half, half), zeros(row_all), not last)
     state = sweep(
         base / weight[...], cost, plan, fresh_plan, row_all, col_dual, (side * half, half), state,
-        into(keep, col_mass, 2 * chips),
+        into(keep, col_mass, 2 * chips), not last,
     )
     tail(keep, row_mass, state, sizes)
     if last:

time: 106 us -> 105 us (level)
  transfers between devices with their start and end apart: 14 -> 14, of which waited for: 6 -> 6; matrix products, arithmetic and copies ran while one was open for 0% -> 0% of each run, Pallas kernels for 5% -> 4%
where the time goes in v11:
time: 105 us; the launch traced here: 104 us
  blocking collectives  46.9 us (45%)
  waiting for transfers between devices  18.2 us (17%)
  starting transfers between devices  17.8 us (17%)
  Pallas kernels  11.1 us (11%)
  local copies, waits for them, and re-layouts  8.7 us (8%)
    all_to_all x4, blocking collectives, exchange(): lax.all_to_all(array, axes, split_axis=0, concat_axis=0, tiled=True, axis...  46.9 us
    all_to_all x3, waiting for transfers between devices, exchange(): lax.all_to_all(array, axes, split_axis=0, concat_axis=0, tiled=True, axis...  14.6 us
    all_to_all x3, starting transfers between devices, exchange(): lax.all_to_all(array, axes, split_axis=0, concat_axis=0, tiled=True, axis...  12 us
    pallas_call x21, Pallas kernels, call(): pl.pallas_call(kernel, out_shape=out_shape, in_specs=[HB if o in held els...  8.71 us
    unnamed x12, local copies, waits for them, and re-layouts  8.7 us
    ppermute x3, waiting for transfers between devices, shards(): lax.ppermute(row_sent, 'narrow', [(n, (n + k) % narrow) for n in range(na...  3.63 us
    ppermute x8, starting transfers between devices, swap(): return lax.ppermute(array, CORE, [(0, 1), (1, 0)])  3.5 us
    pallas_call x1, Pallas kernels, shards(): pl.pallas_call(functools.partial(open_kernel, sizes), out_shape=(big, big...  2.41 us
  transfers between devices with their start and end apart: 14, of which 6 were waited for; matrix products, arithmetic and copies ran while one was open for 0% of the time, Pallas kernels for 4%

profile of v11, /device:TPU:1, one launch (start us, length us, event | category | flops | bytes accessed | tf_op | source)
XLA Modules:
  0.0 103.5 jit_solution(5187746922088273221)
XLA Ops:
  0.6 2.4 %open_step.1 = (f32[128,4096]{1,0:T(8,128)S(1)}, f32[128,4096]{1,0:T(8,128)S(1)}, f32[1,128]{1,0:T(1,128)S(1)}, f32[1,4096]{1,0:T(1,128)S(1)}, f32[1,128]{1,0:T(...) custom-call(f32[128,4096]{1,0:T(8,128)} %refs_0_.1, ...), custom_call_target="tpu_custom_call" | custom-call | flops 3145728 | tf_op jit(solution)/shard_map/open_step/pallas_call | solution.py:385
  3.0 1.5 %collective-permute-start = (f32[1,2048]{1,0:T(1,128)S(1)}, f32[1,2048]{1,0:T(1,128)S(1)}, u32[]{:S(2)}, u32[]{:S(2)}) collective-permute-start(f32[1,2048]{1,0:T(1,128)S(1)} %get-tuple-element.60), channel_id=1, source_target_pairs={{0,4},{4,0},{1,5},{5,1},{2,6},{6,2},{3,7},{7,3},{8,12},{12,8},{9,1... | collective-permute-start | bytes 24584 | tf_op jit(solution)/shard_map/ppermute | solution.py:51
  4.5 0.8 shard_map.85
  5.3 1.3 %copy-done = f32[128,4096]{1,0:T(8,128)} copy-done((f32[128,4096]{1,0:T(8,128)}, f32[128,4096]{1,0:T(8,128)S(1)}, u32[]{:S(2)}) %copy-start) | copy-done | bytes 2097176
  6.6 15.6 %all_to_all.35.got = f32[16,1,2304]{2,1,0:T(1,128)S(1)} all-to-all(f32[16,1,2304]{2,1,0:T(1,128)S(1)} %shard_map.86), channel_id=1, replica_groups={{0,36,68,96,8,44,76,104,16,52,84,112,24,60,92,120},{4,32,64,100,12,40,7..., dimensions={0} | all-to-all | bytes 294912 | tf_op jit(solution)/shard_map/all_to_all | solution.py:25
  22.2 0.7 shard_map.87
  22.9 4.9 %all-to-all-start.1 = ((f32[8,1,2304]{2,1,0:T(1,128)}), f32[8,1,2304]{2,1,0:T(1,128)S(1)}, u32[]{:S(2)}, u32[]{:S(2)}) async-start(f32[8,1,2304]{2,1,0:T(1,128)} %get-tuple-element.61), calls=%async_computation.1 | async-start | bytes 147456 | tf_op jit(solution)/shard_map/all_to_all | solution.py:25
  27.7 0.0 collective-permute-start.1
  27.7 5.0 %all-to-all-done.1.got = f32[8,1,2304]{2,1,0:T(1,128)S(1)} async-done(((f32[8,1,2304]{2,1,0:T(1,128)}), f32[8,1,2304]{2,1,0:T(1,128)S(1)}, u32[]{:S(2)}, u32[]{:S(2)}) %all-to-all-start.1) | async-done | bytes 73760 | tf_op jit(solution)/shard_map/all_to_all | solution.py:25
  32.7 0.1 shard_map.88
  32.8 0.0 copy-start.1
  32.8 1.6 %copy-done.1 = f32[128,4096]{1,0:T(8,128)S(1)} copy-done((f32[128,4096]{1,0:T(8,128)S(1)}, f32[128,4096]{1,0:T(8,128)}, u32[]{:S(2)}) %copy-start.1) | copy-done | bytes 2097176
  34.4 0.4 shard_map.89
  34.9 0.5 collective-permute-start.2
  35.3 0.8 shard_map.90
  36.1 1.3 %copy-done.2 = f32[128,4096]{1,0:T(8,128)} copy-done((f32[128,4096]{1,0:T(8,128)}, f32[128,4096]{1,0:T(8,128)S(1)}, u32[]{:S(2)}) %copy-start.2) | copy-done | bytes 2097176
  37.4 10.4 %all_to_all.36.got = f32[16,1,2304]{2,1,0:T(1,128)S(1)} all-to-all(f32[16,1,2304]{2,1,0:T(1,128)S(1)} %shard_map.91), channel_id=1, replica_groups={{0,36,68,96,8,44,76,104,16,52,84,112,24,60,92,120},{4,32,64,100,12,40,7..., dimensions={0} | all-to-all | bytes 294912 | tf_op jit(solution)/shard_map/all_to_all | solution.py:25
  47.8 0.7 shard_map.92
  48.5 3.4 %all-to-all-start.3 = ((f32[8,1,2304]{2,1,0:T(1,128)}), f32[8,1,2304]{2,1,0:T(1,128)S(1)}, u32[]{:S(2)}, u32[]{:S(2)}) async-start(f32[8,1,2304]{2,1,0:T(1,128)} %get-tuple-element.71), calls=%async_computation.3 | async-start | bytes 147456 | tf_op jit(solution)/shard_map/all_to_all | solution.py:25
  51.9 0.2 collective-permute-start.3
  52.1 4.8 %all-to-all-done.3.got = f32[8,1,2304]{2,1,0:T(1,128)S(1)} async-done(((f32[8,1,2304]{2,1,0:T(1,128)}), f32[8,1,2304]{2,1,0:T(1,128)S(1)}, u32[]{:S(2)}, u32[]{:S(2)}) %all-to-all-start.3) | async-done | bytes 73760 | tf_op jit(solution)/shard_map/all_to_all | solution.py:25
  56.9 0.1 shard_map.93
  57.0 0.0 copy-start.3
  57.0 1.6 %copy-done.3 = f32[128,4096]{1,0:T(8,128)S(1)} copy-done((f32[128,4096]{1,0:T(8,128)S(1)}, f32[128,4096]{1,0:T(8,128)}, u32[]{:S(2)}) %copy-start.3) | copy-done | bytes 2097176
  58.6 0.4 shard_map.94
  59.1 0.5 collective-permute-start.4
  59.5 0.8 shard_map.95
  60.3 1.3 %copy-done.4 = f32[128,4096]{1,0:T(8,128)} copy-done((f32[128,4096]{1,0:T(8,128)}, f32[128,4096]{1,0:T(8,128)S(1)}, u32[]{:S(2)}) %copy-start.4) | copy-done | bytes 2097176
  61.6 10.8 %all_to_all.37.got = f32[16,1,2304]{2,1,0:T(1,128)S(1)} all-to-all(f32[16,1,2304]{2,1,0:T(1,128)S(1)} %shard_map.96), channel_id=1, replica_groups={{0,36,68,96,8,44,76,104,16,52,84,112,24,60,92,120},{4,32,64,100,12,40,7..., dimensions={0} | all-to-all | bytes 294912 | tf_op jit(solution)/shard_map/all_to_all | solution.py:25
  72.4 0.7 shard_map.97
  73.1 3.7 %all-to-all-start.5 = ((f32[8,1,2304]{2,1,0:T(1,128)}), f32[8,1,2304]{2,1,0:T(1,128)S(1)}, u32[]{:S(2)}, u32[]{:S(2)}) async-start(f32[8,1,2304]{2,1,0:T(1,128)} %get-tuple-element.81), calls=%async_computation.5 | async-start | bytes 147456 | tf_op jit(solution)/shard_map/all_to_all | solution.py:25
  76.7 0.2 collective-permute-start.5
  76.9 4.8 %all-to-all-done.5.got = f32[8,1,2304]{2,1,0:T(1,128)S(1)} async-done(((f32[8,1,2304]{2,1,0:T(1,128)}), f32[8,1,2304]{2,1,0:T(1,128)S(1)}, u32[]{:S(2)}, u32[]{:S(2)}) %all-to-all-start.5) | async-done | bytes 73760 | tf_op jit(solution)/shard_map/all_to_all | solution.py:25
  81.7 0.1 shard_map.98
  81.8 0.0 copy-start.5
  81.9 1.6 %copy-done.5 = f32[128,4096]{1,0:T(8,128)S(1)} copy-done((f32[128,4096]{1,0:T(8,128)S(1)}, f32[128,4096]{1,0:T(8,128)}, u32[]{:S(2)}) %copy-start.5) | copy-done | bytes 2097176
  83.4 0.4 shard_map.99
  83.9 0.5 collective-permute-start.6
  84.4 1.0 shard_map.100
  85.4 10.2 %all_to_all.38.got = f32[16,1,2048]{2,1,0:T(1,128)S(1)} all-to-all(f32[16,1,2048]{2,1,0:T(1,128)S(1)} %shard_map.101), channel_id=1, replica_groups={{0,36,68,96,8,44,76,104,16,52,84,112,24,60,92,120},{4,32,64,100,12,40,7..., dimensions={0} | all-to-all | bytes 262144 | tf_op jit(solution)/shard_map/all_to_all | solution.py:25
  95.6 0.3 collective-permute-start.7
  95.9 1.2 %collective-permute-start.10 = (f32[1,128]{1,0:T(1,128)S(1)}, f32[1,128]{1,0:T(1,128)S(1)}, u32[]{:S(2)}, u32[]{:S(2)}) collective-permute-start(f32[1,128]{1,0:T(1,128)S(1)} %get-tuple-element.95.refs_0_), channel_id=1, source_target_pairs={{0,3},{1,0},{2,1},{3,2},{4,7},{5,4},{6,5},{7,6},{8,11},{9,8},{10,9... | collective-permute-start | bytes 1544 | tf_op jit(solution)/shard_map/ppermute | solution.py:430
  97.1 1.1 %collective-permute-start.9 = (f32[1,128]{1,0:T(1,128)S(1)}, f32[1,128]{1,0:T(1,128)S(1)}, u32[]{:S(2)}, u32[]{:S(2)}) collective-permute-start(f32[1,128]{1,0:T(1,128)S(1)} %get-tuple-element.95.refs_0_), channel_id=1, source_target_pairs={{0,2},{1,3},{2,0},{3,1},{4,6},{5,7},{6,4},{7,5},{8,10},{9,11},{10,... | collective-permute-start | bytes 1544 | tf_op jit(solution)/shard_map/ppermute | solution.py:430
  98.2 0.1 collective-permute-done.10.refs_3_
  98.3 2.7 %collective-permute-done.9.refs_2_ = f32[1,128]{1,0:T(1,128)S(1)} collective-permute-done((f32[1,128]{1,0:T(1,128)S(1)}, f32[1,128]{1,0:T(1,128)S(1)}, u32[]{:S(2)}, u32[]{:S(2)}) %collective-permute-start.9) | collective-permute-done | bytes 544 | tf_op jit(solution)/shard_map/ppermute | solution.py:430
  101.0 0.8 collective-permute-done.8.refs_1_
  101.8 1.0 shard_map.103
  102.8 0.7 shard_map.105
  (18 shorter events, 0.1 us)
Async XLA Ops:
  3.0 3.5 %collective-permute-start = (f32[1,2048]{1,0:T(1,128)S(1)}, f32[1,2048]{1,0:T(1,128)S(1)}, u32[]{:S(2)}, u32[]{:S(2)}) collective-permute-start(f32[1,2048]{1,0:T(1,128)S(1)} %get-tuple-element.60), channel_id=1, source_target_pairs={{0,4},{4,0},{1,5},{5,1},{2,6},{6,2},{3,7},{7,3},{8,12},{12,8},{9,1... | collective-permute-start | bytes 24584 | tf_op jit(solution)/shard_map/ppermute | solution.py:51
  5.3 1.3 %copy-start = (f32[128,4096]{1,0:T(8,128)}, f32[128,4096]{1,0:T(8,128)S(1)}, u32[]{:S(2)}) copy-start(f32[128,4096]{1,0:T(8,128)S(1)} %get-tuple-element.64.plan) | copy-start | bytes 6291460
  22.9 9.8 %all-to-all-start.1 = ((f32[8,1,2304]{2,1,0:T(1,128)}), f32[8,1,2304]{2,1,0:T(1,128)S(1)}, u32[]{:S(2)}, u32[]{:S(2)}) async-start(f32[8,1,2304]{2,1,0:T(1,128)} %get-tuple-element.61), calls=%async_computation.1 | async-start | bytes 147456 | tf_op jit(solution)/shard_map/all_to_all | solution.py:25
  27.7 5.1 %collective-permute-start.1 = (f32[1,2048]{1,0:T(1,128)S(1)}, f32[1,2048]{1,0:T(1,128)S(1)}, u32[]{:S(2)}, u32[]{:S(2)}) collective-permute-start(f32[1,2048]{1,0:T(1,128)S(1)} %get-tuple-element.65.mine), channel_id=1, source_target_pairs={{0,4},{4,0},{1,5},{5,1},{2,6},{6,2},{3,7},{7,3},{8,12},{12,8},{9,1... | collective-permute-start | bytes 24584 | tf_op jit(solution)/shard_map/ppermute | solution.py:51
  32.8 1.6 %copy-start.1 = (f32[128,4096]{1,0:T(8,128)S(1)}, f32[128,4096]{1,0:T(8,128)}, u32[]{:S(2)}) copy-start(f32[128,4096]{1,0:T(8,128)} %copy-done) | copy-start | bytes 6291460
  34.9 2.5 %collective-permute-start.2 = (f32[1,2048]{1,0:T(1,128)S(1)}, f32[1,2048]{1,0:T(1,128)S(1)}, u32[]{:S(2)}, u32[]{:S(2)}) collective-permute-start(f32[1,2048]{1,0:T(1,128)S(1)} %get-tuple-element.70), channel_id=1, source_target_pairs={{0,4},{4,0},{1,5},{5,1},{2,6},{6,2},{3,7},{7,3},{8,12},{12,8},{9,1... | collective-permute-start | bytes 24584 | tf_op jit(solution)/shard_map/ppermute | solution.py:51
  36.1 1.3 %copy-start.2 = (f32[128,4096]{1,0:T(8,128)}, f32[128,4096]{1,0:T(8,128)S(1)}, u32[]{:S(2)}) copy-start(f32[128,4096]{1,0:T(8,128)S(1)} %get-tuple-element.74.plan) | copy-start | bytes 6291460
  48.5 8.4 %all-to-all-start.3 = ((f32[8,1,2304]{2,1,0:T(1,128)}), f32[8,1,2304]{2,1,0:T(1,128)S(1)}, u32[]{:S(2)}, u32[]{:S(2)}) async-start(f32[8,1,2304]{2,1,0:T(1,128)} %get-tuple-element.71), calls=%async_computation.3 | async-start | bytes 147456 | tf_op jit(solution)/shard_map/all_to_all | solution.py:25
  51.9 5.1 %collective-permute-start.3 = (f32[1,2048]{1,0:T(1,128)S(1)}, f32[1,2048]{1,0:T(1,128)S(1)}, u32[]{:S(2)}, u32[]{:S(2)}) collective-permute-start(f32[1,2048]{1,0:T(1,128)S(1)} %get-tuple-element.75.mine), channel_id=1, source_target_pairs={{0,4},{4,0},{1,5},{5,1},{2,6},{6,2},{3,7},{7,3},{8,12},{12,8},{9,1... | collective-permute-start | bytes 24584 | tf_op jit(solution)/shard_map/ppermute | solution.py:51
  57.0 1.6 %copy-start.3 = (f32[128,4096]{1,0:T(8,128)S(1)}, f32[128,4096]{1,0:T(8,128)}, u32[]{:S(2)}) copy-start(f32[128,4096]{1,0:T(8,128)} %copy-done.2) | copy-start | bytes 6291460
  59.1 2.5 %collective-permute-start.4 = (f32[1,2048]{1,0:T(1,128)S(1)}, f32[1,2048]{1,0:T(1,128)S(1)}, u32[]{:S(2)}, u32[]{:S(2)}) collective-permute-start(f32[1,2048]{1,0:T(1,128)S(1)} %get-tuple-element.80), channel_id=1, source_target_pairs={{0,4},{4,0},{1,5},{5,1},{2,6},{6,2},{3,7},{7,3},{8,12},{12,8},{9,1... | collective-permute-start | bytes 24584 | tf_op jit(solution)/shard_map/ppermute | solution.py:51
  60.3 1.3 %copy-start.4 = (f32[128,4096]{1,0:T(8,128)}, f32[128,4096]{1,0:T(8,128)S(1)}, u32[]{:S(2)}) copy-start(f32[128,4096]{1,0:T(8,128)S(1)} %get-tuple-element.84.plan) | copy-start | bytes 6291460
  73.1 8.6 %all-to-all-start.5 = ((f32[8,1,2304]{2,1,0:T(1,128)}), f32[8,1,2304]{2,1,0:T(1,128)S(1)}, u32[]{:S(2)}, u32[]{:S(2)}) async-start(f32[8,1,2304]{2,1,0:T(1,128)} %get-tuple-element.81), calls=%async_computation.5 | async-start | bytes 147456 | tf_op jit(solution)/shard_map/all_to_all | solution.py:25
  76.7 5.1 %collective-permute-start.5 = (f32[1,2048]{1,0:T(1,128)S(1)}, f32[1,2048]{1,0:T(1,128)S(1)}, u32[]{:S(2)}, u32[]{:S(2)}) collective-permute-start(f32[1,2048]{1,0:T(1,128)S(1)} %get-tuple-element.85.mine), channel_id=1, source_target_pairs={{0,4},{4,0},{1,5},{5,1},{2,6},{6,2},{3,7},{7,3},{8,12},{12,8},{9,1... | collective-permute-start | bytes 24584 | tf_op jit(solution)/shard_map/ppermute | solution.py:51
  81.8 1.6 %copy-start.5 = (f32[128,4096]{1,0:T(8,128)S(1)}, f32[128,4096]{1,0:T(8,128)}, u32[]{:S(2)}) copy-start(f32[128,4096]{1,0:T(8,128)} %copy-done.4) | copy-start | bytes 6291460
  83.9 1.5 %collective-permute-start.6 = (f32[1,2048]{1,0:T(1,128)S(1)}, f32[1,2048]{1,0:T(1,128)S(1)}, u32[]{:S(2)}, u32[]{:S(2)}) collective-permute-start(f32[1,2048]{1,0:T(1,128)S(1)} %get-tuple-element.91), channel_id=1, source_target_pairs={{0,4},{4,0},{1,5},{5,1},{2,6},{6,2},{3,7},{7,3},{8,12},{12,8},{9,1... | collective-permute-start | bytes 24584 | tf_op jit(solution)/shard_map/ppermute | solution.py:51
  95.6 7.2 %collective-permute-start.7 = (f32[1,2048]{1,0:T(1,128)S(1)}, f32[1,2048]{1,0:T(1,128)S(1)}, u32[]{:S(2)}, u32[]{:S(2)}) collective-permute-start(f32[1,2048]{1,0:T(1,128)S(1)} %shard_map.102.after.mine), channel_id=1, source_target_pairs={{0,4},{4,0},{1,5},{5,1},{2,6},{6,2},{3,7},{7,3},{8,12},{12,8},{9,1... | collective-permute-start | bytes 24584 | tf_op jit(solution)/shard_map/ppermute | solution.py:51
  95.9 2.4 %collective-permute-start.10 = (f32[1,128]{1,0:T(1,128)S(1)}, f32[1,128]{1,0:T(1,128)S(1)}, u32[]{:S(2)}, u32[]{:S(2)}) collective-permute-start(f32[1,128]{1,0:T(1,128)S(1)} %get-tuple-element.95.refs_0_), channel_id=1, source_target_pairs={{0,3},{1,0},{2,1},{3,2},{4,7},{5,4},{6,5},{7,6},{8,11},{9,8},{10,9... | collective-permute-start | bytes 1544 | tf_op jit(solution)/shard_map/ppermute | solution.py:430
  97.1 3.9 %collective-permute-start.9 = (f32[1,128]{1,0:T(1,128)S(1)}, f32[1,128]{1,0:T(1,128)S(1)}, u32[]{:S(2)}, u32[]{:S(2)}) collective-permute-start(f32[1,128]{1,0:T(1,128)S(1)} %get-tuple-element.95.refs_0_), channel_id=1, source_target_pairs={{0,2},{1,3},{2,0},{3,1},{4,6},{5,7},{6,4},{7,5},{8,10},{9,11},{10,... | collective-permute-start | bytes 1544 | tf_op jit(solution)/shard_map/ppermute | solution.py:430
  98.2 3.6 %collective-permute-start.8 = (f32[1,128]{1,0:T(1,128)S(1)}, f32[1,128]{1,0:T(1,128)S(1)}, u32[]{:S(2)}, u32[]{:S(2)}) collective-permute-start(f32[1,128]{1,0:T(1,128)S(1)} %get-tuple-element.95.refs_0_), channel_id=1, source_target_pairs={{0,1},{1,2},{2,3},{3,0},{4,5},{5,6},{6,7},{7,4},{8,9},{9,10},{10,1... | collective-permute-start | bytes 1544 | tf_op jit(solution)/shard_map/ppermute | solution.py:430

commit v12 on v11

--- a/solution.py
+++ b/solution.py
@@ -13,8 +13,8 @@
 ITERS = 4
 LANES = 128
 GROUP = 8
-CHUNKS = 2
-WIDTH = 2
+CHUNKS = 1
+WIDTH = 1
 MOVED = 2
 CORE = "wide_2"
 WIDE = ("wide_0", "wide_1", "wide_2")
@@ -29,6 +29,10 @@
 
 def turned(place, size):
     return (4 * place + size) // (2 * size) % 2
+
+
+def interleaved(place, size):
+    return 2 * place % size + 2 * place // size
 
 
 def crossed():
@@ -37,7 +41,7 @@
     for side in range(sizes[2]):
         groups.append([
             (a * sizes[1] + b) * sizes[2] + (side ^ turned(a, sizes[0]))
-            for b in range(sizes[1])
+            for b in sorted(range(sizes[1]), key=lambda b: interleaved(b, sizes[1]))
             for a in range(sizes[0])
         ])
     return groups
@@ -70,7 +74,8 @@
 def collect_kernel(sizes, got, weight, row_dual, new_weight, new_row, row_all, rows_held):
     narrow, base, _, chips = sizes
     core = lax.axis_index(CORE)
-    place = lax.axis_index("wide_1") * lax.axis_size("wide_0") + lax.axis_index("wide_0")
+    along = interleaved(lax.axis_index("wide_1"), lax.axis_size("wide_1"))
+    place = along * lax.axis_size("wide_0") + lax.axis_index("wide_0")
     squares, rest = None, None
     for c in range(2):
         part = got[c * narrow]

time: 105 us -> 105 us (level)
  transfers between devices with their start and end apart: 14 -> 14, of which waited for: 6 -> 6; matrix products, arithmetic and copies ran while one was open for 0% -> 0% of each run, Pallas kernels for 4% -> 5%
where the time goes in v12:
time: 105 us; the launch traced here: 104 us
  blocking collectives  46.8 us (45%)
  waiting for transfers between devices  18.2 us (17%)
  starting transfers between devices  17.8 us (17%)
  Pallas kernels  11.4 us (11%)
  local copies, waits for them, and re-layouts  8.7 us (8%)
    all_to_all x4, blocking collectives, exchange(): lax.all_to_all(array, axes, split_axis=0, concat_axis=0, tiled=True, axis...  46.8 us
    all_to_all x3, waiting for transfers between devices, exchange(): lax.all_to_all(array, axes, split_axis=0, concat_axis=0, tiled=True, axis...  14.6 us
    all_to_all x3, starting transfers between devices, exchange(): lax.all_to_all(array, axes, split_axis=0, concat_axis=0, tiled=True, axis...  12 us
    pallas_call x21, Pallas kernels, call(): pl.pallas_call(kernel, out_shape=out_shape, in_specs=[HB if o in held els...  9.01 us
    unnamed x12, local copies, waits for them, and re-layouts  8.7 us
    ppermute x3, waiting for transfers between devices, shards(): lax.ppermute(row_sent, 'narrow', [(n, (n + k) % narrow) for n in range(na...  3.63 us
    ppermute x8, starting transfers between devices, swap(): return lax.ppermute(array, CORE, [(0, 1), (1, 0)])  3.49 us
    pallas_call x1, Pallas kernels, shards(): pl.pallas_call(functools.partial(open_kernel, sizes), out_shape=(big, big...  2.35 us
  transfers between devices with their start and end apart: 14, of which 6 were waited for; matrix products, arithmetic and copies ran while one was open for 0% of the time, Pallas kernels for 5%

profile of v12, /device:TPU:1, one launch (start us, length us, event | category | flops | bytes accessed | tf_op | source)
XLA Modules:
  0.0 103.6 jit_solution(8330448863175986509)
XLA Ops:
  0.6 2.3 %open_step.1 = (f32[128,4096]{1,0:T(8,128)S(1)}, f32[128,4096]{1,0:T(8,128)S(1)}, f32[1,128]{1,0:T(1,128)S(1)}, f32[1,4096]{1,0:T(1,128)S(1)}, f32[1,128]{1,0:T(...) custom-call(f32[128,4096]{1,0:T(8,128)} %refs_0_.1, ...), custom_call_target="tpu_custom_call" | custom-call | flops 3145728 | tf_op jit(solution)/shard_map/open_step/pallas_call | solution.py:390
  3.0 1.5 %collective-permute-start = (f32[1,2048]{1,0:T(1,128)S(1)}, f32[1,2048]{1,0:T(1,128)S(1)}, u32[]{:S(2)}, u32[]{:S(2)}) collective-permute-start(f32[1,2048]{1,0:T(1,128)S(1)} %get-tuple-element.60), channel_id=1, source_target_pairs={{0,4},{4,0},{1,5},{5,1},{2,6},{6,2},{3,7},{7,3},{8,12},{12,8},{9,1... | collective-permute-start | bytes 24584 | tf_op jit(solution)/shard_map/ppermute | solution.py:55
  4.4 0.8 shard_map.85
  5.3 1.3 %copy-done = f32[128,4096]{1,0:T(8,128)} copy-done((f32[128,4096]{1,0:T(8,128)}, f32[128,4096]{1,0:T(8,128)S(1)}, u32[]{:S(2)}) %copy-start) | copy-done | bytes 2097176
  6.6 15.6 %all_to_all.35.got = f32[16,1,2304]{2,1,0:T(1,128)S(1)} all-to-all(f32[16,1,2304]{2,1,0:T(1,128)S(1)} %shard_map.86), channel_id=1, replica_groups={{0,36,68,96,16,52,84,112,8,44,76,104,24,60,92,120},{4,32,64,100,20,48,8..., dimensions={0} | all-to-all | bytes 294912 | tf_op jit(solution)/shard_map/all_to_all | solution.py:25
  22.2 0.7 shard_map.87
  22.8 4.9 %all-to-all-start.1 = ((f32[8,1,2304]{2,1,0:T(1,128)}), f32[8,1,2304]{2,1,0:T(1,128)S(1)}, u32[]{:S(2)}, u32[]{:S(2)}) async-start(f32[8,1,2304]{2,1,0:T(1,128)} %get-tuple-element.61), calls=%async_computation.1 | async-start | bytes 147456 | tf_op jit(solution)/shard_map/all_to_all | solution.py:25
  27.7 0.0 collective-permute-start.1
  27.7 5.0 %all-to-all-done.1.got = f32[8,1,2304]{2,1,0:T(1,128)S(1)} async-done(((f32[8,1,2304]{2,1,0:T(1,128)}), f32[8,1,2304]{2,1,0:T(1,128)S(1)}, u32[]{:S(2)}, u32[]{:S(2)}) %all-to-all-start.1) | async-done | bytes 73760 | tf_op jit(solution)/shard_map/all_to_all | solution.py:25
  32.7 0.1 shard_map.88
  32.8 0.0 copy-start.1
  32.8 1.6 %copy-done.1 = f32[128,4096]{1,0:T(8,128)S(1)} copy-done((f32[128,4096]{1,0:T(8,128)S(1)}, f32[128,4096]{1,0:T(8,128)}, u32[]{:S(2)}) %copy-start.1) | copy-done | bytes 2097176
  34.4 0.4 shard_map.89
  34.9 0.5 collective-permute-start.2
  35.3 0.8 shard_map.90
  36.1 1.3 %copy-done.2 = f32[128,4096]{1,0:T(8,128)} copy-done((f32[128,4096]{1,0:T(8,128)}, f32[128,4096]{1,0:T(8,128)S(1)}, u32[]{:S(2)}) %copy-start.2) | copy-done | bytes 2097176
  37.5 10.4 %all_to_all.36.got = f32[16,1,2304]{2,1,0:T(1,128)S(1)} all-to-all(f32[16,1,2304]{2,1,0:T(1,128)S(1)} %shard_map.91), channel_id=1, replica_groups={{0,36,68,96,16,52,84,112,8,44,76,104,24,60,92,120},{4,32,64,100,20,48,8..., dimensions={0} | all-to-all | bytes 294912 | tf_op jit(solution)/shard_map/all_to_all | solution.py:25
  47.8 0.7 shard_map.92
  48.5 3.5 %all-to-all-start.3 = ((f32[8,1,2304]{2,1,0:T(1,128)}), f32[8,1,2304]{2,1,0:T(1,128)S(1)}, u32[]{:S(2)}, u32[]{:S(2)}) async-start(f32[8,1,2304]{2,1,0:T(1,128)} %get-tuple-element.71), calls=%async_computation.3 | async-start | bytes 147456 | tf_op jit(solution)/shard_map/all_to_all | solution.py:25
  52.0 0.2 collective-permute-start.3
  52.1 4.8 %all-to-all-done.3.got = f32[8,1,2304]{2,1,0:T(1,128)S(1)} async-done(((f32[8,1,2304]{2,1,0:T(1,128)}), f32[8,1,2304]{2,1,0:T(1,128)S(1)}, u32[]{:S(2)}, u32[]{:S(2)}) %all-to-all-start.3) | async-done | bytes 73760 | tf_op jit(solution)/shard_map/all_to_all | solution.py:25
  56.9 0.1 shard_map.93
  57.1 0.0 copy-start.3
  57.1 1.6 %copy-done.3 = f32[128,4096]{1,0:T(8,128)S(1)} copy-done((f32[128,4096]{1,0:T(8,128)S(1)}, f32[128,4096]{1,0:T(8,128)}, u32[]{:S(2)}) %copy-start.3) | copy-done | bytes 2097176
  58.7 0.4 shard_map.94
  59.1 0.5 collective-permute-start.4
  59.6 0.8 shard_map.95
  60.4 1.3 %copy-done.4 = f32[128,4096]{1,0:T(8,128)} copy-done((f32[128,4096]{1,0:T(8,128)}, f32[128,4096]{1,0:T(8,128)S(1)}, u32[]{:S(2)}) %copy-start.4) | copy-done | bytes 2097176
  61.7 10.6 %all_to_all.37.got = f32[16,1,2304]{2,1,0:T(1,128)S(1)} all-to-all(f32[16,1,2304]{2,1,0:T(1,128)S(1)} %shard_map.96), channel_id=1, replica_groups={{0,36,68,96,16,52,84,112,8,44,76,104,24,60,92,120},{4,32,64,100,20,48,8..., dimensions={0} | all-to-all | bytes 294912 | tf_op jit(solution)/shard_map/all_to_all | solution.py:25
  72.4 0.7 shard_map.97
  73.1 3.7 %all-to-all-start.5 = ((f32[8,1,2304]{2,1,0:T(1,128)}), f32[8,1,2304]{2,1,0:T(1,128)S(1)}, u32[]{:S(2)}, u32[]{:S(2)}) async-start(f32[8,1,2304]{2,1,0:T(1,128)} %get-tuple-element.81), calls=%async_computation.5 | async-start | bytes 147456 | tf_op jit(solution)/shard_map/all_to_all | solution.py:25
  76.7 0.2 collective-permute-start.5
  76.9 4.8 %all-to-all-done.5.got = f32[8,1,2304]{2,1,0:T(1,128)S(1)} async-done(((f32[8,1,2304]{2,1,0:T(1,128)}), f32[8,1,2304]{2,1,0:T(1,128)S(1)}, u32[]{:S(2)}, u32[]{:S(2)}) %all-to-all-start.5) | async-done | bytes 73760 | tf_op jit(solution)/shard_map/all_to_all | solution.py:25
  81.7 0.1 shard_map.98
  81.8 0.0 copy-start.5
  81.8 1.6 %copy-done.5 = f32[128,4096]{1,0:T(8,128)S(1)} copy-done((f32[128,4096]{1,0:T(8,128)S(1)}, f32[128,4096]{1,0:T(8,128)}, u32[]{:S(2)}) %copy-start.5) | copy-done | bytes 2097176
  83.4 0.4 shard_map.99
  83.9 0.5 collective-permute-start.6
  84.3 1.2 %shard_map.100 = (f32[128,4096]{1,0:T(8,128)S(1)}, f32[1,2304]{1,0:T(1,128)S(1)}, f32[1,128]{1,0:T(1,128)S(1)}, f32[128,4096]{1,0:T(8,128)}) custom-call(f32[8,128]{1,0:T(8,128)S(1)} %get-tuple-element.83.new_weight.weight, f32[128,4096]{1,0:T(8,128)S(1)} %get-tuple-element.52.cost, f32[128,4096]{1,0:T(8,128)S(1)} %copy-done.5, ...), custom_call_target="tpu_custom_call", output_to_operand_aliasing={{0}: (3, {})} | custom-call | flops 3145728 | tf_op jit(solution)/shard_map/pallas_call | solution.py:369
  85.5 10.2 %all_to_all.38.got = f32[16,1,2048]{2,1,0:T(1,128)S(1)} all-to-all(f32[16,1,2048]{2,1,0:T(1,128)S(1)} %shard_map.101), channel_id=1, replica_groups={{0,36,68,96,16,52,84,112,8,44,76,104,24,60,92,120},{4,32,64,100,20,48,8..., dimensions={0} | all-to-all | bytes 262144 | tf_op jit(solution)/shard_map/all_to_all | solution.py:25
  95.7 0.3 collective-permute-start.7
  96.0 1.1 %collective-permute-start.10 = (f32[1,128]{1,0:T(1,128)S(1)}, f32[1,128]{1,0:T(1,128)S(1)}, u32[]{:S(2)}, u32[]{:S(2)}) collective-permute-start(f32[1,128]{1,0:T(1,128)S(1)} %get-tuple-element.95.refs_0_), channel_id=1, source_target_pairs={{0,3},{1,0},{2,1},{3,2},{4,7},{5,4},{6,5},{7,6},{8,11},{9,8},{10,9... | collective-permute-start | bytes 1544 | tf_op jit(solution)/shard_map/ppermute | solution.py:435
  97.1 1.2 %collective-permute-start.9 = (f32[1,128]{1,0:T(1,128)S(1)}, f32[1,128]{1,0:T(1,128)S(1)}, u32[]{:S(2)}, u32[]{:S(2)}) collective-permute-start(f32[1,128]{1,0:T(1,128)S(1)} %get-tuple-element.95.refs_0_), channel_id=1, source_target_pairs={{0,2},{1,3},{2,0},{3,1},{4,6},{5,7},{6,4},{7,5},{8,10},{9,11},{10,... | collective-permute-start | bytes 1544 | tf_op jit(solution)/shard_map/ppermute | solution.py:435
  98.3 0.1 collective-permute-done.10.refs_3_
  98.4 2.6 %collective-permute-done.9.refs_2_ = f32[1,128]{1,0:T(1,128)S(1)} collective-permute-done((f32[1,128]{1,0:T(1,128)S(1)}, f32[1,128]{1,0:T(1,128)S(1)}, u32[]{:S(2)}, u32[]{:S(2)}) %collective-permute-start.9) | collective-permute-done | bytes 544 | tf_op jit(solution)/shard_map/ppermute | solution.py:435
  101.0 0.9 collective-permute-done.8.refs_1_
  101.9 1.0 shard_map.103
  102.9 0.7 shard_map.105
  (18 shorter events, 0.1 us)
Async XLA Ops:
  3.0 3.6 %collective-permute-start = (f32[1,2048]{1,0:T(1,128)S(1)}, f32[1,2048]{1,0:T(1,128)S(1)}, u32[]{:S(2)}, u32[]{:S(2)}) collective-permute-start(f32[1,2048]{1,0:T(1,128)S(1)} %get-tuple-element.60), channel_id=1, source_target_pairs={{0,4},{4,0},{1,5},{5,1},{2,6},{6,2},{3,7},{7,3},{8,12},{12,8},{9,1... | collective-permute-start | bytes 24584 | tf_op jit(solution)/shard_map/ppermute | solution.py:55
  5.2 1.3 %copy-start = (f32[128,4096]{1,0:T(8,128)}, f32[128,4096]{1,0:T(8,128)S(1)}, u32[]{:S(2)}) copy-start(f32[128,4096]{1,0:T(8,128)S(1)} %get-tuple-element.64.plan) | copy-start | bytes 6291460
  22.8 9.8 %all-to-all-start.1 = ((f32[8,1,2304]{2,1,0:T(1,128)}), f32[8,1,2304]{2,1,0:T(1,128)S(1)}, u32[]{:S(2)}, u32[]{:S(2)}) async-start(f32[8,1,2304]{2,1,0:T(1,128)} %get-tuple-element.61), calls=%async_computation.1 | async-start | bytes 147456 | tf_op jit(solution)/shard_map/all_to_all | solution.py:25
  27.7 5.1 %collective-permute-start.1 = (f32[1,2048]{1,0:T(1,128)S(1)}, f32[1,2048]{1,0:T(1,128)S(1)}, u32[]{:S(2)}, u32[]{:S(2)}) collective-permute-start(f32[1,2048]{1,0:T(1,128)S(1)} %get-tuple-element.65.mine), channel_id=1, source_target_pairs={{0,4},{4,0},{1,5},{5,1},{2,6},{6,2},{3,7},{7,3},{8,12},{12,8},{9,1... | collective-permute-start | bytes 24584 | tf_op jit(solution)/shard_map/ppermute | solution.py:55
  32.8 1.6 %copy-start.1 = (f32[128,4096]{1,0:T(8,128)S(1)}, f32[128,4096]{1,0:T(8,128)}, u32[]{:S(2)}) copy-start(f32[128,4096]{1,0:T(8,128)} %copy-done) | copy-start | bytes 6291460
  34.9 2.6 %collective-permute-start.2 = (f32[1,2048]{1,0:T(1,128)S(1)}, f32[1,2048]{1,0:T(1,128)S(1)}, u32[]{:S(2)}, u32[]{:S(2)}) collective-permute-start(f32[1,2048]{1,0:T(1,128)S(1)} %get-tuple-element.70), channel_id=1, source_target_pairs={{0,4},{4,0},{1,5},{5,1},{2,6},{6,2},{3,7},{7,3},{8,12},{12,8},{9,1... | collective-permute-start | bytes 24584 | tf_op jit(solution)/shard_map/ppermute | solution.py:55
  36.1 1.3 %copy-start.2 = (f32[128,4096]{1,0:T(8,128)}, f32[128,4096]{1,0:T(8,128)S(1)}, u32[]{:S(2)}) copy-start(f32[128,4096]{1,0:T(8,128)S(1)} %get-tuple-element.74.plan) | copy-start | bytes 6291460
  48.5 8.4 %all-to-all-start.3 = ((f32[8,1,2304]{2,1,0:T(1,128)}), f32[8,1,2304]{2,1,0:T(1,128)S(1)}, u32[]{:S(2)}, u32[]{:S(2)}) async-start(f32[8,1,2304]{2,1,0:T(1,128)} %get-tuple-element.71), calls=%async_computation.3 | async-start | bytes 147456 | tf_op jit(solution)/shard_map/all_to_all | solution.py:25
  52.0 5.1 %collective-permute-start.3 = (f32[1,2048]{1,0:T(1,128)S(1)}, f32[1,2048]{1,0:T(1,128)S(1)}, u32[]{:S(2)}, u32[]{:S(2)}) collective-permute-start(f32[1,2048]{1,0:T(1,128)S(1)} %get-tuple-element.75.mine), channel_id=1, source_target_pairs={{0,4},{4,0},{1,5},{5,1},{2,6},{6,2},{3,7},{7,3},{8,12},{12,8},{9,1... | collective-permute-start | bytes 24584 | tf_op jit(solution)/shard_map/ppermute | solution.py:55
  57.1 1.6 %copy-start.3 = (f32[128,4096]{1,0:T(8,128)S(1)}, f32[128,4096]{1,0:T(8,128)}, u32[]{:S(2)}) copy-start(f32[128,4096]{1,0:T(8,128)} %copy-done.2) | copy-start | bytes 6291460
  59.1 2.6 %collective-permute-start.4 = (f32[1,2048]{1,0:T(1,128)S(1)}, f32[1,2048]{1,0:T(1,128)S(1)}, u32[]{:S(2)}, u32[]{:S(2)}) collective-permute-start(f32[1,2048]{1,0:T(1,128)S(1)} %get-tuple-element.80), channel_id=1, source_target_pairs={{0,4},{4,0},{1,5},{5,1},{2,6},{6,2},{3,7},{7,3},{8,12},{12,8},{9,1... | collective-permute-start | bytes 24584 | tf_op jit(solution)/shard_map/ppermute | solution.py:55
  60.4 1.3 %copy-start.4 = (f32[128,4096]{1,0:T(8,128)}, f32[128,4096]{1,0:T(8,128)S(1)}, u32[]{:S(2)}) copy-start(f32[128,4096]{1,0:T(8,128)S(1)} %get-tuple-element.84.plan) | copy-start | bytes 6291460
  73.1 8.6 %all-to-all-start.5 = ((f32[8,1,2304]{2,1,0:T(1,128)}), f32[8,1,2304]{2,1,0:T(1,128)S(1)}, u32[]{:S(2)}, u32[]{:S(2)}) async-start(f32[8,1,2304]{2,1,0:T(1,128)} %get-tuple-element.81), calls=%async_computation.5 | async-start | bytes 147456 | tf_op jit(solution)/shard_map/all_to_all | solution.py:25
  76.7 5.1 %collective-permute-start.5 = (f32[1,2048]{1,0:T(1,128)S(1)}, f32[1,2048]{1,0:T(1,128)S(1)}, u32[]{:S(2)}, u32[]{:S(2)}) collective-permute-start(f32[1,2048]{1,0:T(1,128)S(1)} %get-tuple-element.85.mine), channel_id=1, source_target_pairs={{0,4},{4,0},{1,5},{5,1},{2,6},{6,2},{3,7},{7,3},{8,12},{12,8},{9,1... | collective-permute-start | bytes 24584 | tf_op jit(solution)/shard_map/ppermute | solution.py:55
  81.8 1.6 %copy-start.5 = (f32[128,4096]{1,0:T(8,128)S(1)}, f32[128,4096]{1,0:T(8,128)}, u32[]{:S(2)}) copy-start(f32[128,4096]{1,0:T(8,128)} %copy-done.4) | copy-start | bytes 6291460
  83.9 1.7 %collective-permute-start.6 = (f32[1,2048]{1,0:T(1,128)S(1)}, f32[1,2048]{1,0:T(1,128)S(1)}, u32[]{:S(2)}, u32[]{:S(2)}) collective-permute-start(f32[1,2048]{1,0:T(1,128)S(1)} %get-tuple-element.91), channel_id=1, source_target_pairs={{0,4},{4,0},{1,5},{5,1},{2,6},{6,2},{3,7},{7,3},{8,12},{12,8},{9,1... | collective-permute-start | bytes 24584 | tf_op jit(solution)/shard_map/ppermute | solution.py:55
  95.7 7.2 %collective-permute-start.7 = (f32[1,2048]{1,0:T(1,128)S(1)}, f32[1,2048]{1,0:T(1,128)S(1)}, u32[]{:S(2)}, u32[]{:S(2)}) collective-permute-start(f32[1,2048]{1,0:T(1,128)S(1)} %shard_map.102.after.mine), channel_id=1, source_target_pairs={{0,4},{4,0},{1,5},{5,1},{2,6},{6,2},{3,7},{7,3},{8,12},{12,8},{9,1... | collective-permute-start | bytes 24584 | tf_op jit(solution)/shard_map/ppermute | solution.py:55
  96.0 2.4 %collective-permute-start.10 = (f32[1,128]{1,0:T(1,128)S(1)}, f32[1,128]{1,0:T(1,128)S(1)}, u32[]{:S(2)}, u32[]{:S(2)}) collective-permute-start(f32[1,128]{1,0:T(1,128)S(1)} %get-tuple-element.95.refs_0_), channel_id=1, source_target_pairs={{0,3},{1,0},{2,1},{3,2},{4,7},{5,4},{6,5},{7,6},{8,11},{9,8},{10,9... | collective-permute-start | bytes 1544 | tf_op jit(solution)/shard_map/ppermute | solution.py:435
  97.1 3.9 %collective-permute-start.9 = (f32[1,128]{1,0:T(1,128)S(1)}, f32[1,128]{1,0:T(1,128)S(1)}, u32[]{:S(2)}, u32[]{:S(2)}) collective-permute-start(f32[1,128]{1,0:T(1,128)S(1)} %get-tuple-element.95.refs_0_), channel_id=1, source_target_pairs={{0,2},{1,3},{2,0},{3,1},{4,6},{5,7},{6,4},{7,5},{8,10},{9,11},{10,... | collective-permute-start | bytes 1544 | tf_op jit(solution)/shard_map/ppermute | solution.py:435
  98.3 3.6 %collective-permute-start.8 = (f32[1,128]{1,0:T(1,128)S(1)}, f32[1,128]{1,0:T(1,128)S(1)}, u32[]{:S(2)}, u32[]{:S(2)}) collective-permute-start(f32[1,128]{1,0:T(1,128)S(1)} %get-tuple-element.95.refs_0_), channel_id=1, source_target_pairs={{0,1},{1,2},{2,3},{3,0},{4,5},{5,6},{6,7},{7,4},{8,9},{9,10},{10,1... | collective-permute-start | bytes 1544 | tf_op jit(solution)/shard_map/ppermute | solution.py:435
